TPU v7x, 8 devices: a whole 2x2x1 slice. The times are simulated.
8 devices in a mesh: rep: 1 (over z), dp: 8 (over x, y, core).
Axes of the slice: x: 2, y: 2, z: 1, core: 2. Of those that a mesh axis runs over, the one named last changes fastest.
Arguments:
- x: bfloat16 [8, 2048, 1536], P(('rep', 'dp'))
- dy: bfloat16 [8, 2048, 1536], P(('rep', 'dp'))
- w_gate: bfloat16 [2, 1536, 4224], replicated
- w_up: bfloat16 [2, 1536, 4224], replicated
- w_down: bfloat16 [2, 4224, 1536], replicated
- m_w_gate: float32 [2, 1536, 4224], P(None, 'dp')
- m_w_up: float32 [2, 1536, 4224], P(None, 'dp')
- m_w_down: float32 [2, 4224, 1536], P(None, 'dp')
- v_w_gate: float32 [2, 1536, 4224], P(None, 'dp')
- v_w_up: float32 [2, 1536, 4224], P(None, 'dp')
- v_w_down: float32 [2, 4224, 1536], P(None, 'dp')
Outputs:
- output 1: bfloat16 [2, 1536, 4224], P('rep')
- output 2: bfloat16 [2, 1536, 4224], P('rep')
- output 3: bfloat16 [2, 4224, 1536], P('rep')
- output 4: float32 [2, 1536, 4224], P('rep', 'dp')
- output 5: float32 [2, 1536, 4224], P('rep', 'dp')
- output 6: float32 [2, 4224, 1536], P('rep', 'dp')
- output 7: float32 [2, 1536, 4224], P('rep', 'dp')
- output 8: float32 [2, 1536, 4224], P('rep', 'dp')
- output 9: float32 [2, 4224, 1536], P('rep', 'dp')
All inputs are finite; a program needn't handle non-finite values.
Results may differ from a plain program's by a relative error of at most 0.022.
Values are sent between devices in bfloat16 or wider.
A program may use at most 2 GiB of HBM per device.

v0:
```python
import jax
import jax.numpy as jnp
from jax import lax

NAMES = ("w_gate", "w_up", "w_down")


def matmul(a, w):
    return jnp.dot(a, w, preferred_element_type=jnp.float32).astype(jnp.bfloat16)


def normed(h):
    wide = h.astype(jnp.float32)
    scale = lax.rsqrt(jnp.mean(wide**2, -1, keepdims=True) + 1e-6)
    return (wide * scale).astype(jnp.bfloat16)


def layer(h, w):
    a = normed(h)
    gate = jnp.dot(a, w["w_gate"], preferred_element_type=jnp.float32)
    up = jnp.dot(a, w["w_up"], preferred_element_type=jnp.float32)
    return h + matmul((jax.nn.silu(gate) * up).astype(jnp.bfloat16), w["w_down"])


def adamw(w, m, v, g):
    m = 0.9 * m + 0.1 * g
    v = 0.95 * v + 0.05 * g * g
    step = m * lax.rsqrt(v + 1e-8) + 0.1 * w
    return (w - 0.02 * step).astype(jnp.bfloat16), m, v


def clipped(gradients, sum_of_squares, count):
    factor = jnp.minimum(1.0, 0.5 * lax.rsqrt(sum_of_squares / count + 1e-30))
    return [g * factor for g in gradients]


def stack(weights, h):
    for number in range(weights["w_gate"].shape[0]):
        h = layer(h, {name: w[number] for name, w in weights.items()})
    return h


def solution(mesh):
    groups = mesh.shape["rep"]

    def step(x, dy, *arrays):
        weights, m, v = (arrays[i : i + 3] for i in (0, 3, 6))
        x, dy = (t.reshape(groups, -1, *t.shape[1:]) for t in (x, dy))

        def of_a_group(x, dy):
            _, back = jax.vjp(lambda w: stack(w, x), dict(zip(NAMES, weights, strict=True)))
            by_weights = back(dy)[0]
            gradients = [by_weights[name].astype(jnp.float32) for name in NAMES]
            gradients = clipped(gradients, sum(jnp.sum(g * g) for g in gradients), sum(g.size for g in gradients))
            new = [adamw(w.astype(jnp.float32), m, v, g) for w, m, v, g in zip(weights, m, v, gradients, strict=True)]
            return tuple(one[which] for which in range(3) for one in new)

        return tuple(t.reshape(-1, *t.shape[2:]) for t in jax.vmap(of_a_group)(x, dy))

    return step
```

profile of v0, /device:TPU:0, one launch (start us, length us, event | category | flops | bytes accessed | tf_op | source)
XLA Modules:
  0.0 1748.6 jit_solution(10612067977941227142)
XLA Ops:
  7.2 4.1 fusion.53
  11.3 8.8 copy
  20.1 37.6 %fusion.47 = f32[2048,4224]{1,0:T(8,128)} fusion(bf16[2,1536,4224]{2,1,0:T(8,128)(2,1)} %param, bf16[1,2048,1536]{2,1,0:T(8,128)(2,1)} %param.4, f32[2048]{0:T(1024)S(1)} %add_rsqrt_fusion), kind=kOutput, calls=%fused_computation.64 | convolution fusion | flops 26584547328 | bytes 53878784 | tf_op jit(solution)/vmap(jvp())/dot_general | solution.py:20
  57.8 34.3 %fusion.45 = f32[2048,4224]{1,0:T(8,128)} fusion(bf16[2,1536,4224]{2,1,0:T(8,128)(2,1)} %param.5, bf16[1,2048,1536]{2,1,0:T(8,128)(2,1)S(1)} %bitcast.341, f32[2048]{0:T(1024)S(1)} %add_rsqrt_fusion), kind=kOutput, calls=%fused_computation.62 | convolution fusion | flops 26584547328 | bytes 53878784 | tf_op jit(solution)/vmap(jvp())/dot_general | solution.py:21
  92.0 28.6 %fusion.26 = bf16[2048,4224]{1,0:T(8,128)(2,1)} fusion(f32[2048,4224]{1,0:T(8,128)} %fusion.45, f32[2048,4224]{1,0:T(8,128)} %fusion.47), kind=kLoop, calls=%fused_computation.41 | loop fusion | flops 51904512 | bytes 86507520
  120.6 48.6 %fusion.57 = (f32[2048]{0:T(1024)S(1)}, bf16[1,2048,1536]{1,2,0:T(8,128)(2,1)}) fusion(bf16[1,2048,1536]{1,2,0:T(8,128)(2,1)} %copy, bf16[2048,4224]{1,0:T(8,128)(2,1)} %fusion.26, bf16[2,4224,1536]{2,1,0:T(8,128)(2,1)} %param.3), kind=kOutput, calls=%fused_computation.74 | convolution fusion | flops 26590836736 | bytes 42868736 | tf_op jit(solution)/vmap(jvp())/dot_general | solution.py:9
  169.9 37.5 %fusion.35 = f32[2048,4224]{1,0:T(8,128)} fusion(bf16[2,1536,4224]{2,1,0:T(8,128)(2,1)} %param, bf16[1,2048,1536]{1,2,0:T(8,128)(2,1)} %get-tuple-element.10, f32[2048]{0:T(1024)S(1)} %bitcast.345), kind=kOutput, calls=%fused_computation.52 | convolution fusion | flops 26584547328 | bytes 53878784 | tf_op jit(solution)/vmap(jvp())/dot_general | solution.py:20
  207.4 35.5 %fusion.39 = f32[2048,4224]{1,0:T(8,128)} fusion(bf16[2,1536,4224]{2,1,0:T(8,128)(2,1)} %param.5, bf16[1,2048,1536]{1,2,0:T(8,128)(2,1)S(1)} %copy-done.3, f32[2048]{0:T(1024)S(1)} %bitcast.346), kind=kOutput, calls=%fused_computation.56 | convolution fusion | flops 26584547328 | bytes 53878784 | tf_op jit(solution)/vmap(jvp())/dot_general | solution.py:21
  242.9 40.9 %fusion.28 = f32[4224,1536]{1,0:T(8,128)} fusion(f32[2048,4224]{1,0:T(8,128)} %fusion.39, f32[2048,4224]{1,0:T(8,128)} %fusion.35, bf16[1,2048,1536]{2,1,0:T(8,128)(2,1)} %param.2), kind=kOutput, calls=%fused_computation.43 | convolution fusion | flops 26627014656 | bytes 101449728 | tf_op jit(solution)/vmap(transpose(jvp()))/dot_general | solution.py:9
  283.8 35.9 %convolution_convert_fusion.1 = bf16[2048,4224]{1,0:T(8,128)(2,1)} fusion(bf16[2,4224,1536]{2,1,0:T(8,128)(2,1)} %param.3, bf16[1,2048,1536]{2,1,0:T(8,128)(2,1)} %param.2), kind=kOutput, calls=%fused_computation.40 | convolution fusion | flops 26583760896 | bytes 36569088 | tf_op jit(solution)/vmap(transpose(jvp()))/dot_general | solution.py:9
  319.7 8.7 copy.1
  328.4 37.0 %fusion.6 = bf16[2048,4224]{1,0:T(8,128)(2,1)} fusion(f32[2048,4224]{1,0:T(8,128)} %fusion.35, f32[2048,4224]{1,0:T(8,128)} %fusion.39, bf16[2048,4224]{1,0:T(8,128)(2,1)} %convolution_convert_fusion.1), kind=kLoop, calls=%fused_computation.11 | loop fusion | flops 103809024 | bytes 103809024
  365.4 38.6 %fusion.75 = bf16[2048,1536]{0,1:T(8,128)(2,1)} fusion(bf16[2,1536,4224]{2,1,0:T(8,128)(2,1)} %param.5, bf16[2048,4224]{1,0:T(8,128)(2,1)} %convolution_convert_fusion.1, f32[2048,4224]{1,0:T(8,128)} %fusion.35), kind=kOutput, calls=%fused_computation.103 | convolution fusion | flops 26630160384 | bytes 71172096 | tf_op jit(solution)/vmap(transpose(jvp()))/dot_general | solution.py:21
  404.0 39.2 %fusion.59 = (f32[2048]{0:T(1024)S(1)}, bf16[2048,1536]{0,1:T(8,128)(2,1)}) fusion(bf16[1,2048,1536]{1,2,0:T(8,128)(2,1)} %get-tuple-element.10, bf16[2048,1536]{0,1:T(8,128)(2,1)} %fusion.75, bf16[2048,4224]{1,0:T(8,128)(2,1)} %fusion.6, bf16[2,1536,4224]{2,1,0:T(8,128)(2,1)} %param), kind=kOutput, calls=%fused_computation.76 | convolution fusion | flops 26590836736 | bytes 49160192 | tf_op jit(solution)/vmap(transpose(jvp()))/dot_general | solution.py:20
  443.2 8.6 fusion.109
  451.8 2.7 copy-done.4
  454.5 34.3 %fusion.139 = f32[1536,4224]{0,1:T(8,128)} fusion(bf16[2048,1536]{0,1:T(8,128)(2,1)S(1)} %fusion.109, bf16[2048,4224]{1,0:T(8,128)(2,1)} %fusion.26), kind=kOutput, calls=%fused_computation.161 | convolution fusion | flops 26575110144 | bytes 49545216 | tf_op jit(solution)/vmap(transpose(jvp()))/dot_general | solution.py:9
  488.9 45.8 %fusion.22 = f32[4224,1536]{0,1:T(8,128)} fusion(bf16[2048,4224]{1,0:T(8,128)(2,1)} %convolution_convert_fusion.1, f32[2048,4224]{1,0:T(8,128)} %fusion.35, bf16[1,2048,1536]{1,2,0:T(8,128)(2,1)} %get-tuple-element.10, f32[2048]{0:T(1024)S(1)} %bitcast.348), kind=kOutput, calls=%fused_computation.33 | convolution fusion | flops 26636451840 | bytes 84156416 | tf_op jit(solution)/vmap(transpose(jvp()))/dot_general | solution.py:21
  534.8 36.4 %convolution_convert_fusion = bf16[2048,4224]{1,0:T(8,128)(2,1)} fusion(bf16[2048,1536]{0,1:T(8,128)(2,1)} %copy-done.4, bf16[2,4224,1536]{2,1,0:T(8,128)(2,1)} %param.3), kind=kOutput, calls=%fused_computation.39 | convolution fusion | flops 26583760896 | bytes 36569088 | tf_op jit(solution)/vmap(transpose(jvp()))/dot_general | solution.py:9
  571.2 43.9 %fusion.2 = f32[4224,1536]{0,1:T(8,128)} fusion(bf16[2048,4224]{1,0:T(8,128)(2,1)} %convolution_convert_fusion, f32[2048,4224]{1,0:T(8,128)} %fusion.47, bf16[1,2048,1536]{2,1,0:T(8,128)(2,1)} %param.4, f32[2048]{0:T(1024)S(1)} %copy-done.11), kind=kOutput, calls=%fused_computation.8 | convolution fusion | flops 26636451840 | bytes 84156416 | tf_op jit(solution)/vmap(transpose(jvp()))/dot_general | solution.py:21
  615.1 0.6 copy-done.9
  615.8 36.1 %fusion.120 = f32[4224,1536]{0,1:T(8,128)} fusion(bf16[2048,4224]{1,0:T(8,128)(2,1)} %fusion.6, bf16[1,2048,1536]{1,2,0:T(8,128)(2,1)} %get-tuple-element.10, f32[2048]{0:T(1024)S(1)} %bitcast.349), kind=kOutput, calls=%fused_computation.137 | convolution fusion | flops 26584547328 | bytes 49553408 | tf_op jit(solution)/vmap(transpose(jvp()))/dot_general | solution.py:20
  652.0 57.5 %fusion.10 = f32[4224,1536]{0,1:T(8,128)} fusion(f32[2048,4224]{1,0:T(8,128)} %fusion.47, f32[2048,4224]{1,0:T(8,128)} %fusion.45, bf16[2048,4224]{1,0:T(8,128)(2,1)} %convolution_convert_fusion, bf16[1,2048,1536]{2,1,0:T(8,128)(2,1)} %param.4, f32[2048]{0:T(1024)S(1)} %copy-done.11), kind=kOutput, calls=%fused_computation.15 | convolution fusion | flops 26679705600 | bytes 118759424 | tf_op jit(solution)/vmap(transpose(jvp()))/dot_general | solution.py:20
  709.8 2.4 convert_bitcast_fusion.4
  712.2 2.7 convert_bitcast_fusion.3
  714.9 1.1 copy-done.1
  716.0 2.3 fusion.93
  718.3 81.7 %reduce-scatter.23.cloned.1.call-done = f32[4224,192]{0,1:T(8,128)} async-done(((f32[4224,1536]{0,1:T(8,128)}), f32[4224,192]{0,1:T(8,128)}) %reduce-scatter.23.cloned.1.call-update) | async-done | bytes 3244048
  800.0 2.1 convert_bitcast_fusion.6
  802.1 153.4 %reduce-scatter.25.cloned.1.call-done = f32[4224,192]{0,1:T(8,128)} async-done(((f32[4224,1536]{0,1:T(8,128)}), f32[4224,192]{0,1:T(8,128)}) %reduce-scatter.25.cloned.1.call-update) | async-done | bytes 3244048
  955.5 2.1 convert_bitcast_fusion.5
  957.6 2.3 fusion.92
  959.9 151.2 %reduce-scatter.19.cloned.1.call-done = f32[4224,192]{0,1:T(8,128)} async-done(((f32[4224,1536]{0,1:T(8,128)}), f32[4224,192]{0,1:T(8,128)}) %reduce-scatter.19.cloned.1.call-update) | async-done | bytes 3244048
  1111.1 3.2 convert_bitcast_fusion.8
  1114.3 152.3 %reduce-scatter.21.cloned.1.call-done = f32[4224,192]{0,1:T(8,128)} async-done(((f32[4224,1536]{0,1:T(8,128)}), f32[4224,192]{0,1:T(8,128)}) %reduce-scatter.21.cloned.1.call-update) | async-done | bytes 3244048
  1266.6 2.1 convert_bitcast_fusion.7
  1268.7 1.1 copy-done.2
  1269.9 3.7 fusion.91
  1275.5 22.2 %all-reduce.16 = f32[]{:T(128)} all-reduce(f32[]{:T(128)S(6)} %add.114), channel_id=5, replica_groups=mesh['rep'=1,'dp'=8] {'dp'}, use_global_device_ids=true, to_apply=%region_3.4.clone | all-reduce | flops 1 | bytes 8 | tf_op jit(solution)/vmap()/reduce_sum | solution.py:54
  1298.4 11.7 fusion.129
  1310.1 13.8 fusion.128
  1324.0 10.9 fusion.127
  1335.0 100.2 %all-gather.14.cloned.1.call-done = bf16[1,2,4224,1536]{3,2,1,0:T(8,128)(2,1)} async-done(((bf16[1,2,528,1536]{3,2,1,0:T(8,128)(2,1)}), bf16[1,2,4224,1536]{3,2,1,0:T(8,128)(2,1)}) %all-gather.14.cloned.1.call-update) | async-done | bytes 25952272 | tf_op jit(solution)/reshape | solution.py:58
  1435.2 125.4 %all-gather.10.cloned.1.call-done = bf16[1,2,1536,4224]{3,2,1,0:T(8,128)(2,1)} async-done(((bf16[1,2,192,4224]{3,2,1,0:T(8,128)(2,1)}), bf16[1,2,1536,4224]{3,2,1,0:T(8,128)(2,1)}) %all-gather.10.cloned.1.call-update) | async-done | bytes 25952272 | tf_op jit(solution)/reshape | solution.py:58
  1560.6 125.4 %all-gather.12.cloned.1.call-done = bf16[1,2,1536,4224]{3,2,1,0:T(8,128)(2,1)} async-done(((bf16[1,2,192,4224]{3,2,1,0:T(8,128)(2,1)}), bf16[1,2,1536,4224]{3,2,1,0:T(8,128)(2,1)}) %all-gather.12.cloned.1.call-update) | async-done | bytes 25952272 | tf_op jit(solution)/reshape | solution.py:58
  1686.0 23.8 %copy.5 = bf16[2,1536,4224]{2,1,0:T(8,128)(2,1)} copy(bf16[2,1536,4224]{2,1,0:T(8,128)(2,1)} %bitcast.338) | data formatting | bytes 51904512
  1709.8 22.6 %copy.6 = bf16[2,1536,4224]{2,1,0:T(8,128)(2,1)} copy(bf16[2,1536,4224]{2,1,0:T(8,128)(2,1)} %bitcast.339) | data formatting | bytes 51904512
  1732.5 9.2 copy.7
  (64 shorter events, 1.5 us)
Async XLA Ops:
  7.2 702.6 %reduce-scatter.27.cloned.1.call-start = ((), (), s32[]{:S(2)}) async-start(), calls=%async_computation.13 | async-start | bytes 29196288
  11.3 46.4 %slice-start.7 = ((s8[6291456]{0:T(1024)(128)(4,1)}), s8[2097152]{0:T(1024)(128)(4,1)S(1)}, s32[]{:S(2)}) async-start(s8[6291456]{0:T(1024)(128)(4,1)} %bitcast.340), calls=%async_computation.22 | async-start | bytes 4194304
  20.1 37.7 %copy-start.10 = (f32[2048]{0:T(1024)}, f32[2048]{0:T(1024)S(1)}, u32[]{:S(2)}) copy-start(f32[2048]{0:T(1024)S(1)} %add_rsqrt_fusion) | copy-start | bytes 24580
  20.1 37.7 %slice-start.8 = ((s8[6291456]{0:T(1024)(128)(4,1)}), s8[4194304]{0:T(1024)(128)(4,1)S(1)}, s32[]{:S(2)}) async-start(s8[6291456]{0:T(1024)(128)(4,1)} %bitcast.340), calls=%async_computation.23 | async-start | bytes 8388608
  169.3 0.6 copy-start.5
  169.3 38.1 %copy-start.7 = (f32[1,2048]{1,0:T(1,128)}, f32[1,2048]{1,0:T(1,128)S(1)}, u32[]{:S(2)}) copy-start(f32[1,2048]{1,0:T(1,128)S(1)} %rsqrt.32) | copy-start | bytes 24580
  169.9 37.5 %copy-start.3 = (bf16[1,2048,1536]{1,2,0:T(8,128)(2,1)S(1)}, bf16[1,2048,1536]{1,2,0:T(8,128)(2,1)}, u32[]{:S(2)}) copy-start(bf16[1,2048,1536]{1,2,0:T(8,128)(2,1)} %get-tuple-element.10) | copy-start | bytes 18874372
  283.8 428.4 %reduce-scatter.29.cloned.1.call-start = ((), (), s32[]{:S(2)}) async-start(), calls=%async_computation.14 | async-start | bytes 29196288
  404.0 39.2 %copy-start.6 = (f32[2048]{0:T(1024)S(1)}, f32[2048]{0:T(1024)}, u32[]{:S(2)}) copy-start(f32[2048]{0:T(1024)} %copy-done.5) | copy-start | bytes 24580
  404.0 39.2 %copy-start.8 = (f32[1,2048]{1,0:T(1,128)S(1)}, f32[1,2048]{1,0:T(1,128)}, u32[]{:S(2)}) copy-start(f32[1,2048]{1,0:T(1,128)} %copy-done.7) | copy-start | bytes 24580
  451.8 2.7 copy-start.4
  488.8 311.1 %reduce-scatter.23.cloned.1.call-start = ((), (), s32[]{:S(2)}) async-start(), calls=%async_computation.11 | async-start | bytes 29196288
  534.8 36.4 %copy-start.11 = (f32[2048]{0:T(1024)S(1)}, f32[2048]{0:T(1024)}, u32[]{:S(2)}) copy-start(f32[2048]{0:T(1024)} %copy-done.10) | copy-start | bytes 24580
  534.8 420.7 %reduce-scatter.25.cloned.1.call-start = ((), (), s32[]{:S(2)}) async-start(), calls=%async_computation.12 | async-start | bytes 29196288
  615.1 0.7 copy-start.9
  615.1 496.0 %reduce-scatter.19.cloned.1.call-start = ((), (), s32[]{:S(2)}) async-start(), calls=%async_computation.9 | async-start | bytes 29196288
  651.9 614.7 %reduce-scatter.21.cloned.1.call-start = ((), (), s32[]{:S(2)}) async-start(), calls=%async_computation.10 | async-start | bytes 29196288
  709.5 725.7 %all-gather.14.cloned.1.call-start = ((), (), s32[]{:S(2)}) async-start(), calls=%async_computation.8 | async-start | bytes 29196288 | tf_op jit(solution)/reshape | solution.py:58
  712.2 6.2 copy-start
  714.9 1.2 copy-start.1
  1268.7 1.2 copy-start.2
  1310.1 250.5 %all-gather.10.cloned.1.call-start = ((), (), s32[]{:S(2)}) async-start(), calls=%async_computation.6 | async-start | bytes 29196288 | tf_op jit(solution)/reshape | solution.py:58
  1324.0 362.0 %all-gather.12.cloned.1.call-start = ((), (), s32[]{:S(2)}) async-start(), calls=%async_computation.7 | async-start | bytes 29196288 | tf_op jit(solution)/reshape | solution.py:58
  1686.0 46.4 %slice-start = ((s8[25952256]{0:T(1024)(128)(4,1)}), s8[4194304]{0:T(1024)(128)(4,1)S(1)}, s32[]{:S(2)}) async-start(s8[25952256]{0:T(1024)(128)(4,1)} %bitcast.335), calls=%async_computation.15 | async-start | bytes 8388608
  1686.0 46.4 %slice-start.1 = ((s8[25952256]{0:T(1024)(128)(4,1)}), s8[4194304]{0:T(1024)(128)(4,1)S(1)}, s32[]{:S(2)}) async-start(s8[25952256]{0:T(1024)(128)(4,1)} %bitcast.335), calls=%async_computation.16 | async-start | bytes 8388608
  1686.0 46.4 %slice-start.2 = ((s8[25952256]{0:T(1024)(128)(4,1)}), s8[4194304]{0:T(1024)(128)(4,1)S(1)}, s32[]{:S(2)}) async-start(s8[25952256]{0:T(1024)(128)(4,1)} %bitcast.335), calls=%async_computation.17 | async-start | bytes 8388608
  1686.0 46.4 %slice-start.3 = ((s8[25952256]{0:T(1024)(128)(4,1)}), s8[4194304]{0:T(1024)(128)(4,1)S(1)}, s32[]{:S(2)}) async-start(s8[25952256]{0:T(1024)(128)(4,1)} %bitcast.335), calls=%async_computation.18 | async-start | bytes 8388608
  1709.8 22.6 %slice-start.4 = ((s8[25952256]{0:T(1024)(128)(4,1)}), s8[4194304]{0:T(1024)(128)(4,1)S(1)}, s32[]{:S(2)}) async-start(s8[25952256]{0:T(1024)(128)(4,1)} %bitcast.335), calls=%async_computation.19 | async-start | bytes 8388608
  1709.8 22.6 %slice-start.5 = ((s8[25952256]{0:T(1024)(128)(4,1)}), s8[4194304]{0:T(1024)(128)(4,1)S(1)}, s32[]{:S(2)}) async-start(s8[25952256]{0:T(1024)(128)(4,1)} %bitcast.335), calls=%async_computation.20 | async-start | bytes 8388608
  1709.8 22.6 %slice-start.6 = ((s8[25952256]{0:T(1024)(128)(4,1)}), s8[786432]{0:T(1024)(128)(4,1)S(1)}, s32[]{:S(2)}) async-start(s8[25952256]{0:T(1024)(128)(4,1)} %bitcast.335), calls=%async_computation.21 | async-start | bytes 1572864
Sparse Core Ops, SparseCore 0:
  283.9 154.2 reduce-scatter.26
  489.0 155.8 reduce-scatter.28
  648.5 151.4 reduce-scatter.22
  804.0 151.4 reduce-scatter.24
  959.5 151.5 reduce-scatter.18
  1115.1 151.4 reduce-scatter.20
  1310.2 124.8 all-gather.13
  1437.6 122.9 all-gather.9
  1563.0 122.9 all-gather.11
where the time goes:
time: 1760 us; the launch traced here: 1750 us
  waiting for transfers between devices  890 us (51%)
  matrix products  602 us (34%)
  other arithmetic  137 us (8%)
  local copies, waits for them, and re-layouts  79.3 us (5%)
  blocking collectives  22.2 us (1%)
    unnamed x15, waiting for transfers between devices  539 us
    reshape x3, waiting for transfers between devices, step(): t.reshape(-1, *t.shape[2:])  351 us
    dot_general x5, matrix products, layer(): gate = jnp.dot(a, w['w_gate'], preferred_element_type=jnp.float32)  208 us
    dot_general x5, matrix products, layer(): up = jnp.dot(a, w['w_up'], preferred_element_type=jnp.float32)  198 us
    dot_general x5, matrix products, matmul(): jnp.dot(a, w, preferred_element_type=jnp.float32).astype(jnp.bfloat16)  196 us
    unnamed x47, local copies, waits for them, and re-layouts  79.3 us
    unnamed x5, other arithmetic  74.1 us
    reshape x3, other arithmetic, step(): t.reshape(-1, *t.shape[2:])  36.4 us
  transfers between devices with their start and end apart: 9, of which 7 were waited for; matrix products, arithmetic and copies ran while one was open for 27% of the time, Pallas kernels for 0%

commit v1 on v0

v1 whole, which is shorter than its diff:
```python
import functools

import jax
import jax.numpy as jnp
from jax import lax
from jax.experimental import pallas as pl
from jax.experimental.pallas import tpu as pltpu
from jax.sharding import PartitionSpec as P


BF = jnp.bfloat16
F32 = jnp.float32
MESH = pl.DeviceIdType.MESH
TOKENS, D, FF, LAYERS = 2048, 1536, 4224, 2
BLOCK = 256
STEPS = -(-FF // BLOCK)
LAST = FF - (STEPS - 1) * BLOCK
PART = D // 8
SUB = BLOCK // 8
OWN_DOWN = FF // 8
LAST_SUB = OWN_DOWN - (STEPS - 1) * SUB
HALF = PART // 2
CHUNK = PART + HALF
COUNT = 3 * LAYERS * D * FF
VMEM_LIMIT = 67043328


ANY = pl.BlockSpec(memory_space=pl.ANY)
PIECES = [(n, l) for n in range(3) for l in range(LAYERS)]


def dot(a, b, ca, cb):
    return lax.dot_general(a, b, (((ca,), (cb,)), ((), ())), preferred_element_type=F32)


def resident(shape):
    return pl.BlockSpec(shape, lambda *_: (0,) * len(shape), pipeline_mode=pl.Buffered(1))


def cost(units, bytes_accessed):
    return pl.CostEstimate(flops=int(units * 2 * TOKENS * D * FF), bytes_accessed=int(bytes_accessed), transcendentals=0)


def normed(h):
    wide = h.astype(F32)
    scale = lax.rsqrt(jnp.mean(wide * wide, -1, keepdims=True) + 1e-6)
    return (wide * scale).astype(BF)


def forward_kernel(with_down, h_ref, wg_ref, wu_ref, *refs):
    if with_down:
        wd_ref, a_out, ht_ref, sl_ref, q_ref, next_out, a_ref, hid_ref, acc_ref, sems = refs
    else:
        a_out, ht_ref, sl_ref, q_ref, a_ref, hid_ref, sems = refs
    j = pl.program_id(0)
    keep = pltpu.make_async_copy(a_ref, a_out, sems.at[0])

    @pl.when(j == 0)
    def _():
        @pl.loop(0, TOKENS // 256)
        def _(i):
            r = pl.ds(pl.multiple_of(i * 256, 256), 256)
            a_ref[r, :] = normed(h_ref[r, :])

        keep.start()
        if with_down:
            acc_ref[...] = jnp.zeros_like(acc_ref)

    for i in range(4):
        r = slice(512 * i, 512 * i + 512)
        g = dot(a_ref[r, :], wg_ref[0], 1, 0)
        u = dot(a_ref[r, :], wu_ref[0], 1, 0)
        s = jax.nn.sigmoid(g)
        sl = g * s
        sl_ref[r, :] = sl
        q_ref[r, :] = u * (s * (1.0 + g * (1.0 - s)))
        hid = (sl * u).astype(BF)
        hid_ref[r, :] = hid
        ht_ref[:, r] = hid.T

    if with_down:

        @pl.when(j < STEPS - 1)
        def _():
            acc_ref[...] += dot(hid_ref[...], wd_ref[0], 1, 0)

        @pl.when(j == STEPS - 1)
        def _():
            acc_ref[...] += dot(hid_ref[:, :LAST], wd_ref[0, :LAST, :], 1, 0)

    @pl.when(j == STEPS - 1)
    def _():
        keep.wait()
        if with_down:

            @pl.loop(0, TOKENS // 256)
            def _(i):
                r = pl.ds(pl.multiple_of(i * 256, 256), 256)
                a_ref[r, :] = h_ref[r, :] + acc_ref[r, :].astype(BF)

            move = pltpu.make_async_copy(a_ref, next_out, sems.at[1])
            move.start()
            move.wait()


def forward(l, h, wg, wu, wd=None):
    with_down = wd is not None
    column = pl.BlockSpec((1, D, BLOCK), lambda j: (l, 0, j))
    state = jax.ShapeDtypeStruct((TOKENS, D), BF)
    wide = pl.BlockSpec((TOKENS, BLOCK), lambda j: (0, j))
    in_specs = [resident((TOKENS, D)), column, column]
    out_shape = [state, jax.ShapeDtypeStruct((FF, TOKENS), BF)] + [jax.ShapeDtypeStruct((TOKENS, FF), F32)] * 2
    out_specs = [ANY, pl.BlockSpec((BLOCK, TOKENS), lambda j: (j, 0)), wide, wide]
    scratch = [pltpu.VMEM((TOKENS, D), BF), pltpu.VMEM((TOKENS, BLOCK), BF)]
    args = [h, wg, wu]
    if with_down:
        in_specs.append(pl.BlockSpec((1, BLOCK, D), lambda j: (l, j, 0)))
        out_shape.append(state)
        out_specs.append(ANY)
        scratch.append(pltpu.VMEM((TOKENS, D), F32))
        args.append(wd)
    return pl.pallas_call(
        functools.partial(forward_kernel, with_down),
        grid=(STEPS,),
        in_specs=in_specs,
        out_specs=out_specs,
        out_shape=out_shape,
        scratch_shapes=scratch + [pltpu.SemaphoreType.DMA((2,))],
        compiler_params=pltpu.CompilerParams(vmem_limit_bytes=VMEM_LIMIT),
        cost_estimate=cost(3 if with_down else 2, 130e6),
    )(*args)


class Lags:
    def __init__(self, first, second, third, b, e):
        self.first, self.second, self.third = first, second, third
        self.s = third + 1
        self.a = first + third + 2 * (first == 0)
        self.b, self.e = b, e
        self.c = second + third - 2 * first
        self.d = 2 * (third - second)


def backward_kernel(lags, with_da, a_ref, dy_ref, wd_ref, sl_ref, q_ref, ht_ref, *refs):
    if with_da:
        wg_ref, wu_ref, *refs = refs
    g_gate, g_up, g_down, sq_ref, *refs = refs
    if with_da:
        da_out, acc_ref, *refs = refs
    dgu_ref, s_ref, a2_ref, bx, by, cx, cy, ex, ey, dx, dy2, og, ou, od, *sems = refs
    s_send, a_recv, bx_send, by_send, cx_recv, cy_recv, ex_send, ey_send, dx_recv, dy_recv, out_sem, da_sem = sems
    j = pl.program_id(0)
    me = lax.axis_index("dp")
    x, y, c = lax.div(me, 4), lax.rem(lax.div(me, 2), 2), lax.rem(me, 2)
    to_core, to_x, to_y = ({"dp": me + k * (1 - 2 * t)} for k, t in ((1, c), (4, x), (2, y)))

    def remote(src, dst, send, recv, to):
        return pltpu.make_async_remote_copy(src_ref=src, dst_ref=dst, send_sem=send, recv_sem=recv, device_id=to, device_id_type=MESH)

    def pair(i):
        s, a = lax.rem(i, lags.s), lax.rem(i, lags.a)
        return remote(s_ref.at[s, :, :, :, 1 - c], a2_ref.at[a], s_send.at[s], a_recv.at[a], to_core)

    def first(i):
        b, k = lax.rem(i, lags.b), lax.rem(i, lags.c)
        return (
            remote(bx.at[b], cx.at[k], bx_send.at[b], cx_recv.at[k], to_x),
            remote(by.at[b], cy.at[k], by_send.at[b], cy_recv.at[k], to_y),
        )

    def second(i):
        e, k = lax.rem(i, lags.e), lax.rem(i, lags.d)
        return (
            remote(ex.at[e], dx.at[k], ex_send.at[e], dx_recv.at[k], to_x),
            remote(ey.at[e], dy2.at[k], ey_send.at[e], dy_recv.at[k], to_y),
        )

    def outs(i, last):
        o = lax.rem(i, 2)
        if last:
            wide, deep = pl.ds((STEPS - 1) * BLOCK, LAST), pl.ds((STEPS - 1) * SUB, LAST_SUB)
            srcs = og.at[o, :, pl.ds(0, LAST)], ou.at[o, :, pl.ds(0, LAST)], od.at[o, pl.ds(0, LAST_SUB)]
        else:
            wide, deep = pl.ds(pl.multiple_of(i * BLOCK, BLOCK), BLOCK), pl.ds(pl.multiple_of(i * SUB, SUB), SUB)
            srcs = og.at[o], ou.at[o], od.at[o]
        dsts = g_gate.at[:, wide], g_up.at[:, wide], g_down.at[deep]
        return [pltpu.make_async_copy(s, d, out_sem.at[o, n]) for n, (s, d) in enumerate(zip(srcs, dsts))]

    def total(*terms):
        return functools.reduce(lambda p, q: p + q, [t.astype(F32) for t in terms])

    def take_first(i):
        pair(i).wait()
        s, a, b = lax.rem(i, lags.s), lax.rem(i, lags.a), lax.rem(i, lags.b)

        @pl.when(i >= lags.b)
        def _():
            for copy in first(i - lags.b):
                copy.wait_send()

        for t in range(2):
            bx[b, t, :PART] = total(s_ref[s, 0, 1 - x, t, c], a2_ref[a, 0, 1 - x, t]).astype(BF)
            bx[b, t, PART:] = total(s_ref[s, 2, 1 - x, t, c, :HALF], a2_ref[a, 2, 1 - x, t, :HALF]).astype(BF)
            by[b, t, :PART] = total(s_ref[s, 1, t, 1 - y, c], a2_ref[a, 1, t, 1 - y]).astype(BF)
            by[b, t, PART:] = total(s_ref[s, 2, t, 1 - y, c, HALF:], a2_ref[a, 2, t, 1 - y, HALF:]).astype(BF)
        for copy in first(i):
            copy.start()

    def take_second(i):
        for copy in first(i):
            copy.wait_recv()
        s, a, k, e = lax.rem(i, lags.s), lax.rem(i, lags.a), lax.rem(i, lags.c), lax.rem(i, lags.e)

        @pl.when(i >= lags.e)
        def _():
            for copy in second(i - lags.e):
                copy.wait_send()

        ey[e, :PART] = total(s_ref[s, 0, x, 1 - y, c], a2_ref[a, 0, x, 1 - y], cx[k, 1 - y, :PART]).astype(BF)
        ey[e, PART:] = total(s_ref[s, 2, x, 1 - y, c, :HALF], a2_ref[a, 2, x, 1 - y, :HALF], cx[k, 1 - y, PART:]).astype(BF)
        ex[e, :PART] = total(s_ref[s, 1, 1 - x, y, c], a2_ref[a, 1, 1 - x, y], cy[k, 1 - x, :PART]).astype(BF)
        ex[e, PART:] = total(s_ref[s, 2, 1 - x, y, c, HALF:], a2_ref[a, 2, 1 - x, y, HALF:], cy[k, 1 - x, PART:]).astype(BF)
        for copy in second(i):
            copy.start()

    def take_third(i):
        for copy in second(i):
            copy.wait_recv()
        s, a, k, d, o = (lax.rem(i, n) for n in (lags.s, lags.a, lags.c, lags.d, 2))

        @pl.when(i >= 2)
        def _():
            for copy in outs(i - 2, False):
                copy.wait()

        gate = total(s_ref[s, 0, x, y, c], a2_ref[a, 0, x, y], cx[k, y, :PART], dy2[d, :PART]).astype(BF)
        up = total(s_ref[s, 1, x, y, c], a2_ref[a, 1, x, y], cy[k, x, :PART], dx[d, :PART]).astype(BF)
        og[o] = gate
        ou[o] = up
        low = total(s_ref[s, 2, x, y, c, :HALF], a2_ref[a, 2, x, y, :HALF], cx[k, y, PART:], dy2[d, PART:]).astype(BF)
        high = total(s_ref[s, 2, x, y, c, HALF:], a2_ref[a, 2, x, y, HALF:], cy[k, x, PART:], dx[d, PART:]).astype(BF)
        downs = [half[SUB * n : SUB * n + SUB] for half in (low, high) for n in range(HALF // SUB)]
        for n, one in enumerate(downs):
            od[o, :, BLOCK * n : BLOCK * n + BLOCK] = one

        def squares(t):
            wide = t.astype(F32)
            return jnp.sum((wide * wide).reshape(-1, 8, t.shape[-1]), 0)

        @pl.when(i < STEPS - 1)
        def _():
            sq_ref[...] += squares(gate) + squares(up) + squares(low) + squares(high)
            for copy in outs(i, False):
                copy.start()

        @pl.when(i == STEPS - 1)
        def _():
            sq_ref[:, :LAST] += squares(gate[:, :LAST]) + squares(up[:, :LAST])
            sq_ref[...] += sum(squares(one[:LAST_SUB]) for one in downs)
            for copy in outs(i, True):
                copy.start()

    @pl.when(j == 0)
    def _():
        sq_ref[...] = jnp.zeros_like(sq_ref)
        if with_da:
            acc_ref[...] = jnp.zeros_like(acc_ref)
        barrier = pltpu.get_barrier_semaphore()
        for to in (to_core, to_x, to_y):
            pl.semaphore_signal(barrier, inc=1, device_id=to, device_id_type=MESH)
        pl.semaphore_wait(barrier, 3)

    @pl.when(j < STEPS)
    def _():
        s = lax.rem(j, lags.s)
        for i in range(4):
            r = slice(512 * i, 512 * i + 512)
            dh = dot(dy_ref[r, :], wd_ref[0], 1, 1).astype(BF).astype(F32)
            dgu_ref[r, :BLOCK] = (dh * q_ref[r, :]).astype(BF)
            dgu_ref[r, BLOCK:] = (dh * sl_ref[r, :]).astype(BF)
        for h in range(2):
            gu = dot(a_ref[:, D // 2 * h : D // 2 * (h + 1)], dgu_ref[...], 0, 0)
            for o in range(4):
                for t in range(2):
                    s_ref[s, t, h, o // 2, o % 2] = gu[PART * o : PART * o + PART, BLOCK * t : BLOCK * t + BLOCK].astype(BF)
        for h in range(2):
            down = dot(ht_ref[...].reshape(BLOCK, TOKENS), dy_ref[:, D // 2 * h : D // 2 * (h + 1)], 1, 0)
            for o in range(8):
                for n in range(3):
                    s_ref[s, 2, o // 4, o // 2 % 2, o % 2, SUB * (3 * h + n) : SUB * (3 * h + n + 1)] = down[
                        SUB * o : SUB * o + SUB, BLOCK * n : BLOCK * n + BLOCK
                    ].astype(BF)
        if lags.first == 0:
            pair(j).start()

    if with_da:

        def add_da(width):
            for i in range(4):
                r = slice(512 * i, 512 * i + 512)
                acc_ref[r, :] += dot(dgu_ref[r, :width], wg_ref[0, :, :width], 1, 1) + dot(
                    dgu_ref[r, BLOCK : BLOCK + width], wu_ref[0, :, :width], 1, 1
                )

        pl.when(j < STEPS - 1)(functools.partial(add_da, BLOCK))
        pl.when(j == STEPS - 1)(functools.partial(add_da, LAST))

    pl.when((j >= lags.third) & (j < STEPS + lags.third))(lambda: take_third(j - lags.third))
    pl.when((j >= lags.second) & (j < STEPS + lags.second))(lambda: take_second(j - lags.second))
    pl.when((j >= lags.first) & (j < STEPS + lags.first))(lambda: take_first(j - lags.first))
    if lags.first > 0:
        pl.when(j < STEPS)(lambda: pair(j).start())

    if with_da:

        @pl.when(j == STEPS)
        def _():
            for n in range(3):
                wide = slice(512 * n, 512 * n + 512)
                dgu_ref[...] = acc_ref[:, wide].astype(BF)
                move = pltpu.make_async_copy(dgu_ref, da_out.at[:, pl.ds(512 * n, 512)], da_sem)
                move.start()
                move.wait()

    @pl.when(j == STEPS + lags.third - 1)
    def _():
        for i in range(STEPS - lags.b, STEPS):
            for copy in first(jnp.int32(i)):
                copy.wait_send()
        for i in range(STEPS - lags.e, STEPS):
            for copy in second(jnp.int32(i)):
                copy.wait_send()
        for i in range(STEPS - 2, STEPS):
            for copy in outs(jnp.int32(i), i == STEPS - 1):
                copy.wait()


def backward(l, lags, a, dy, wd, sl, q, ht, wg=None, wu=None):
    with_da = wg is not None
    at = lambda j: jnp.minimum(j, STEPS - 1)
    wide = pl.BlockSpec((TOKENS, BLOCK), lambda j: (0, at(j)))
    in_specs = [
        resident((TOKENS, D)),
        resident((TOKENS, D)),
        pl.BlockSpec((1, BLOCK, D), lambda j: (l, at(j), 0)),
        wide,
        wide,
        pl.BlockSpec((8, SUB, TOKENS), lambda j: (0, at(j), 0)),
    ]
    args = [a, dy, wd, sl, q, ht.reshape(8, OWN_DOWN, TOKENS)]
    out_shape = [jax.ShapeDtypeStruct((PART, FF), BF)] * 2 + [jax.ShapeDtypeStruct((OWN_DOWN, D), BF), jax.ShapeDtypeStruct((8, BLOCK), F32)]
    out_specs = [ANY] * 3 + [pl.BlockSpec((8, BLOCK), lambda j: (0, 0))]
    scratch = []
    if with_da:
        column = pl.BlockSpec((1, D, BLOCK), lambda j: (l, 0, at(j)))
        in_specs += [column, column]
        args += [wg, wu]
        out_shape.append(jax.ShapeDtypeStruct((TOKENS, D), BF))
        out_specs.append(ANY)
        scratch.append(pltpu.VMEM((TOKENS, D), F32))
    piece = (PART, BLOCK)
    scratch += [
        pltpu.VMEM((TOKENS, 2 * BLOCK), BF),
        pltpu.VMEM((lags.s, 3, 2, 2, 2) + piece, BF),
        pltpu.VMEM((lags.a, 3, 2, 2) + piece, BF),
        *[pltpu.VMEM((lags.b, 2, CHUNK, BLOCK), BF)] * 2,
        *[pltpu.VMEM((lags.c, 2, CHUNK, BLOCK), BF)] * 2,
        *[pltpu.VMEM((lags.e, CHUNK, BLOCK), BF)] * 2,
        *[pltpu.VMEM((lags.d, CHUNK, BLOCK), BF)] * 2,
        *[pltpu.VMEM((2,) + piece, BF)] * 2,
        pltpu.VMEM((2, SUB, D), BF),
    ]
    counts = (lags.s, lags.a, lags.b, lags.b, lags.c, lags.c, lags.e, lags.e, lags.d, lags.d)
    scratch += [pltpu.SemaphoreType.DMA((n,)) for n in counts]
    scratch += [pltpu.SemaphoreType.DMA((2, 3)), pltpu.SemaphoreType.DMA]
    return pl.pallas_call(
        functools.partial(backward_kernel, lags, with_da),
        grid=(STEPS + lags.third,),
        in_specs=in_specs,
        out_specs=out_specs,
        out_shape=out_shape,
        scratch_shapes=scratch,
        compiler_params=pltpu.CompilerParams(vmem_limit_bytes=VMEM_LIMIT, collective_id=l, has_side_effects=True),
        cost_estimate=cost(6 if with_da else 4, 150e6),
    )(*args)


def factor_kernel(p_ref, q_ref, f_ref, buf, send, recv):
    me = lax.axis_index("dp")
    barrier = pltpu.get_barrier_semaphore()
    peers = [lax.rem(me + k, 8) for k in range(1, 8)]
    for peer in peers:
        pl.semaphore_signal(barrier, inc=1, device_id={"dp": peer}, device_id_type=MESH)
    both = p_ref[...] + q_ref[...]
    buf[me] = both[:, :128] + both[:, 128:]
    pl.semaphore_wait(barrier, 7)

    def copy(k):
        return pltpu.make_async_remote_copy(
            src_ref=buf.at[me], dst_ref=buf.at[me], send_sem=send.at[k], recv_sem=recv.at[k], device_id={"dp": peers[k]}, device_id_type=MESH
        )

    for k in range(7):
        copy(k).start()
    for k in range(7):
        copy(k).wait()
    every = buf[0]
    for k in range(1, 8):
        every = every + buf[k]
    total = jnp.sum(jnp.sum(every, axis=1, keepdims=True), axis=0, keepdims=True)
    f_ref[...] = jnp.broadcast_to(jnp.minimum(1.0, 0.5 * lax.rsqrt(total / COUNT + 1e-30)), (8, 128))


def clip_factor(p, q):
    return pl.pallas_call(
        factor_kernel,
        in_specs=[pl.BlockSpec(memory_space=pltpu.VMEM)] * 2,
        out_specs=pl.BlockSpec(memory_space=pltpu.VMEM),
        out_shape=jax.ShapeDtypeStruct((8, 128), F32),
        scratch_shapes=[pltpu.VMEM((8, 8, 128), F32), pltpu.SemaphoreType.DMA((7,)), pltpu.SemaphoreType.DMA((7,))],
        compiler_params=pltpu.CompilerParams(collective_id=2, has_side_effects=True),
        name="factor",
    )(p, q)


def adamw_kernel(at_ref, f_ref, g_ref, w_ref, m_ref, v_ref, *refs):
    nw_ref, nm_ref, nv_ref = refs[-3:]
    g = g_ref[...].astype(F32) * f_ref[0:1, 0:1]
    w = w_ref[0].astype(F32)
    m = 0.9 * m_ref[0] + 0.1 * g
    v = 0.95 * v_ref[0] + 0.05 * g * g
    nm_ref[0] = m
    nv_ref[0] = v
    nw_ref[...] = (w - 0.02 * (m * lax.rsqrt(v + 1e-8) + 0.1 * w)).astype(BF)


def adamw(l, at, factor, g, w, m, v, so_far=None):
    rows, columns = g.shape
    deep = rows // 3
    moment = pl.BlockSpec((1, deep, columns), lambda i, at: (l, i, 0))
    flat = pl.BlockSpec((deep, columns), lambda i, at: (i, 0))
    in_specs = [
        pl.BlockSpec((8, 128), lambda i, at: (0, 0)),
        flat,
        pl.BlockSpec((1, deep, columns), lambda i, at: (l, 3 * at[0] + i, 0)),
        moment,
        moment,
    ]
    args = [factor, g, w, m, v]
    aliases = {}
    if so_far is not None:
        in_specs += [ANY, ANY]
        args += so_far
        aliases = {6: 1, 7: 2}
    return pl.pallas_call(
        adamw_kernel,
        grid_spec=pltpu.PrefetchScalarGridSpec(num_scalar_prefetch=1, grid=(3,), in_specs=in_specs, out_specs=[flat, moment, moment]),
        out_shape=[jax.ShapeDtypeStruct(g.shape, BF)] + [jax.ShapeDtypeStruct(m.shape, F32)] * 2,
        input_output_aliases=aliases,
        compiler_params=pltpu.CompilerParams(vmem_limit_bytes=48 << 20),
        cost_estimate=cost(0.1, 22 * rows * columns),
    )(at, *args)


def place_kernel(n, owners_ref, *refs):
    out_ref = refs[-1]
    s = pl.program_id(0)
    for k in range(n):

        @pl.when(s == k)
        def _():
            out_ref[0] = refs[k][...]


def place(l, owners, pieces, so_far):
    n = len(pieces)
    rows, columns = pieces[0].shape
    cut = 1 if n > 1 else 3
    deep = rows // cut
    in_specs = [
        pl.BlockSpec((deep, columns), lambda s, i, own, k=k: (jnp.where(s == k, i, jnp.where(s < k, 0, cut - 1)), 0)) for k in range(n)
    ]
    args = list(pieces)
    aliases = {}
    if so_far is not None:
        in_specs.append(ANY)
        args.append(so_far)
        aliases = {n + 1: 0}
    return pl.pallas_call(
        functools.partial(place_kernel, n),
        grid_spec=pltpu.PrefetchScalarGridSpec(
            num_scalar_prefetch=1,
            grid=(n, cut),
            in_specs=in_specs,
            out_specs=pl.BlockSpec((1, deep, columns), lambda s, i, own: (l, cut * own[s] + i, 0)),
        ),
        out_shape=jax.ShapeDtypeStruct((LAYERS, 8 * rows, columns), BF),
        input_output_aliases=aliases,
        compiler_params=pltpu.CompilerParams(vmem_limit_bytes=48 << 20),
        cost_estimate=cost(0.1 * n, 4 * n * rows * columns),
    )(owners, *args)


def solution(mesh):
    def swap(t, mask):
        return lax.ppermute(t, "dp", [(i, i ^ mask) for i in range(8)])

    def step(x, dy, wg, wu, wd, mg, mu, md, vg, vu, vd):
        x, dy = x[0], dy[0]
        me = lax.axis_index("dp")
        a0, ht0, sl0, q0, h1 = forward(0, x, wg, wu, wd)
        a1, ht1, sl1, q1 = forward(1, h1, wg, wu)
        g1 = backward(1, Lags(0, 1, 2, 2, 2), a1, dy, wd, sl1, q1, ht1, wg, wu)
        _, back = jax.vjp(normed, h1)
        dh1 = dy + back(g1[4])[0]
        g0 = backward(0, Lags(1, 3, 4, 3, 3), a0, dh1, wd, sl0, q0, ht0)
        factor = clip_factor(g0[3], g1[3])
        at = me[None].astype(jnp.int32)
        owners = {k: (me ^ k).astype(jnp.int32) for k in range(8)}
        mats = ((wg, mg, vg), (wu, mu, vu), (wd, md, vd))
        moments, whole = [None] * 3, [None] * 3

        def put(n, l, have, group):
            whole[n] = place(l, jnp.stack([owners[k] for k in group]), [have[k] for k in group], whole[n])

        everything = []
        for number, (n, l) in enumerate(PIECES):
            have = {}
            everything.append(have)
            have[0], *moments[n] = adamw(l, at, factor, (g0, g1)[l][n], *mats[n], moments[n])
            have[4] = swap(have[0], 4)
            have[2] = swap(have[0], 2)
            have[6] = swap(have[4], 2) if number % 2 else swap(have[2], 4)
            for k in (0, 4, 2, 6):
                have[k + 1] = swap(have[k], 1)
            put(n, l, have, (0, 1))
            put(n, l, have, (4, 2, 5, 3))
        for number, (n, l) in enumerate(PIECES):
            put(n, l, everything[number], (6,))
            put(n, l, everything[number], (7,))
        new_w, new_m, new_v = whole, [m[0] for m in moments], [m[1] for m in moments]
        return tuple(new_w + new_m + new_v)

    whole, rows = P(None, None, None), P(None, "dp", None)
    return jax.shard_map(
        step,
        mesh=mesh,
        in_specs=(P(("rep", "dp")),) * 2 + (whole,) * 3 + (rows,) * 6,
        out_specs=(P("rep"),) * 3 + (P("rep", "dp"),) * 6,
        check_vma=False,
    )
```

time: 1760 us -> 1010 us (0.57)
  Pallas kernels: 0 us -> 704 us
  waiting for transfers between devices: 890 us -> 240 us
  matrix products: 602 us -> 0 us
  other arithmetic: 137 us -> 18.5 us
  local copies, waits for them, and re-layouts: 79.3 us -> 13.9 us
  blocking collectives: 22.2 us -> 0 us
  starting transfers between devices: 0.58 us -> 22.5 us
    pallas_call x0 -> x35, Pallas kernels: none -> 704 us  [the longest x2 401 us: backward(): pl.pallas_call(functools.partial(backward_kernel, lags, with_da), grid=(S...]
    dot_general x15 -> x0, matrix products: 602 us -> none  [the longest x5 208 us: layer(): gate = jnp.dot(a, w['w_gate'], preferred_element_type=jnp.float32)]
    unnamed x15 -> x0, waiting for transfers between devices: 539 us -> none
    reshape x3 -> x0, waiting for transfers between devices: 351 us -> none  [step(): t.reshape(-1, *t.shape[2:])]
    ppermute x0 -> x42, waiting for transfers between devices: none -> 240 us  [swap(): return lax.ppermute(t, 'dp', [(i, i ^ mask) for i in range(8)])]
    unnamed x5 -> x0, other arithmetic: 74.1 us -> none
    unnamed x47 -> x64, local copies, waits for them, and re-layouts: 79.3 us -> 13.9 us
    reshape x3 -> x0, other arithmetic: 36.4 us -> none  [step(): t.reshape(-1, *t.shape[2:])]
  transfers between devices with their start and end apart: 9 -> 42, of which waited for: 7 -> 14; matrix products, arithmetic and copies ran while one was open for 27% -> 0% of each run, Pallas kernels for 0% -> 11%
where the time goes in v1:
time: 1010 us; the launch traced here: 999 us
  Pallas kernels  704 us (70%)
  waiting for transfers between devices  240 us (24%)
  starting transfers between devices  22.5 us (2%)
  other arithmetic  18.5 us (2%)
  local copies, waits for them, and re-layouts  13.9 us (1%)
    pallas_call x2, Pallas kernels, backward(): pl.pallas_call(functools.partial(backward_kernel, lags, with_da), grid=(S...  401 us
    ppermute x42, waiting for transfers between devices, swap(): return lax.ppermute(t, 'dp', [(i, i ^ mask) for i in range(8)])  240 us
    pallas_call x2, Pallas kernels, forward(): pl.pallas_call(functools.partial(forward_kernel, with_down), grid=(STEPS,...  174 us
    pallas_call x24, Pallas kernels, place(): pl.pallas_call(functools.partial(place_kernel, n), grid_spec=pltpu.Prefet...  76.8 us
    pallas_call x6, Pallas kernels, adamw(): pl.pallas_call(adamw_kernel, grid_spec=pltpu.PrefetchScalarGridSpec(num_s...  45.6 us
    ppermute x42, starting transfers between devices, swap(): return lax.ppermute(t, 'dp', [(i, i ^ mask) for i in range(8)])  22.5 us
  transfers between devices with their start and end apart: 42, of which 14 were waited for; matrix products, arithmetic and copies ran while one was open for 0% of the time, Pallas kernels for 11%

profile of v1, /device:TPU:0, one launch (start us, length us, event | category | flops | bytes accessed | tf_op | source)
XLA Modules:
  0.0 999.2 jit_solution(10654843653779548492)
XLA Ops:
  0.6 104.6 %shard_map.178 = (bf16[2048,1536]{1,0:T(8,128)(2,1)}, bf16[4224,2048]{1,0:T(8,128)(2,1)}, f32[2048,4224]{1,0:T(8,128)}, f32[2048,4224]{1,0:T(8,128)}, bf16[2048,1536]{1,0:T(8,128)(2,1)}) custom-call(bf16[2048,1536]{1,0:T(8,128)(2,1)} %bitcast.14, bf16[2,1536,4224]{2,1,0:T(8,128)(2,1)} %w_ref.7, bf16[2,1536,4224]{2,1,0:T(8,128)(2,1)} %w_ref.9, ...), custom_call_target="tpu_custom_call" | custom-call | flops 79725330432 | bytes 130000000 | tf_op jit(solution)/shard_map/pallas_call | solution.py:122
  105.3 69.0 %shard_map.179 = (bf16[2048,1536]{1,0:T(8,128)(2,1)}, bf16[4224,2048]{1,0:T(8,128)(2,1)}, f32[2048,4224]{1,0:T(8,128)}, f32[2048,4224]{1,0:T(8,128)}) custom-call(bf16[2048,1536]{1,0:T(8,128)(2,1)} %get-tuple-element.46.h_ref, bf16[2,1536,4224]{2,1,0:T(8,128)(2,1)} %w_ref.7, bf16[2,1536,4224]{2,1,0:T(8,128)(2,1)} %w_ref.9), custom_call_target="tpu_custom_call" | custom-call | flops 53150220288 | bytes 130000000 | tf_op jit(solution)/shard_map/pallas_call | solution.py:122
  174.3 213.3 %shard_map.180 = (bf16[192,4224]{1,0:T(8,128)(2,1)}, bf16[192,4224]{1,0:T(8,128)(2,1)}, bf16[528,1536]{1,0:T(8,128)(2,1)}, f32[8,256]{1,0:T(8,128)}, bf16[2048,1536]{1,0:T(8,128)(2,1)}) custom-call(bf16[2048,1536]{1,0:T(8,128)(2,1)} %get-tuple-element.47.a_ref, bf16[2048,1536]{1,0:T(8,128)(2,1)} %bitcast.13, bf16[2,4224,1536]{2,1,0:T(8,128)(2,1)} %w_ref.11, ...), custom_call_target="tpu_custom_call" | custom-call | flops 159450660864 | bytes 150000000 | tf_op jit(solution)/shard_map/pallas_call | solution.py:376
  387.6 7.2 fusion
  394.8 11.1 %fusion.3.dy_ref = bf16[2048,1536]{1,0:T(8,128)(2,1)} fusion(bf16[2048,1536]{1,0:T(8,128)(2,1)} %get-tuple-element.46.h_ref, bf16[2048,1536]{1,0:T(8,128)(2,1)} %get-tuple-element.51, f32[2048]{0:T(1024)S(1)} %get-tuple-element.84, f32[2048]{0:T(1024)S(1)} %get-tuple-element.83, bf16[1,2048,1536]{2,1,0:T(8,128)(2,1)} %param.12), kind=kLoop, calls=%fused_computation.8 | loop fusion | flops 25165824 | bytes 25182208 | tf_op jit(solution)/shard_map/add | solution.py:515
  405.9 188.1 %shard_map.181 = (bf16[192,4224]{1,0:T(8,128)(2,1)}, bf16[192,4224]{1,0:T(8,128)(2,1)}, bf16[528,1536]{1,0:T(8,128)(2,1)}, f32[8,256]{1,0:T(8,128)}) custom-call(bf16[2048,1536]{1,0:T(8,128)(2,1)} %get-tuple-element.45.a_ref, bf16[2048,1536]{1,0:T(8,128)(2,1)} %fusion.3.dy_ref, bf16[2,4224,1536]{2,1,0:T(8,128)(2,1)} %w_ref.11, ...), custom_call_target="tpu_custom_call" | custom-call | flops 106300440576 | bytes 150000000 | tf_op jit(solution)/shard_map/pallas_call | solution.py:376
  594.0 6.1 factor.1.f_ref
  602.2 7.4 shard_map.202
  611.8 7.5 shard_map.203
  620.4 7.4 shard_map.192
  629.9 18.2 %collective-permute-done.38.refs_0_ = bf16[528,1536]{1,0:T(8,128)(2,1)} collective-permute-done((bf16[528,1536]{1,0:T(8,128)(2,1)S(1)}, bf16[528,1536]{1,0:T(8,128)(2,1)}, u32[]{:S(2)}, u32[]{:S(2)}) %collective-permute-start.38) | collective-permute-done | bytes 1622048 | tf_op jit(solution)/shard_map/ppermute | solution.py:506
  653.5 7.4 shard_map.193
  660.9 8.7 shard_map.182
  669.5 13.3 %collective-permute-done.28.refs_0_ = bf16[528,1536]{1,0:T(8,128)(2,1)S(1)} collective-permute-done((bf16[528,1536]{1,0:T(8,128)(2,1)S(1)}, bf16[528,1536]{1,0:T(8,128)(2,1)S(1)}, u32[]{:S(2)}, u32[]{:S(2)}) %collective-permute-start.28) | collective-permute-done | bytes 1622048 | tf_op jit(solution)/shard_map/ppermute | solution.py:506
  685.9 31.8 %collective-permute-done.24.refs_0_ = bf16[192,4224]{1,0:T(8,128)(2,1)} collective-permute-done((bf16[192,4224]{1,0:T(8,128)(2,1)S(1)}, bf16[192,4224]{1,0:T(8,128)(2,1)}, u32[]{:S(2)}, u32[]{:S(2)}) %collective-permute-start.24) | collective-permute-done | bytes 1622048 | tf_op jit(solution)/shard_map/ppermute | solution.py:506
  719.7 7.3 shard_map.183
  729.2 23.2 %collective-permute-done.14.refs_0_ = bf16[192,4224]{1,0:T(8,128)(2,1)} collective-permute-done((bf16[192,4224]{1,0:T(8,128)(2,1)S(1)}, bf16[192,4224]{1,0:T(8,128)(2,1)}, u32[]{:S(2)}, u32[]{:S(2)}) %collective-permute-start.14) | collective-permute-done | bytes 1622048 | tf_op jit(solution)/shard_map/ppermute | solution.py:506
  755.6 31.6 %collective-permute-done.10.refs_0_ = bf16[192,4224]{1,0:T(8,128)(2,1)} collective-permute-done((bf16[192,4224]{1,0:T(8,128)(2,1)}, bf16[192,4224]{1,0:T(8,128)(2,1)}, u32[]{:S(2)}, u32[]{:S(2)}) %collective-permute-start.10) | collective-permute-done | bytes 1622048 | tf_op jit(solution)/shard_map/ppermute | solution.py:506
  790.2 2.4 shard_map.204.refs_4_
  792.8 2.4 shard_map.194.refs_4_
  796.4 24.9 %collective-permute-done.refs_0_ = bf16[192,4224]{1,0:T(8,128)(2,1)} collective-permute-done((bf16[192,4224]{1,0:T(8,128)(2,1)S(1)}, bf16[192,4224]{1,0:T(8,128)(2,1)}, u32[]{:S(2)}, u32[]{:S(2)}) %collective-permute-start) | collective-permute-done | bytes 1622048 | tf_op jit(solution)/shard_map/ppermute | solution.py:506
  821.9 3.8 shard_map.184.refs_4_
  825.7 6.0 shard_map.205.refs_2_
  831.7 2.4 shard_map.206.refs_4_
  837.1 5.1 shard_map.207.refs_1_
  842.5 1.6 copy-done.29
  844.0 6.0 shard_map.195.refs_2_
  850.1 2.4 shard_map.196.refs_4_
  852.5 19.5 %collective-permute-done.32.refs_0_ = bf16[528,1536]{1,0:T(8,128)(2,1)S(1)} collective-permute-done((bf16[528,1536]{1,0:T(8,128)(2,1)S(1)}, bf16[528,1536]{1,0:T(8,128)(2,1)S(1)}, u32[]{:S(2)}, u32[]{:S(2)}) %collective-permute-start.32) | collective-permute-done | bytes 1622048 | tf_op jit(solution)/shard_map/ppermute | solution.py:506
  874.6 6.0 shard_map.197.refs_1_
  881.6 6.5 shard_map.185.refs_2_
  888.1 20.8 %collective-permute-done.29.refs_0_ = bf16[528,1536]{1,0:T(8,128)(2,1)S(1)} collective-permute-done((bf16[528,1536]{1,0:T(8,128)(2,1)S(1)}, bf16[528,1536]{1,0:T(8,128)(2,1)S(1)}, u32[]{:S(2)}, u32[]{:S(2)}) %collective-permute-start.29) | collective-permute-done | bytes 1622048 | tf_op jit(solution)/shard_map/ppermute | solution.py:506
  910.0 3.8 shard_map.186.refs_4_
  915.3 6.5 shard_map.187.refs_1_
  921.8 22.9 %collective-permute-done.4.refs_0_ = bf16[192,4224]{1,0:T(8,128)(2,1)S(1)} collective-permute-done((bf16[192,4224]{1,0:T(8,128)(2,1)}, bf16[192,4224]{1,0:T(8,128)(2,1)S(1)}, u32[]{:S(2)}, u32[]{:S(2)}) %collective-permute-start.4) | collective-permute-done | bytes 1622048 | tf_op jit(solution)/shard_map/ppermute | solution.py:506
  944.7 1.7 shard_map.208.refs_1_
  946.3 1.7 shard_map.198.refs_1_
  948.5 1.7 shard_map.188.refs_1_
  950.2 29.8 %collective-permute-done.1.refs_0_ = bf16[192,4224]{1,0:T(8,128)(2,1)S(1)} collective-permute-done((bf16[192,4224]{1,0:T(8,128)(2,1)}, bf16[192,4224]{1,0:T(8,128)(2,1)S(1)}, u32[]{:S(2)}, u32[]{:S(2)}) %collective-permute-start.1) | collective-permute-done | bytes 1622048 | tf_op jit(solution)/shard_map/ppermute | solution.py:506
  980.5 3.4 shard_map.209.refs_1_
  983.9 1.7 shard_map.210.refs_1_
  985.6 1.7 shard_map.199.refs_1_
  987.3 1.7 shard_map.200.refs_1_
  988.9 1.7 shard_map.189.refs_1_
  990.6 1.7 shard_map.190.refs_1_
  992.3 1.7 shard_map.211
  994.0 3.4 shard_map.201
  997.4 1.7 shard_map.191
  (140 shorter events, 38.8 us)
Async XLA Ops:
  609.6 18.2 %collective-permute-start.41 = (bf16[528,1536]{1,0:T(8,128)(2,1)S(1)}, bf16[528,1536]{1,0:T(8,128)(2,1)S(1)}, u32[]{:S(2)}, u32[]{:S(2)}) collective-permute-start(bf16[528,1536]{1,0:T(8,128)(2,1)S(1)} %get-tuple-element.74.refs_0_), channel_id=1, source_target_pairs={{0,1},{1,0},{2,3},{3,2},{4,5},{5,4},{6,7},{7,6}} | collective-permute-start | bytes 4866056 | tf_op jit(solution)/shard_map/ppermute | solution.py:506
  609.7 38.4 %collective-permute-start.38 = (bf16[528,1536]{1,0:T(8,128)(2,1)S(1)}, bf16[528,1536]{1,0:T(8,128)(2,1)}, u32[]{:S(2)}, u32[]{:S(2)}) collective-permute-start(bf16[528,1536]{1,0:T(8,128)(2,1)S(1)} %get-tuple-element.74.refs_0_), channel_id=1, source_target_pairs={{0,4},{1,5},{2,6},{3,7},{4,0},{5,1},{6,2},{7,3}} | collective-permute-start | bytes 4866056 | tf_op jit(solution)/shard_map/ppermute | solution.py:506
  610.7 38.3 %collective-permute-start.31 = (bf16[528,1536]{1,0:T(8,128)(2,1)S(1)}, bf16[528,1536]{1,0:T(8,128)(2,1)S(1)}, u32[]{:S(2)}, u32[]{:S(2)}) collective-permute-start(bf16[528,1536]{1,0:T(8,128)(2,1)S(1)} %get-tuple-element.74.refs_0_), channel_id=1, source_target_pairs={{0,2},{1,3},{2,0},{3,1},{4,6},{5,7},{6,4},{7,5}} | collective-permute-start | bytes 4866056 | tf_op jit(solution)/shard_map/ppermute | solution.py:506
  619.4 30.7 %collective-permute-start.37 = (bf16[528,1536]{1,0:T(8,128)(2,1)S(1)}, bf16[528,1536]{1,0:T(8,128)(2,1)S(1)}, u32[]{:S(2)}, u32[]{:S(2)}) collective-permute-start(bf16[528,1536]{1,0:T(8,128)(2,1)S(1)} %get-tuple-element.73.refs_0_), channel_id=1, source_target_pairs={{0,1},{1,0},{2,3},{3,2},{4,5},{5,4},{6,7},{7,6}} | collective-permute-start | bytes 4866056 | tf_op jit(solution)/shard_map/ppermute | solution.py:506
  619.4 63.4 %collective-permute-start.28 = (bf16[528,1536]{1,0:T(8,128)(2,1)S(1)}, bf16[528,1536]{1,0:T(8,128)(2,1)S(1)}, u32[]{:S(2)}, u32[]{:S(2)}) collective-permute-start(bf16[528,1536]{1,0:T(8,128)(2,1)S(1)} %get-tuple-element.73.refs_0_), channel_id=1, source_target_pairs={{0,4},{1,5},{2,6},{3,7},{4,0},{5,1},{6,2},{7,3}} | collective-permute-start | bytes 4866056 | tf_op jit(solution)/shard_map/ppermute | solution.py:506
  620.4 33.1 %copy-start.15 = (bf16[192,4224]{1,0:T(8,128)(2,1)S(1)}, bf16[192,4224]{1,0:T(8,128)(2,1)}, u32[]{:S(2)}) copy-start(bf16[192,4224]{1,0:T(8,128)(2,1)} %get-tuple-element.63.g_ref) | copy-start | bytes 4866052
  628.9 54.8 %collective-permute-start.34 = (bf16[528,1536]{1,0:T(8,128)(2,1)S(1)}, bf16[528,1536]{1,0:T(8,128)(2,1)S(1)}, u32[]{:S(2)}, u32[]{:S(2)}) collective-permute-start(bf16[528,1536]{1,0:T(8,128)(2,1)S(1)} %get-tuple-element.73.refs_0_), channel_id=1, source_target_pairs={{0,2},{1,3},{2,0},{3,1},{4,6},{5,7},{6,4},{7,5}} | collective-permute-start | bytes 4866056 | tf_op jit(solution)/shard_map/ppermute | solution.py:506
  648.1 36.7 %collective-permute-start.27 = (bf16[192,4224]{1,0:T(8,128)(2,1)S(1)}, bf16[192,4224]{1,0:T(8,128)(2,1)S(1)}, u32[]{:S(2)}, u32[]{:S(2)}) collective-permute-start(bf16[192,4224]{1,0:T(8,128)(2,1)S(1)} %get-tuple-element.68.refs_0_), channel_id=1, source_target_pairs={{0,1},{1,0},{2,3},{3,2},{4,5},{5,4},{6,7},{7,6}} | collective-permute-start | bytes 4866056 | tf_op jit(solution)/shard_map/ppermute | solution.py:506
  649.0 68.7 %collective-permute-start.24 = (bf16[192,4224]{1,0:T(8,128)(2,1)S(1)}, bf16[192,4224]{1,0:T(8,128)(2,1)}, u32[]{:S(2)}, u32[]{:S(2)}) collective-permute-start(bf16[192,4224]{1,0:T(8,128)(2,1)S(1)} %get-tuple-element.68.refs_0_), channel_id=1, source_target_pairs={{0,4},{1,5},{2,6},{3,7},{4,0},{5,1},{6,2},{7,3}} | collective-permute-start | bytes 4866056 | tf_op jit(solution)/shard_map/ppermute | solution.py:506
  651.3 67.4 %collective-permute-start.17 = (bf16[192,4224]{1,0:T(8,128)(2,1)S(1)}, bf16[192,4224]{1,0:T(8,128)(2,1)}, u32[]{:S(2)}, u32[]{:S(2)}) collective-permute-start(bf16[192,4224]{1,0:T(8,128)(2,1)S(1)} %get-tuple-element.68.refs_0_), channel_id=1, source_target_pairs={{0,2},{1,3},{2,0},{3,1},{4,6},{5,7},{6,4},{7,5}} | collective-permute-start | bytes 4866056 | tf_op jit(solution)/shard_map/ppermute | solution.py:506
  660.9 58.8 %copy-start.10 = (bf16[192,4224]{1,0:T(8,128)(2,1)S(1)}, bf16[192,4224]{1,0:T(8,128)(2,1)}, u32[]{:S(2)}) copy-start(bf16[192,4224]{1,0:T(8,128)(2,1)} %get-tuple-element.57.g_ref) | copy-start | bytes 4866052
  682.8 44.2 %copy-start.22 = (bf16[528,1536]{1,0:T(8,128)(2,1)}, bf16[528,1536]{1,0:T(8,128)(2,1)S(1)}, u32[]{:S(2)}) copy-start(bf16[528,1536]{1,0:T(8,128)(2,1)S(1)} %collective-permute-done.28.refs_0_) | copy-start | bytes 4866052
  682.8 44.2 %collective-permute-start.23 = (bf16[192,4224]{1,0:T(8,128)(2,1)S(1)}, bf16[192,4224]{1,0:T(8,128)(2,1)S(1)}, u32[]{:S(2)}, u32[]{:S(2)}) collective-permute-start(bf16[192,4224]{1,0:T(8,128)(2,1)S(1)} %get-tuple-element.67.refs_0_), channel_id=1, source_target_pairs={{0,1},{1,0},{2,3},{3,2},{4,5},{5,4},{6,7},{7,6}} | collective-permute-start | bytes 4866056 | tf_op jit(solution)/shard_map/ppermute | solution.py:506
  683.8 35.9 %copy-start.26 = (bf16[528,1536]{1,0:T(8,128)(2,1)}, bf16[528,1536]{1,0:T(8,128)(2,1)S(1)}, u32[]{:S(2)}) copy-start(bf16[528,1536]{1,0:T(8,128)(2,1)S(1)} %collective-permute-done.34.refs_1_) | copy-start | bytes 4866052
  683.8 68.7 %collective-permute-start.14 = (bf16[192,4224]{1,0:T(8,128)(2,1)S(1)}, bf16[192,4224]{1,0:T(8,128)(2,1)}, u32[]{:S(2)}, u32[]{:S(2)}) collective-permute-start(bf16[192,4224]{1,0:T(8,128)(2,1)S(1)} %get-tuple-element.67.refs_0_), channel_id=1, source_target_pairs={{0,4},{1,5},{2,6},{3,7},{4,0},{5,1},{6,2},{7,3}} | collective-permute-start | bytes 4866056 | tf_op jit(solution)/shard_map/ppermute | solution.py:506
  684.8 42.1 %copy-start.13 = (bf16[192,4224]{1,0:T(8,128)(2,1)}, bf16[192,4224]{1,0:T(8,128)(2,1)S(1)}, u32[]{:S(2)}) copy-start(bf16[192,4224]{1,0:T(8,128)(2,1)S(1)} %collective-permute-done.27.refs_1_) | copy-start | bytes 4866052
  684.8 68.6 %collective-permute-start.20 = (bf16[192,4224]{1,0:T(8,128)(2,1)S(1)}, bf16[192,4224]{1,0:T(8,128)(2,1)}, u32[]{:S(2)}, u32[]{:S(2)}) collective-permute-start(bf16[192,4224]{1,0:T(8,128)(2,1)S(1)} %get-tuple-element.67.refs_0_), channel_id=1, source_target_pairs={{0,2},{1,3},{2,0},{3,1},{4,6},{5,7},{6,4},{7,5}} | collective-permute-start | bytes 4866056 | tf_op jit(solution)/shard_map/ppermute | solution.py:506
  717.7 36.8 %collective-permute-start.13 = (bf16[192,4224]{1,0:T(8,128)(2,1)}, bf16[192,4224]{1,0:T(8,128)(2,1)S(1)}, u32[]{:S(2)}, u32[]{:S(2)}) collective-permute-start(bf16[192,4224]{1,0:T(8,128)(2,1)} %get-tuple-element.62.refs_0_), channel_id=1, source_target_pairs={{0,1},{1,0},{2,3},{3,2},{4,5},{5,4},{6,7},{7,6}} | collective-permute-start | bytes 4866056 | tf_op jit(solution)/shard_map/ppermute | solution.py:506
  718.6 68.6 %collective-permute-start.10 = (bf16[192,4224]{1,0:T(8,128)(2,1)}, bf16[192,4224]{1,0:T(8,128)(2,1)}, u32[]{:S(2)}, u32[]{:S(2)}) collective-permute-start(bf16[192,4224]{1,0:T(8,128)(2,1)} %get-tuple-element.62.refs_0_), channel_id=1, source_target_pairs={{0,4},{1,5},{2,6},{3,7},{4,0},{5,1},{6,2},{7,3}} | collective-permute-start | bytes 4866056 | tf_op jit(solution)/shard_map/ppermute | solution.py:506
  728.2 67.0 %collective-permute-start.3 = (bf16[192,4224]{1,0:T(8,128)(2,1)}, bf16[192,4224]{1,0:T(8,128)(2,1)}, u32[]{:S(2)}, u32[]{:S(2)}) collective-permute-start(bf16[192,4224]{1,0:T(8,128)(2,1)} %get-tuple-element.62.refs_0_), channel_id=1, source_target_pairs={{0,2},{1,3},{2,0},{3,1},{4,6},{5,7},{6,4},{7,5}} | collective-permute-start | bytes 4866056 | tf_op jit(solution)/shard_map/ppermute | solution.py:506
  752.4 43.8 %collective-permute-start.9 = (bf16[192,4224]{1,0:T(8,128)(2,1)S(1)}, bf16[192,4224]{1,0:T(8,128)(2,1)}, u32[]{:S(2)}, u32[]{:S(2)}) collective-permute-start(bf16[192,4224]{1,0:T(8,128)(2,1)S(1)} %get-tuple-element.61.refs_0_), channel_id=1, source_target_pairs={{0,1},{1,0},{2,3},{3,2},{4,5},{5,4},{6,7},{7,6}} | collective-permute-start | bytes 4866056 | tf_op jit(solution)/shard_map/ppermute | solution.py:506
  753.4 68.0 %collective-permute-start = (bf16[192,4224]{1,0:T(8,128)(2,1)S(1)}, bf16[192,4224]{1,0:T(8,128)(2,1)}, u32[]{:S(2)}, u32[]{:S(2)}) collective-permute-start(bf16[192,4224]{1,0:T(8,128)(2,1)S(1)} %get-tuple-element.61.refs_0_), channel_id=1, source_target_pairs={{0,4},{1,5},{2,6},{3,7},{4,0},{5,1},{6,2},{7,3}} | collective-permute-start | bytes 4866056 | tf_op jit(solution)/shard_map/ppermute | solution.py:506
  755.6 65.8 %collective-permute-start.39 = (bf16[528,1536]{1,0:T(8,128)(2,1)}, bf16[528,1536]{1,0:T(8,128)(2,1)}, u32[]{:S(2)}, u32[]{:S(2)}) collective-permute-start(bf16[528,1536]{1,0:T(8,128)(2,1)} %collective-permute-done.38.refs_0_), channel_id=1, source_target_pairs={{0,1},{1,0},{2,3},{3,2},{4,5},{5,4},{6,7},{7,6}} | collective-permute-start | bytes 4866056 | tf_op jit(solution)/shard_map/ppermute | solution.py:506
  787.2 38.5 %collective-permute-start.40 = (bf16[528,1536]{1,0:T(8,128)(2,1)}, bf16[528,1536]{1,0:T(8,128)(2,1)}, u32[]{:S(2)}, u32[]{:S(2)}) collective-permute-start(bf16[528,1536]{1,0:T(8,128)(2,1)} %copy-done.24), channel_id=1, source_target_pairs={{0,1},{1,0},{2,3},{3,2},{4,5},{5,4},{6,7},{7,6}} | collective-permute-start | bytes 4866056 | tf_op jit(solution)/shard_map/ppermute | solution.py:506
  795.2 30.5 %copy-start.25 = (bf16[528,1536]{1,0:T(8,128)(2,1)S(1)}, bf16[528,1536]{1,0:T(8,128)(2,1)}, u32[]{:S(2)}) copy-start(bf16[528,1536]{1,0:T(8,128)(2,1)} %copy-done.24) | copy-start | bytes 4866052
  795.2 38.9 %collective-permute-start.6 = (bf16[192,4224]{1,0:T(8,128)(2,1)S(1)}, bf16[192,4224]{1,0:T(8,128)(2,1)}, u32[]{:S(2)}, u32[]{:S(2)}) collective-permute-start(bf16[192,4224]{1,0:T(8,128)(2,1)S(1)} %get-tuple-element.61.refs_0_), channel_id=1, source_target_pairs={{0,2},{1,3},{2,0},{3,1},{4,6},{5,7},{6,4},{7,5}} | collective-permute-start | bytes 4866056 | tf_op jit(solution)/shard_map/ppermute | solution.py:506
  796.2 38.9 %collective-permute-start.35 = (bf16[528,1536]{1,0:T(8,128)(2,1)S(1)}, bf16[528,1536]{1,0:T(8,128)(2,1)S(1)}, u32[]{:S(2)}, u32[]{:S(2)}) collective-permute-start(bf16[528,1536]{1,0:T(8,128)(2,1)S(1)} %copy-done.23), channel_id=1, source_target_pairs={{0,1},{1,0},{2,3},{3,2},{4,5},{5,4},{6,7},{7,6}} | collective-permute-start | bytes 4866056 | tf_op jit(solution)/shard_map/ppermute | solution.py:506
  821.4 13.9 %collective-permute-start.36 = (bf16[528,1536]{1,0:T(8,128)(2,1)S(1)}, bf16[528,1536]{1,0:T(8,128)(2,1)}, u32[]{:S(2)}, u32[]{:S(2)}) collective-permute-start(bf16[528,1536]{1,0:T(8,128)(2,1)S(1)} %copy-done.27), channel_id=1, source_target_pairs={{0,1},{1,0},{2,3},{3,2},{4,5},{5,4},{6,7},{7,6}} | collective-permute-start | bytes 4866056 | tf_op jit(solution)/shard_map/ppermute | solution.py:506
  821.4 14.2 %collective-permute-start.25 = (bf16[192,4224]{1,0:T(8,128)(2,1)}, bf16[192,4224]{1,0:T(8,128)(2,1)S(1)}, u32[]{:S(2)}, u32[]{:S(2)}) collective-permute-start(bf16[192,4224]{1,0:T(8,128)(2,1)} %collective-permute-done.24.refs_0_), channel_id=1, source_target_pairs={{0,1},{1,0},{2,3},{3,2},{4,5},{5,4},{6,7},{7,6}} | collective-permute-start | bytes 4866056 | tf_op jit(solution)/shard_map/ppermute | solution.py:506
  825.7 16.5 %collective-permute-start.26 = (bf16[192,4224]{1,0:T(8,128)(2,1)}, bf16[192,4224]{1,0:T(8,128)(2,1)}, u32[]{:S(2)}, u32[]{:S(2)}) collective-permute-start(bf16[192,4224]{1,0:T(8,128)(2,1)} %collective-permute-done.17.refs_1_), channel_id=1, source_target_pairs={{0,1},{1,0},{2,3},{3,2},{4,5},{5,4},{6,7},{7,6}} | collective-permute-start | bytes 4866056 | tf_op jit(solution)/shard_map/ppermute | solution.py:506
  834.1 37.8 %collective-permute-start.32 = (bf16[528,1536]{1,0:T(8,128)(2,1)S(1)}, bf16[528,1536]{1,0:T(8,128)(2,1)S(1)}, u32[]{:S(2)}, u32[]{:S(2)}) collective-permute-start(bf16[528,1536]{1,0:T(8,128)(2,1)S(1)} %copy-done.25), channel_id=1, source_target_pairs={{0,4},{1,5},{2,6},{3,7},{4,0},{5,1},{6,2},{7,3}} | collective-permute-start | bytes 4866056 | tf_op jit(solution)/shard_map/ppermute | solution.py:506
  835.1 37.9 %collective-permute-start.21 = (bf16[192,4224]{1,0:T(8,128)(2,1)}, bf16[192,4224]{1,0:T(8,128)(2,1)S(1)}, u32[]{:S(2)}, u32[]{:S(2)}) collective-permute-start(bf16[192,4224]{1,0:T(8,128)(2,1)} %collective-permute-done.14.refs_0_), channel_id=1, source_target_pairs={{0,1},{1,0},{2,3},{3,2},{4,5},{5,4},{6,7},{7,6}} | collective-permute-start | bytes 4866056 | tf_op jit(solution)/shard_map/ppermute | solution.py:506
  835.3 38.8 %collective-permute-start.22 = (bf16[192,4224]{1,0:T(8,128)(2,1)}, bf16[192,4224]{1,0:T(8,128)(2,1)}, u32[]{:S(2)}, u32[]{:S(2)}) collective-permute-start(bf16[192,4224]{1,0:T(8,128)(2,1)} %collective-permute-done.20.refs_1_), channel_id=1, source_target_pairs={{0,1},{1,0},{2,3},{3,2},{4,5},{5,4},{6,7},{7,6}} | collective-permute-start | bytes 4866056 | tf_op jit(solution)/shard_map/ppermute | solution.py:506
  836.9 37.2 %collective-permute-start.11 = (bf16[192,4224]{1,0:T(8,128)(2,1)}, bf16[192,4224]{1,0:T(8,128)(2,1)}, u32[]{:S(2)}, u32[]{:S(2)}) collective-permute-start(bf16[192,4224]{1,0:T(8,128)(2,1)} %collective-permute-done.10.refs_0_), channel_id=1, source_target_pairs={{0,1},{1,0},{2,3},{3,2},{4,5},{5,4},{6,7},{7,6}} | collective-permute-start | bytes 4866056 | tf_op jit(solution)/shard_map/ppermute | solution.py:506
  842.1 38.5 %collective-permute-start.12 = (bf16[192,4224]{1,0:T(8,128)(2,1)}, bf16[192,4224]{1,0:T(8,128)(2,1)}, u32[]{:S(2)}, u32[]{:S(2)}) collective-permute-start(bf16[192,4224]{1,0:T(8,128)(2,1)} %collective-permute-done.3.refs_1_), channel_id=1, source_target_pairs={{0,1},{1,0},{2,3},{3,2},{4,5},{5,4},{6,7},{7,6}} | collective-permute-start | bytes 4866056 | tf_op jit(solution)/shard_map/ppermute | solution.py:506
  871.9 37.0 %collective-permute-start.29 = (bf16[528,1536]{1,0:T(8,128)(2,1)S(1)}, bf16[528,1536]{1,0:T(8,128)(2,1)S(1)}, u32[]{:S(2)}, u32[]{:S(2)}) collective-permute-start(bf16[528,1536]{1,0:T(8,128)(2,1)S(1)} %copy-done.23), channel_id=1, source_target_pairs={{0,2},{1,3},{2,0},{3,1},{4,6},{5,7},{6,4},{7,5}} | collective-permute-start | bytes 4866056 | tf_op jit(solution)/shard_map/ppermute | solution.py:506
  873.0 40.8 %collective-permute-start.18 = (bf16[192,4224]{1,0:T(8,128)(2,1)}, bf16[192,4224]{1,0:T(8,128)(2,1)S(1)}, u32[]{:S(2)}, u32[]{:S(2)}) collective-permute-start(bf16[192,4224]{1,0:T(8,128)(2,1)} %collective-permute-done.17.refs_1_), channel_id=1, source_target_pairs={{0,4},{1,5},{2,6},{3,7},{4,0},{5,1},{6,2},{7,3}} | collective-permute-start | bytes 4866056 | tf_op jit(solution)/shard_map/ppermute | solution.py:506
  874.1 40.7 %collective-permute-start.7 = (bf16[192,4224]{1,0:T(8,128)(2,1)}, bf16[192,4224]{1,0:T(8,128)(2,1)}, u32[]{:S(2)}, u32[]{:S(2)}) collective-permute-start(bf16[192,4224]{1,0:T(8,128)(2,1)} %collective-permute-done.refs_0_), channel_id=1, source_target_pairs={{0,1},{1,0},{2,3},{3,2},{4,5},{5,4},{6,7},{7,6}} | collective-permute-start | bytes 4866056 | tf_op jit(solution)/shard_map/ppermute | solution.py:506
  874.1 40.7 %collective-permute-start.8 = (bf16[192,4224]{1,0:T(8,128)(2,1)}, bf16[192,4224]{1,0:T(8,128)(2,1)}, u32[]{:S(2)}, u32[]{:S(2)}) collective-permute-start(bf16[192,4224]{1,0:T(8,128)(2,1)} %collective-permute-done.6.refs_1_), channel_id=1, source_target_pairs={{0,1},{1,0},{2,3},{3,2},{4,5},{5,4},{6,7},{7,6}} | collective-permute-start | bytes 4866056 | tf_op jit(solution)/shard_map/ppermute | solution.py:506
  880.6 64.0 %collective-permute-start.4 = (bf16[192,4224]{1,0:T(8,128)(2,1)}, bf16[192,4224]{1,0:T(8,128)(2,1)S(1)}, u32[]{:S(2)}, u32[]{:S(2)}) collective-permute-start(bf16[192,4224]{1,0:T(8,128)(2,1)} %collective-permute-done.3.refs_1_), channel_id=1, source_target_pairs={{0,4},{1,5},{2,6},{3,7},{4,0},{5,1},{6,2},{7,3}} | collective-permute-start | bytes 4866056 | tf_op jit(solution)/shard_map/ppermute | solution.py:506
  908.9 39.1 %collective-permute-start.15 = (bf16[192,4224]{1,0:T(8,128)(2,1)}, bf16[192,4224]{1,0:T(8,128)(2,1)S(1)}, u32[]{:S(2)}, u32[]{:S(2)}) collective-permute-start(bf16[192,4224]{1,0:T(8,128)(2,1)} %collective-permute-done.14.refs_0_), channel_id=1, source_target_pairs={{0,2},{1,3},{2,0},{3,1},{4,6},{5,7},{6,4},{7,5}} | collective-permute-start | bytes 4866056 | tf_op jit(solution)/shard_map/ppermute | solution.py:506
  913.7 66.3 %collective-permute-start.1 = (bf16[192,4224]{1,0:T(8,128)(2,1)}, bf16[192,4224]{1,0:T(8,128)(2,1)S(1)}, u32[]{:S(2)}, u32[]{:S(2)}) collective-permute-start(bf16[192,4224]{1,0:T(8,128)(2,1)} %collective-permute-done.refs_0_), channel_id=1, source_target_pairs={{0,2},{1,3},{2,0},{3,1},{4,6},{5,7},{6,4},{7,5}} | collective-permute-start | bytes 4866056 | tf_op jit(solution)/shard_map/ppermute | solution.py:506
  914.7 65.3 %collective-permute-start.33 = (bf16[528,1536]{1,0:T(8,128)(2,1)S(1)}, bf16[528,1536]{1,0:T(8,128)(2,1)}, u32[]{:S(2)}, u32[]{:S(2)}) collective-permute-start(bf16[528,1536]{1,0:T(8,128)(2,1)S(1)} %collective-permute-done.32.refs_0_), channel_id=1, source_target_pairs={{0,1},{1,0},{2,3},{3,2},{4,5},{5,4},{6,7},{7,6}} | collective-permute-start | bytes 4866056 | tf_op jit(solution)/shard_map/ppermute | solution.py:506
  914.8 70.9 %collective-permute-start.19 = (bf16[192,4224]{1,0:T(8,128)(2,1)S(1)}, bf16[192,4224]{1,0:T(8,128)(2,1)S(1)}, u32[]{:S(2)}, u32[]{:S(2)}) collective-permute-start(bf16[192,4224]{1,0:T(8,128)(2,1)S(1)} %collective-permute-done.18.refs_0_), channel_id=1, source_target_pairs={{0,1},{1,0},{2,3},{3,2},{4,5},{5,4},{6,7},{7,6}} | collective-permute-start | bytes 4866056 | tf_op jit(solution)/shard_map/ppermute | solution.py:506
  944.7 44.3 %collective-permute-start.5 = (bf16[192,4224]{1,0:T(8,128)(2,1)S(1)}, bf16[192,4224]{1,0:T(8,128)(2,1)S(1)}, u32[]{:S(2)}, u32[]{:S(2)}) collective-permute-start(bf16[192,4224]{1,0:T(8,128)(2,1)S(1)} %collective-permute-done.4.refs_0_), channel_id=1, source_target_pairs={{0,1},{1,0},{2,3},{3,2},{4,5},{5,4},{6,7},{7,6}} | collective-permute-start | bytes 4866056 | tf_op jit(solution)/shard_map/ppermute | solution.py:506
  948.0 44.3 %collective-permute-start.30 = (bf16[528,1536]{1,0:T(8,128)(2,1)S(1)}, bf16[528,1536]{1,0:T(8,128)(2,1)S(1)}, u32[]{:S(2)}, u32[]{:S(2)}) collective-permute-start(bf16[528,1536]{1,0:T(8,128)(2,1)S(1)} %collective-permute-done.29.refs_0_), channel_id=1, source_target_pairs={{0,1},{1,0},{2,3},{3,2},{4,5},{5,4},{6,7},{7,6}} | collective-permute-start | bytes 4866056 | tf_op jit(solution)/shard_map/ppermute | solution.py:506
  980.0 13.9 %collective-permute-start.16 = (bf16[192,4224]{1,0:T(8,128)(2,1)S(1)}, bf16[192,4224]{1,0:T(8,128)(2,1)}, u32[]{:S(2)}, u32[]{:S(2)}) collective-permute-start(bf16[192,4224]{1,0:T(8,128)(2,1)S(1)} %collective-permute-done.15.refs_0_), channel_id=1, source_target_pairs={{0,1},{1,0},{2,3},{3,2},{4,5},{5,4},{6,7},{7,6}} | collective-permute-start | bytes 4866056 | tf_op jit(solution)/shard_map/ppermute | solution.py:506
  980.0 17.3 %collective-permute-start.2 = (bf16[192,4224]{1,0:T(8,128)(2,1)S(1)}, bf16[192,4224]{1,0:T(8,128)(2,1)S(1)}, u32[]{:S(2)}, u32[]{:S(2)}) collective-permute-start(bf16[192,4224]{1,0:T(8,128)(2,1)S(1)} %collective-permute-done.1.refs_0_), channel_id=1, source_target_pairs={{0,1},{1,0},{2,3},{3,2},{4,5},{5,4},{6,7},{7,6}} | collective-permute-start | bytes 4866056 | tf_op jit(solution)/shard_map/ppermute | solution.py:506
  (26 other events, 181.5 us)

commit v2 on v1

v2 whole, which is shorter than its diff:
```python
import functools

import jax
import jax.numpy as jnp
from jax import lax
from jax.experimental import pallas as pl
from jax.experimental.pallas import tpu as pltpu
from jax.sharding import PartitionSpec as P


BF = jnp.bfloat16
F32 = jnp.float32
MESH = pl.DeviceIdType.MESH
TOKENS, D, FF, LAYERS = 2048, 1536, 4224, 2
BLOCK = 256
STEPS = -(-FF // BLOCK)
LAST = FF - (STEPS - 1) * BLOCK
PART = D // 8
SUB = BLOCK // 8
OWN_DOWN = FF // 8
LAST_SUB = OWN_DOWN - (STEPS - 1) * SUB
HALF = PART // 2
CHUNK = PART + HALF
COUNT = 3 * LAYERS * D * FF
VMEM_LIMIT = 67043328


ANY = pl.BlockSpec(memory_space=pl.ANY)
GROUPS = {"own": (0, 1), "near": (4, 2, 5, 3), "across": (6,), "last": (7,)}


def dot(a, b, ca, cb):
    return lax.dot_general(a, b, (((ca,), (cb,)), ((), ())), preferred_element_type=F32)


def resident(shape):
    return pl.BlockSpec(shape, lambda *_: (0,) * len(shape), pipeline_mode=pl.Buffered(1))


def cost(units, bytes_accessed):
    return pl.CostEstimate(flops=int(units * 2 * TOKENS * D * FF), bytes_accessed=int(bytes_accessed), transcendentals=0)


def normed(h):
    wide = h.astype(F32)
    scale = lax.rsqrt(jnp.mean(wide * wide, -1, keepdims=True) + 1e-6)
    return (wide * scale).astype(BF)


class Weights:
    def __init__(self, l, wg, wu, wd, gu_ref, down_ref, sems):
        self.l, self.wg, self.wu, self.wd, self.gu_ref, self.down_ref, self.sems = l, wg, wu, wd, gu_ref, down_ref, sems

    def copies(self, j, last):
        slot = lax.rem(j, 2)
        width = LAST if last else BLOCK
        start = (STEPS - 1) * BLOCK if last else pl.multiple_of(j * BLOCK, BLOCK)
        columns = pl.ds(start, width)
        pairs = [
            (self.wg.at[self.l, :, columns], self.gu_ref.at[slot, :, pl.ds(0, width)]),
            (self.wu.at[self.l, :, columns], self.gu_ref.at[slot, :, pl.ds(BLOCK, width)]),
        ]
        if self.wd is not None:
            pairs.append((self.wd.at[self.l, columns], self.down_ref.at[slot, pl.ds(0, width)]))
        return [pltpu.make_async_copy(src, dst, self.sems.at[slot, n]) for n, (src, dst) in enumerate(pairs)]

    def each(self, j, act):
        @pl.when(j < STEPS - 1)
        def _():
            for copy in self.copies(j, False):
                act(copy)

        @pl.when(j == STEPS - 1)
        def _():
            for copy in self.copies(j, True):
                act(copy)

    def start(self, j):
        self.each(j, lambda copy: copy.start())

    def wait(self, j):
        self.each(j, lambda copy: copy.wait())


def forward_kernel(l, with_down, h_ref, wg, wu, *refs):
    if with_down:
        wd, a_out, ht_ref, sl_ref, q_ref, next_out, a_ref, gu_ref, w_sems, sems, hid_ref, acc_ref, down_ref = refs
    else:
        a_out, ht_ref, sl_ref, q_ref, a_ref, gu_ref, w_sems, sems = refs
        wd = hid_ref = down_ref = None
    j = pl.program_id(0)
    weights = Weights(l, wg, wu, wd, gu_ref, down_ref, w_sems)
    keep = pltpu.make_async_copy(a_ref, a_out, sems.at[0])

    @pl.when(j == 0)
    def _():
        weights.start(j)

        @pl.loop(0, TOKENS // 256)
        def _(i):
            r = pl.ds(pl.multiple_of(i * 256, 256), 256)
            a_ref[r, :] = normed(h_ref[r, :])
            if with_down:
                acc_ref[r, :] = jnp.zeros((256, D), F32)

        keep.start()

    weights.start(j + 1)
    weights.wait(j)
    slot = lax.rem(j, 2)
    for i in range(8):
        r = slice(256 * i, 256 * i + 256)
        gu = dot(a_ref[r, :], gu_ref[slot], 1, 0)
        g, u = gu[:, :BLOCK], gu[:, BLOCK:]
        s = jax.nn.sigmoid(g)
        sl = g * s
        sl_ref[r, :] = sl
        q_ref[r, :] = u * (s * (1.0 + g * (1.0 - s)))
        hid = (sl * u).astype(BF)
        if with_down:
            hid_ref[r, :] = hid
        ht_ref[:, r] = hid.T

    if with_down:

        @pl.when(j == STEPS - 1)
        def _():
            hid_ref[:, LAST:] = jnp.zeros((TOKENS, BLOCK - LAST), BF)

        acc_ref[...] += dot(hid_ref[...], down_ref[slot], 1, 0)

    @pl.when(j == STEPS - 1)
    def _():
        keep.wait()
        if with_down:

            @pl.loop(0, TOKENS // 256)
            def _(i):
                r = pl.ds(pl.multiple_of(i * 256, 256), 256)
                a_ref[r, :] = h_ref[r, :] + acc_ref[r, :].astype(BF)

            move = pltpu.make_async_copy(a_ref, next_out, sems.at[1])
            move.start()
            move.wait()


def forward(l, h, wg, wu, wd=None):
    with_down = wd is not None
    state = jax.ShapeDtypeStruct((TOKENS, D), BF)
    wide = pl.BlockSpec((TOKENS, BLOCK), lambda j: (0, j))
    in_specs = [resident((TOKENS, D)), ANY, ANY]
    out_shape = [state, jax.ShapeDtypeStruct((FF, TOKENS), BF)] + [jax.ShapeDtypeStruct((TOKENS, FF), F32)] * 2
    out_specs = [ANY, pl.BlockSpec((BLOCK, TOKENS), lambda j: (j, 0)), wide, wide]
    scratch = [
        pltpu.VMEM((TOKENS, D), BF),
        pltpu.VMEM((2, D, 2 * BLOCK), BF),
        pltpu.SemaphoreType.DMA((2, 3)),
        pltpu.SemaphoreType.DMA((2,)),
    ]
    args = [h, wg, wu]
    if with_down:
        in_specs.append(ANY)
        out_shape.append(state)
        out_specs.append(ANY)
        scratch += [pltpu.VMEM((TOKENS, BLOCK), BF), pltpu.VMEM((TOKENS, D), F32), pltpu.VMEM((2, BLOCK, D), BF)]
        args.append(wd)
    return pl.pallas_call(
        functools.partial(forward_kernel, l, with_down),
        grid=(STEPS,),
        in_specs=in_specs,
        out_specs=out_specs,
        out_shape=out_shape,
        scratch_shapes=scratch,
        compiler_params=pltpu.CompilerParams(vmem_limit_bytes=VMEM_LIMIT),
        cost_estimate=cost(3 if with_down else 2, 130e6),
    )(*args)


class Lags:
    def __init__(self, second, third, b, e):
        self.second, self.third, self.b, self.e = second, third, b, e
        self.s = third + 1
        self.a = third + 2
        self.c = second + third
        self.d = 2 * (third - second)


def backward_kernel(l, lags, a_in, dy_ref, wd_ref, sl_ref, q_ref, ht_ref, *refs):
    with_da = l == 1
    if with_da:
        wg, wu, h_in, g_gate, g_up, g_down, sq_ref, dh_out, acc_ref, gu_ref, w_sems, *refs = refs
        weights = Weights(l, wg, wu, None, gu_ref, None, w_sems)
    else:
        other_ref, g_gate, g_up, g_down, f_ref, sq_ref, every_ref, f_send, f_recv, *refs = refs
    a_ref, dgu_ref, s_ref, a2_ref, bx, by, cx, cy, ex, ey, dx, dy2, og, ou, od, *sems = refs
    s_send, a_recv, bx_send, by_send, cx_recv, cy_recv, ex_send, ey_send, dx_recv, dy_recv, out_sem, a_sem = sems
    j = pl.program_id(0)
    me = lax.axis_index("dp")
    x, y, c = lax.div(me, 4), lax.rem(lax.div(me, 2), 2), lax.rem(me, 2)
    to_core, to_x, to_y = ({"dp": me + k * (1 - 2 * t)} for k, t in ((1, c), (4, x), (2, y)))
    others = [{"dp": lax.rem(me + k, 8)} for k in range(1, 8)]

    def remote(src, dst, send, recv, to):
        return pltpu.make_async_remote_copy(src_ref=src, dst_ref=dst, send_sem=send, recv_sem=recv, device_id=to, device_id_type=MESH)

    def columns(last):
        return pl.ds(0, LAST if last else BLOCK)

    def pair(i, last, which=(0, 1)):
        s, a, w = lax.rem(i, lags.s), lax.rem(i, lags.a), columns(last)
        return [
            remote(s_ref.at[s, n, :, :, 1 - c, :, w], a2_ref.at[a, n, :, :, :, w], s_send.at[s, k], a_recv.at[a, k], to_core)
            for k, n in ((k, (pl.ds(0, 2), pl.ds(2, 1))[k]) for k in which)
        ]

    def first(i, last):
        b, k, w = lax.rem(i, lags.b), lax.rem(i, lags.c), columns(last)
        return [
            remote(bx.at[b, :, :, w], cx.at[k, :, :, w], bx_send.at[b], cx_recv.at[k], to_x),
            remote(by.at[b, :, :, w], cy.at[k, :, :, w], by_send.at[b], cy_recv.at[k], to_y),
        ]

    def second(i, last):
        e, k, w = lax.rem(i, lags.e), lax.rem(i, lags.d), columns(last)
        return [
            remote(ex.at[e, :, w], dx.at[k, :, w], ex_send.at[e], dx_recv.at[k], to_x),
            remote(ey.at[e, :, w], dy2.at[k, :, w], ey_send.at[e], dy_recv.at[k], to_y),
        ]

    def outs(i, last):
        o = lax.rem(i, 2)
        if last:
            wide, deep = pl.ds((STEPS - 1) * BLOCK, LAST), pl.ds((STEPS - 1) * SUB, LAST_SUB)
            srcs = og.at[o, :, pl.ds(0, LAST)], ou.at[o, :, pl.ds(0, LAST)], od.at[o, pl.ds(0, LAST_SUB)]
        else:
            wide, deep = pl.ds(pl.multiple_of(i * BLOCK, BLOCK), BLOCK), pl.ds(pl.multiple_of(i * SUB, SUB), SUB)
            srcs = og.at[o], ou.at[o], od.at[o]
        dsts = g_gate.at[:, wide], g_up.at[:, wide], g_down.at[deep]
        return [pltpu.make_async_copy(s, d, out_sem.at[o, n]) for n, (s, d) in enumerate(zip(srcs, dsts))]

    def each(i, copies, act):
        @pl.when(i < STEPS - 1)
        def _():
            for copy in copies(i, False):
                act(copy)

        @pl.when(i == STEPS - 1)
        def _():
            for copy in copies(i, True):
                act(copy)

    def start(copy):
        copy.start()

    def total(*terms):
        return functools.reduce(lambda p, q: p + q, [t.astype(F32) for t in terms])

    def take_first(i):
        each(i, pair, lambda copy: copy.wait())
        s, a, b = lax.rem(i, lags.s), lax.rem(i, lags.a), lax.rem(i, lags.b)

        @pl.when(i >= lags.b)
        def _():
            for copy in first(i - lags.b, False):
                copy.wait_send()

        for t in range(2):
            bx[b, t, :PART] = total(s_ref[s, 0, 1 - x, t, c], a2_ref[a, 0, 1 - x, t]).astype(BF)
            bx[b, t, PART:] = total(s_ref[s, 2, 1 - x, t, c, :HALF], a2_ref[a, 2, 1 - x, t, :HALF]).astype(BF)
            by[b, t, :PART] = total(s_ref[s, 1, t, 1 - y, c], a2_ref[a, 1, t, 1 - y]).astype(BF)
            by[b, t, PART:] = total(s_ref[s, 2, t, 1 - y, c, HALF:], a2_ref[a, 2, t, 1 - y, HALF:]).astype(BF)
        each(i, first, start)

    def take_second(i):
        each(i, first, lambda copy: copy.wait_recv())
        s, a, k, e = lax.rem(i, lags.s), lax.rem(i, lags.a), lax.rem(i, lags.c), lax.rem(i, lags.e)

        @pl.when(i >= lags.e)
        def _():
            for copy in second(i - lags.e, False):
                copy.wait_send()

        ey[e, :PART] = total(s_ref[s, 0, x, 1 - y, c], a2_ref[a, 0, x, 1 - y], cx[k, 1 - y, :PART]).astype(BF)
        ey[e, PART:] = total(s_ref[s, 2, x, 1 - y, c, :HALF], a2_ref[a, 2, x, 1 - y, :HALF], cx[k, 1 - y, PART:]).astype(BF)
        ex[e, :PART] = total(s_ref[s, 1, 1 - x, y, c], a2_ref[a, 1, 1 - x, y], cy[k, 1 - x, :PART]).astype(BF)
        ex[e, PART:] = total(s_ref[s, 2, 1 - x, y, c, HALF:], a2_ref[a, 2, 1 - x, y, HALF:], cy[k, 1 - x, PART:]).astype(BF)
        each(i, second, start)

    def take_third(i):
        each(i, second, lambda copy: copy.wait_recv())
        s, a, k, d, o = (lax.rem(i, n) for n in (lags.s, lags.a, lags.c, lags.d, 2))

        @pl.when(i >= 2)
        def _():
            for copy in outs(i - 2, False):
                copy.wait()

        gate = total(s_ref[s, 0, x, y, c], a2_ref[a, 0, x, y], cx[k, y, :PART], dy2[d, :PART]).astype(BF)
        up = total(s_ref[s, 1, x, y, c], a2_ref[a, 1, x, y], cy[k, x, :PART], dx[d, :PART]).astype(BF)
        og[o] = gate
        ou[o] = up
        low = total(s_ref[s, 2, x, y, c, :HALF], a2_ref[a, 2, x, y, :HALF], cx[k, y, PART:], dy2[d, PART:]).astype(BF)
        high = total(s_ref[s, 2, x, y, c, HALF:], a2_ref[a, 2, x, y, HALF:], cy[k, x, PART:], dx[d, PART:]).astype(BF)
        downs = [half[SUB * n : SUB * n + SUB] for half in (low, high) for n in range(HALF // SUB)]

        def squares(t):
            wide = t.astype(F32)
            return jnp.sum((wide * wide).reshape(-1, 8, t.shape[-1]), 0)

        @pl.when(i < STEPS - 1)
        def _():
            for n, one in enumerate(downs):
                od[o, :, BLOCK * n : BLOCK * n + BLOCK] = one
            sq_ref[...] += squares(gate) + squares(up) + squares(low) + squares(high)

        @pl.when(i == STEPS - 1)
        def _():
            for n, one in enumerate(downs):
                od[o, :LAST_SUB, BLOCK * n : BLOCK * n + LAST] = one[:LAST_SUB, :LAST]
                od[o, :LAST_SUB, BLOCK * n + LAST : BLOCK * n + BLOCK] = one[LAST_SUB:, :LAST]
            sq_ref[:, :LAST] += sum(squares(t[:, :LAST]) for t in (gate, up, low, high))

        each(i, outs, start)

    take_a = pltpu.make_async_copy(a_in, a_ref, a_sem.at[0])

    barrier = pltpu.get_barrier_semaphore()
    greeted = (to_core, to_x, to_y) if with_da else others

    @pl.when(j == 0)
    def _():
        take_a.start()
        for to in greeted:
            pl.semaphore_signal(barrier, inc=1, device_id=to, device_id_type=MESH)
        sq_ref[...] = jnp.zeros_like(sq_ref)
        if with_da:
            weights.start(j)

            @pl.loop(0, TOKENS // 256)
            def _(i):
                acc_ref[pl.ds(pl.multiple_of(i * 256, 256), 256), :] = jnp.zeros((256, D), F32)

    @pl.when(j < STEPS)
    def _():
        if with_da:
            weights.start(j + 1)
        s = lax.rem(j, lags.s)
        for i in range(4):
            r = slice(512 * i, 512 * i + 512)
            dh = dot(dy_ref[r, :], wd_ref[0], 1, 1).astype(BF).astype(F32)
            dgu_ref[r, :BLOCK] = (dh * q_ref[r, :]).astype(BF)
            dgu_ref[r, BLOCK:] = (dh * sl_ref[r, :]).astype(BF)

        pl.when(j == 0)(lambda: take_a.wait())

        @pl.when(j == STEPS - 1)
        def _():
            dgu_ref[:, LAST:BLOCK] = jnp.zeros((TOKENS, BLOCK - LAST), BF)
            dgu_ref[:, BLOCK + LAST :] = jnp.zeros((TOKENS, BLOCK - LAST), BF)

        for h in range(2):
            gu = dot(a_ref[:, D // 2 * h : D // 2 * (h + 1)], dgu_ref[...], 0, 0)
            for o in range(4):
                for t in range(2):
                    s_ref[s, t, h, o // 2, o % 2] = gu[PART * o : PART * o + PART, BLOCK * t : BLOCK * t + BLOCK].astype(BF)
        pl.when(j == 0)(lambda: pl.semaphore_wait(barrier, len(greeted)))
        each(j, functools.partial(pair, which=(0,)), start)
        for h in range(2):
            down = dot(ht_ref[...].reshape(BLOCK, TOKENS), dy_ref[:, D // 2 * h : D // 2 * (h + 1)], 1, 0)
            for o in range(8):
                for n in range(3):
                    s_ref[s, 2, o // 4, o // 2 % 2, o % 2, SUB * (3 * h + n) : SUB * (3 * h + n + 1)] = down[
                        SUB * o : SUB * o + SUB, BLOCK * n : BLOCK * n + BLOCK
                    ].astype(BF)

        @pl.when(j == STEPS - 1)
        def _():
            for o in range(8):
                for n in range(6):
                    at = o // 4, o // 2 % 2, o % 2
                    s_ref[(s, 2, *at, slice(SUB * n + LAST_SUB, SUB * n + SUB), slice(0, LAST))] = s_ref[
                        (s, 2, *at, slice(SUB * n, SUB * n + LAST_SUB), slice(LAST, BLOCK))
                    ]

        each(j, functools.partial(pair, which=(1,)), start)
        if with_da:
            weights.wait(j)
            for i in range(4):
                r = slice(512 * i, 512 * i + 512)
                acc_ref[r, :] += dot(dgu_ref[r, :], gu_ref[lax.rem(j, 2)], 1, 1)

    if with_da:
        take_h = pltpu.make_async_copy(h_in, a_ref, a_sem.at[1])
        give_dh = pltpu.make_async_copy(a_ref, dh_out, a_sem.at[2])
        pl.when(j == STEPS - 1)(lambda: take_h.start())

        @pl.when(j == STEPS)
        def _():
            take_h.wait()

            @pl.loop(0, TOKENS // 128)
            def _(i):
                r = pl.ds(pl.multiple_of(i * 128, 128), 128)
                h = a_ref[r, :].astype(F32)
                da = acc_ref[r, :].astype(BF).astype(F32)
                scale = lax.rsqrt(jnp.mean(h * h, -1, keepdims=True) + 1e-6)
                along = jnp.sum(da * h, -1, keepdims=True) * (scale * scale * scale) * (1.0 / D)
                a_ref[r, :] = dy_ref[r, :] + (da * scale - h * along).astype(BF)

            give_dh.start()

    pl.when((j >= lags.third) & (j < STEPS + lags.third))(lambda: take_third(j - lags.third))
    pl.when((j >= lags.second) & (j < STEPS + lags.second))(lambda: take_second(j - lags.second))
    pl.when(j < STEPS)(lambda: take_first(j))

    @pl.when(j == STEPS + lags.third - 1)
    def _():
        if not with_da:
            both = sq_ref[...] + other_ref[...]
            every_ref[me] = both[:, :128] + both[:, 128:]
            for n, to in enumerate(others):
                remote(every_ref.at[me], every_ref.at[me], f_send.at[n], f_recv.at[n], to).start()
        for i in range(STEPS - lags.b, STEPS):
            for copy in first(jnp.int32(i), i == STEPS - 1):
                copy.wait_send()
        for i in range(STEPS - lags.e, STEPS):
            for copy in second(jnp.int32(i), i == STEPS - 1):
                copy.wait_send()
        for i in range(STEPS - 2, STEPS):
            for copy in outs(jnp.int32(i), i == STEPS - 1):
                copy.wait()
        if with_da:
            give_dh.wait()
        else:
            for n, to in enumerate(others):
                remote(every_ref.at[me], every_ref.at[me], f_send.at[n], f_recv.at[n], to).wait()
            squares = functools.reduce(lambda p, q: p + q, [every_ref[n] for n in range(8)])
            squares = jnp.sum(jnp.sum(squares, axis=1, keepdims=True), axis=0, keepdims=True)
            f_ref[...] = jnp.broadcast_to(jnp.minimum(1.0, 0.5 * lax.rsqrt(squares / COUNT + 1e-30)), (8, 128))


def backward(l, lags, a, dy, wd, sl, q, ht, *more):
    with_da = l == 1
    at = lambda j: jnp.minimum(j, STEPS - 1)
    wide = pl.BlockSpec((TOKENS, BLOCK), lambda j: (0, at(j)))
    sums = pl.BlockSpec((8, BLOCK), lambda j: (0, 0))
    in_specs = [
        ANY,
        resident((TOKENS, D)),
        pl.BlockSpec((1, BLOCK, D), lambda j: (l, at(j), 0)),
        wide,
        wide,
        pl.BlockSpec((8, SUB, TOKENS), lambda j: (0, at(j), 0)),
    ]
    args = [a, dy, wd, sl, q, ht.reshape(8, OWN_DOWN, TOKENS), *more]
    out_shape = [jax.ShapeDtypeStruct((PART, FF), BF)] * 2 + [jax.ShapeDtypeStruct((OWN_DOWN, D), BF)]
    if with_da:
        in_specs += [ANY] * 3
        out_shape += [jax.ShapeDtypeStruct((8, BLOCK), F32), jax.ShapeDtypeStruct((TOKENS, D), BF)]
        out_specs = [ANY] * 3 + [sums, ANY]
        scratch = [pltpu.VMEM((TOKENS, D), F32), pltpu.VMEM((2, D, 2 * BLOCK), BF), pltpu.SemaphoreType.DMA((2, 3))]
    else:
        in_specs += [sums]
        out_shape += [jax.ShapeDtypeStruct((8, 128), F32)]
        out_specs = [ANY] * 3 + [pl.BlockSpec((8, 128), lambda j: (0, 0))]
        scratch = [pltpu.VMEM((8, BLOCK), F32), pltpu.VMEM((8, 8, 128), F32), *[pltpu.SemaphoreType.DMA((7,))] * 2]
    piece = (PART, BLOCK)
    scratch += [
        pltpu.VMEM((TOKENS, D), BF),
        pltpu.VMEM((TOKENS, 2 * BLOCK), BF),
        pltpu.VMEM((lags.s, 3, 2, 2, 2) + piece, BF),
        pltpu.VMEM((lags.a, 3, 2, 2) + piece, BF),
        *[pltpu.VMEM((lags.b, 2, CHUNK, BLOCK), BF)] * 2,
        *[pltpu.VMEM((lags.c, 2, CHUNK, BLOCK), BF)] * 2,
        *[pltpu.VMEM((lags.e, CHUNK, BLOCK), BF)] * 2,
        *[pltpu.VMEM((lags.d, CHUNK, BLOCK), BF)] * 2,
        *[pltpu.VMEM((2,) + piece, BF)] * 2,
        pltpu.VMEM((2, SUB, D), BF),
    ]
    scratch += [pltpu.SemaphoreType.DMA((n, 2)) for n in (lags.s, lags.a)]
    scratch += [pltpu.SemaphoreType.DMA((n,)) for n in (lags.b, lags.b, lags.c, lags.c, lags.e, lags.e, lags.d, lags.d)]
    scratch += [pltpu.SemaphoreType.DMA((2, 3)), pltpu.SemaphoreType.DMA((3,))]
    return pl.pallas_call(
        functools.partial(backward_kernel, l, lags),
        grid=(STEPS + lags.third,),
        in_specs=in_specs,
        out_specs=out_specs,
        out_shape=out_shape,
        scratch_shapes=scratch,
        compiler_params=pltpu.CompilerParams(vmem_limit_bytes=VMEM_LIMIT, collective_id=l, has_side_effects=True),
        cost_estimate=cost(6 if with_da else 4, 150e6),
    )(*args)


def adamw_kernel(at_ref, f_ref, g_ref, w_ref, m_ref, v_ref, *refs):
    nw_ref, nm_ref, nv_ref = refs[-3:]
    factor = f_ref[0:1, 0:1]

    @pl.loop(0, g_ref.shape[0] // 16)
    def _(i):
        r = pl.ds(pl.multiple_of(i * 16, 16), 16)
        g = g_ref[r, :].astype(F32) * factor
        w = w_ref[0, r, :].astype(F32)
        m = 0.9 * m_ref[0, r, :] + 0.1 * g
        v = 0.95 * v_ref[0, r, :] + 0.05 * g * g
        nm_ref[0, r, :] = m
        nv_ref[0, r, :] = v
        nw_ref[r, :] = (w - 0.02 * (m * lax.rsqrt(v + 1e-8) + 0.1 * w)).astype(BF)


def adamw(l, skip, count, at, factor, g, w, m, v, so_far=None):
    rows, columns = g.shape
    deep = rows // 3
    moment = pl.BlockSpec((1, deep, columns), lambda i, at: (l, skip + i, 0))
    in_specs = [
        pl.BlockSpec((8, 128), lambda i, at: (0, 0)),
        pl.BlockSpec((deep, columns), lambda i, at: (skip + i, 0)),
        pl.BlockSpec((1, deep, columns), lambda i, at: (l, 3 * at[0] + skip + i, 0)),
        moment,
        moment,
    ]
    args = [factor, g, w, m, v]
    aliases = {}
    if so_far is not None:
        in_specs += [ANY, ANY]
        args += so_far
        aliases = {6: 1, 7: 2}
    return pl.pallas_call(
        adamw_kernel,
        grid_spec=pltpu.PrefetchScalarGridSpec(
            num_scalar_prefetch=1,
            grid=(count,),
            in_specs=in_specs,
            out_specs=[pl.BlockSpec((deep, columns), lambda i, at: (i, 0)), moment, moment],
        ),
        out_shape=[jax.ShapeDtypeStruct((count * deep, columns), BF)] + [jax.ShapeDtypeStruct(m.shape, F32)] * 2,
        input_output_aliases=aliases,
        compiler_params=pltpu.CompilerParams(vmem_limit_bytes=48 << 20),
        cost_estimate=cost(0.03 * count, 22 * count * deep * columns),
    )(at, *args)


def place_kernel(n, owners_ref, *refs):
    out_ref = refs[-1]
    s = pl.program_id(0)
    for k in range(n):

        @pl.when(s == k)
        def _():
            out_ref[0] = refs[k][...]


def place(l, skip, count, owners, pieces, so_far, whole):
    n = len(pieces)
    rows, columns = pieces[0].shape
    deep = rows // count

    def of(k):
        return lambda s, i, own: (jnp.where(s == k, i, jnp.where(s < k, 0, count - 1)), 0)

    in_specs = [pl.BlockSpec((deep, columns), of(k)) for k in range(n)]
    args = list(pieces)
    aliases = {}
    if so_far is not None:
        in_specs.append(ANY)
        args.append(so_far)
        aliases = {n + 1: 0}
    return pl.pallas_call(
        functools.partial(place_kernel, n),
        grid_spec=pltpu.PrefetchScalarGridSpec(
            num_scalar_prefetch=1,
            grid=(n, count),
            in_specs=in_specs,
            out_specs=pl.BlockSpec((1, deep, columns), lambda s, i, own: (l, 3 * own[s] + skip + i, 0)),
        ),
        out_shape=jax.ShapeDtypeStruct(whole.shape, BF),
        input_output_aliases=aliases,
        compiler_params=pltpu.CompilerParams(vmem_limit_bytes=48 << 20),
        cost_estimate=cost(0.03 * n * count, 4 * n * rows * columns),
    )(owners, *args)


PIECES = [(0, l, 0, 1) for l in range(2)] + [(0, l, 1, 2) for l in range(2)] + [(1, l, 0, 3) for l in range(2)]
PIECES += [(2, l, 0, 2) for l in range(2)] + [(2, l, 2, 1) for l in range(2)]


def solution(mesh):
    def swap(t, mask):
        return lax.ppermute(t, "dp", [(i, i ^ mask) for i in range(8)])

    def step(x, dy, wg, wu, wd, mg, mu, md, vg, vu, vd):
        x, dy = x[0], dy[0]
        me = lax.axis_index("dp")
        a0, ht0, sl0, q0, h1 = forward(0, x, wg, wu, wd)
        a1, ht1, sl1, q1 = forward(1, h1, wg, wu)
        *g1, squares, dh1 = backward(1, Lags(1, 2, 2, 2), a1, dy, wd, sl1, q1, ht1, wg, wu, h1)
        *g0, factor = backward(0, Lags(2, 4, 3, 3), a0, dh1, wd, sl0, q0, ht0, squares)
        at = me[None].astype(jnp.int32)
        groups = {name: jnp.stack([me ^ k for k in group]).astype(jnp.int32) for name, group in GROUPS.items()}
        mats = ((wg, mg, vg), (wu, mu, vu), (wd, md, vd))
        moments, whole = [None] * 3, [None] * 3

        def put(kind, number, have):
            n, l, skip, count = PIECES[number]
            whole[n] = place(l, skip, count, groups[kind], [have[k] for k in GROUPS[kind]], whole[n], mats[n][0])

        everything = []
        for number, (n, l, skip, count) in enumerate(PIECES):
            have = {}
            everything.append(have)
            have[0], *moments[n] = adamw(l, skip, count, at, factor, (g0, g1)[l][n], *mats[n], moments[n])
            have[4] = swap(have[0], 4)
            have[2] = swap(have[0], 2)
            have[6] = swap(have[4], 2) if number % 2 else swap(have[2], 4)
            for k in (0, 4, 2, 6):
                have[k + 1] = swap(have[k], 1)
            put("own", number, have)
            put("near", number, have)
        for number, have in enumerate(everything):
            put("across", number, have)
            put("last", number, have)
        return tuple(whole + [m[0] for m in moments] + [m[1] for m in moments])

    whole, rows = P(None, None, None), P(None, "dp", None)
    return jax.shard_map(
        step,
        mesh=mesh,
        in_specs=(P(("rep", "dp")),) * 2 + (whole,) * 3 + (rows,) * 6,
        out_specs=(P("rep"),) * 3 + (P("rep", "dp"),) * 6,
        check_vma=False,
    )
```

time: 1010 us -> 1020 us (level)
  Pallas kernels: 704 us -> 734 us
  waiting for transfers between devices: 240 us -> 216 us
  other arithmetic: 18.5 us -> 0.16 us
  starting transfers between devices: 22.5 us -> 37.4 us
  local copies, waits for them, and re-layouts: 13.9 us -> 26.6 us
    pallas_call x24 -> x40, Pallas kernels: 76.8 us -> 111 us  [place(): pl.pallas_call(functools.partial(place_kernel, n), grid_spec=pltpu.Prefet...]
    ppermute x42 -> x70, waiting for transfers between devices: 240 us -> 216 us  [swap(): return lax.ppermute(t, 'dp', [(i, i ^ mask) for i in range(8)])]
    pallas_call x5 -> x4, Pallas kernels: 581 us -> 566 us  [the longest x2 396 us: backward(): pl.pallas_call(functools.partial(backward_kernel, l, lags), grid=(STEPS +...]
    ppermute x42 -> x70, starting transfers between devices: 22.5 us -> 37.4 us  [swap(): return lax.ppermute(t, 'dp', [(i, i ^ mask) for i in range(8)])]
    unnamed x64 -> x182, local copies, waits for them, and re-layouts: 13.9 us -> 26.6 us
    pallas_call x6 -> x10, Pallas kernels: 45.6 us -> 56.9 us  [adamw(): pl.pallas_call(adamw_kernel, grid_spec=pltpu.PrefetchScalarGridSpec(num_s...]
    add x1 -> x0, other arithmetic: 11.1 us -> none  [step(): dh1 = dy + back(g1[4])[0]]
  transfers between devices with their start and end apart: 42 -> 70, of which waited for: 14 -> 22; matrix products, arithmetic and copies ran while one was open for 0% -> 0% of each run, Pallas kernels for 11% -> 15%
where the time goes in v2:
time: 1020 us
  Pallas kernels  734 us (72%)
  waiting for transfers between devices  216 us (21%)
  starting transfers between devices  37.4 us (4%)
  local copies, waits for them, and re-layouts  26.6 us (3%)
    pallas_call x2, Pallas kernels, backward(): pl.pallas_call(functools.partial(backward_kernel, l, lags), grid=(STEPS +...  396 us
    ppermute x70, waiting for transfers between devices, swap(): return lax.ppermute(t, 'dp', [(i, i ^ mask) for i in range(8)])  216 us
    pallas_call x2, Pallas kernels, forward(): pl.pallas_call(functools.partial(forward_kernel, l, with_down), grid=(STE...  170 us
    pallas_call x40, Pallas kernels, place(): pl.pallas_call(functools.partial(place_kernel, n), grid_spec=pltpu.Prefet...  111 us
    pallas_call x10, Pallas kernels, adamw(): pl.pallas_call(adamw_kernel, grid_spec=pltpu.PrefetchScalarGridSpec(num_s...  56.9 us
    ppermute x70, starting transfers between devices, swap(): return lax.ppermute(t, 'dp', [(i, i ^ mask) for i in range(8)])  37.4 us
    unnamed x182, local copies, waits for them, and re-layouts  26.6 us
  transfers between devices with their start and end apart: 70, of which 22 were waited for; matrix products, arithmetic and copies ran while one was open for 0% of the time, Pallas kernels for 15%

profile of v2, /device:TPU:0, one launch (start us, length us, event | category | flops | bytes accessed | tf_op | source)
XLA Modules:
  0.0 1015.4 jit_solution(2636347184670196408)
XLA Ops:
  0.6 102.8 %shard_map.178 = (bf16[2048,1536]{1,0:T(8,128)(2,1)}, bf16[4224,2048]{1,0:T(8,128)(2,1)}, f32[2048,4224]{1,0:T(8,128)}, f32[2048,4224]{1,0:T(8,128)}, bf16[2048,1536]{1,0:T(8,128)(2,1)}) custom-call(bf16[2048,1536]{1,0:T(8,128)(2,1)} %bitcast.12, bf16[2,1536,4224]{2,1,0:T(8,128)(2,1)} %w_ref.13, bf16[2,1536,4224]{2,1,0:T(8,128)(2,1)} %w_ref.15, ...), custom_call_target="tpu_custom_call" | custom-call | flops 79725330432 | bytes 130000000 | tf_op jit(solution)/shard_map/pallas_call | solution.py:167
  103.4 67.5 %shard_map.179 = (bf16[2048,1536]{1,0:T(8,128)(2,1)}, bf16[4224,2048]{1,0:T(8,128)(2,1)}, f32[2048,4224]{1,0:T(8,128)}, f32[2048,4224]{1,0:T(8,128)}) custom-call(bf16[2048,1536]{1,0:T(8,128)(2,1)} %get-tuple-element.58.h_ref.refs_2_, bf16[2,1536,4224]{2,1,0:T(8,128)(2,1)} %w_ref.13, bf16[2,1536,4224]{2,1,0:T(8,128)(2,1)} %w_ref.15), custom_call_target="tpu_custom_call" | custom-call | flops 53150220288 | bytes 130000000 | tf_op jit(solution)/shard_map/pallas_call | solution.py:167
  171.0 213.9 %shard_map.180 = (bf16[192,4224]{1,0:T(8,128)(2,1)}, bf16[192,4224]{1,0:T(8,128)(2,1)}, bf16[528,1536]{1,0:T(8,128)(2,1)}, f32[8,256]{1,0:T(8,128)}, bf16[2048,1536]{1,0:T(8,128)(2,1)}) custom-call(bf16[2048,1536]{1,0:T(8,128)(2,1)} %get-tuple-element.59.a_in, bf16[2048,1536]{1,0:T(8,128)(2,1)} %bitcast.13, bf16[2,4224,1536]{2,1,0:T(8,128)(2,1)} %w_ref.19, ...), custom_call_target="tpu_custom_call" | custom-call | flops 159450660864 | bytes 150000000 | tf_op jit(solution)/shard_map/pallas_call | solution.py:483
  384.9 181.9 %shard_map.181 = (bf16[192,4224]{1,0:T(8,128)(2,1)}, bf16[192,4224]{1,0:T(8,128)(2,1)}, bf16[528,1536]{1,0:T(8,128)(2,1)}, f32[8,128]{1,0:T(8,128)}) custom-call(bf16[2048,1536]{1,0:T(8,128)(2,1)} %get-tuple-element.57.a_in, bf16[2048,1536]{1,0:T(8,128)(2,1)} %get-tuple-element.63.dy_ref, bf16[2,4224,1536]{2,1,0:T(8,128)(2,1)} %w_ref.19, ...), custom_call_target="tpu_custom_call" | custom-call | flops 106300440576 | bytes 150000000 | tf_op jit(solution)/shard_map/pallas_call | solution.py:483
  568.9 5.4 shard_map.212
  574.3 5.6 shard_map.213
  580.0 4.5 shard_map.214
  586.7 4.2 shard_map.215
  592.3 4.2 shard_map.182
  602.2 8.6 collective-permute-done.42.refs_0_
  612.9 4.1 shard_map.183
  618.5 5.0 collective-permute-done.9.refs_1_
  628.8 8.7 collective-permute-done.6.refs_0_
  641.8 20.1 %collective-permute-done.51.refs_1_ = bf16[352,1536]{1,0:T(8,128)(2,1)} collective-permute-done((bf16[352,1536]{1,0:T(8,128)(2,1)S(1)}, bf16[352,1536]{1,0:T(8,128)(2,1)}, u32[]{:S(2)}, u32[]{:S(2)}) %collective-permute-start.51) | collective-permute-done | bytes 1081376 | tf_op jit(solution)/shard_map/ppermute | solution.py:589
  664.3 18.1 %collective-permute-done.48.refs_0_ = bf16[352,1536]{1,0:T(8,128)(2,1)S(1)} collective-permute-done((bf16[352,1536]{1,0:T(8,128)(2,1)S(1)}, bf16[352,1536]{1,0:T(8,128)(2,1)S(1)}, u32[]{:S(2)}, u32[]{:S(2)}) %collective-permute-start.48) | collective-permute-done | bytes 1081376 | tf_op jit(solution)/shard_map/ppermute | solution.py:589
  686.8 5.6 shard_map.184
  693.9 4.0 collective-permute-done.46.refs_0_
  703.5 5.7 shard_map.185
  713.9 8.8 shard_map.202
  722.7 2.3 collective-permute-done.16.refs_0_
  726.3 8.7 shard_map.203
  740.2 8.0 collective-permute-done.refs_0_
  748.2 4.2 collective-permute-done.12.refs_1_
  752.4 5.9 collective-permute-done.10.refs_0_
  758.3 2.4 shard_map.216.refs_4_
  760.7 3.5 shard_map.187.refs_2_
  766.4 2.4 shard_map.189.refs_2_
  768.9 3.5 shard_map.190.refs_4_
  775.8 5.2 shard_map.204.refs_4_
  781.5 6.2 shard_map.217.refs_2_
  787.7 6.5 shard_map.191.refs_2_
  794.2 15.9 %collective-permute-done.31.refs_1_ = bf16[192,4224]{1,0:T(8,128)(2,1)S(1)} collective-permute-done((bf16[192,4224]{1,0:T(8,128)(2,1)S(1)}, bf16[192,4224]{1,0:T(8,128)(2,1)S(1)}, u32[]{:S(2)}, u32[]{:S(2)}) %collective-permute-start.31) | collective-permute-done | bytes 1622048 | tf_op jit(solution)/shard_map/ppermute | solution.py:589
  812.1 34.7 %collective-permute-done.28.refs_0_ = bf16[192,4224]{1,0:T(8,128)(2,1)S(1)} collective-permute-done((bf16[192,4224]{1,0:T(8,128)(2,1)S(1)}, bf16[192,4224]{1,0:T(8,128)(2,1)S(1)}, u32[]{:S(2)}, u32[]{:S(2)}) %collective-permute-start.28) | collective-permute-done | bytes 1622048 | tf_op jit(solution)/shard_map/ppermute | solution.py:589
  846.9 4.7 shard_map.192.refs_4_
  852.2 8.1 shard_map.193.refs_1_
  860.9 2.4 shard_map.218.refs_4_
  871.0 6.2 shard_map.219.refs_2_
  878.9 2.4 shard_map.221.refs_2_
  881.3 40.4 %collective-permute-done.49.refs_0_ = bf16[352,1536]{1,0:T(8,128)(2,1)S(1)} collective-permute-done((bf16[352,1536]{1,0:T(8,128)(2,1)S(1)}, bf16[352,1536]{1,0:T(8,128)(2,1)S(1)}, u32[]{:S(2)}, u32[]{:S(2)}) %collective-permute-start.49) | collective-permute-done | bytes 1081376 | tf_op jit(solution)/shard_map/ppermute | solution.py:589
  925.0 19.4 %collective-permute-done.1.refs_0_ = bf16[128,4224]{1,0:T(8,128)(2,1)S(1)} collective-permute-done((bf16[128,4224]{1,0:T(8,128)(2,1)}, bf16[128,4224]{1,0:T(8,128)(2,1)S(1)}, u32[]{:S(2)}, u32[]{:S(2)}) %collective-permute-start.1) | collective-permute-done | bytes 1081376 | tf_op jit(solution)/shard_map/ppermute | solution.py:589
  947.8 2.4 shard_map.223.refs_1_
  951.3 2.1 shard_map.198.refs_1_
  953.3 2.2 shard_map.225.refs_1_
  966.3 2.1 shard_map.201
  970.7 7.8 shard_map.205.refs_2_
  981.2 14.2 %collective-permute-done.32.refs_0_ = bf16[192,4224]{1,0:T(8,128)(2,1)S(1)} collective-permute-done((bf16[192,4224]{1,0:T(8,128)(2,1)S(1)}, bf16[192,4224]{1,0:T(8,128)(2,1)S(1)}, u32[]{:S(2)}, u32[]{:S(2)}) %collective-permute-start.32) | collective-permute-done | bytes 1622048 | tf_op jit(solution)/shard_map/ppermute | solution.py:589
  995.9 3.3 shard_map.206.refs_4_
  1000.0 8.7 shard_map.207.refs_1_
  (330 shorter events, 99.5 us)
Async XLA Ops:
  590.9 19.8 %collective-permute-start.42 = (bf16[176,1536]{1,0:T(8,128)(2,1)S(1)}, bf16[176,1536]{1,0:T(8,128)(2,1)S(1)}, u32[]{:S(2)}, u32[]{:S(2)}) collective-permute-start(bf16[176,1536]{1,0:T(8,128)(2,1)S(1)} %get-tuple-element.95.refs_0_), channel_id=1, source_target_pairs={{0,4},{1,5},{2,6},{3,7},{4,0},{5,1},{6,2},{7,3}} | collective-permute-start | bytes 1622024 | tf_op jit(solution)/shard_map/ppermute | solution.py:589
  597.3 19.7 %collective-permute-start.54 = (bf16[176,1536]{1,0:T(8,128)(2,1)S(1)}, bf16[176,1536]{1,0:T(8,128)(2,1)S(1)}, u32[]{:S(2)}, u32[]{:S(2)}) collective-permute-start(bf16[176,1536]{1,0:T(8,128)(2,1)S(1)} %get-tuple-element.95.refs_0_), channel_id=1, source_target_pairs={{0,2},{1,3},{2,0},{3,1},{4,6},{5,7},{6,4},{7,5}} | collective-permute-start | bytes 1622024 | tf_op jit(solution)/shard_map/ppermute | solution.py:589
  600.3 23.1 %collective-permute-start.9 = (bf16[64,4224]{1,0:T(8,128)(2,1)S(1)}, bf16[64,4224]{1,0:T(8,128)(2,1)}, u32[]{:S(2)}, u32[]{:S(2)}) collective-permute-start(bf16[64,4224]{1,0:T(8,128)(2,1)S(1)} %get-tuple-element.80.refs_0_), channel_id=1, source_target_pairs={{0,2},{1,3},{2,0},{3,1},{4,6},{5,7},{6,4},{7,5}} | collective-permute-start | bytes 1622024 | tf_op jit(solution)/shard_map/ppermute | solution.py:589
  602.1 37.2 %collective-permute-start.69 = (bf16[352,1536]{1,0:T(8,128)(2,1)S(1)}, bf16[352,1536]{1,0:T(8,128)(2,1)S(1)}, u32[]{:S(2)}, u32[]{:S(2)}) collective-permute-start(bf16[352,1536]{1,0:T(8,128)(2,1)S(1)} %get-tuple-element.98.refs_0_), channel_id=1, source_target_pairs={{0,1},{1,0},{2,3},{3,2},{4,5},{5,4},{6,7},{7,6}} | collective-permute-start | bytes 3244040 | tf_op jit(solution)/shard_map/ppermute | solution.py:589
  617.8 19.7 %collective-permute-start.6 = (bf16[64,4224]{1,0:T(8,128)(2,1)S(1)}, bf16[64,4224]{1,0:T(8,128)(2,1)S(1)}, u32[]{:S(2)}, u32[]{:S(2)}) collective-permute-start(bf16[64,4224]{1,0:T(8,128)(2,1)S(1)} %get-tuple-element.79.refs_0_), channel_id=1, source_target_pairs={{0,4},{1,5},{2,6},{3,7},{4,0},{5,1},{6,2},{7,3}} | collective-permute-start | bytes 1622024 | tf_op jit(solution)/shard_map/ppermute | solution.py:589
  625.9 36.0 %collective-permute-start.51 = (bf16[352,1536]{1,0:T(8,128)(2,1)S(1)}, bf16[352,1536]{1,0:T(8,128)(2,1)}, u32[]{:S(2)}, u32[]{:S(2)}) collective-permute-start(bf16[352,1536]{1,0:T(8,128)(2,1)S(1)} %get-tuple-element.98.refs_0_), channel_id=1, source_target_pairs={{0,2},{1,3},{2,0},{3,1},{4,6},{5,7},{6,4},{7,5}} | collective-permute-start | bytes 3244040 | tf_op jit(solution)/shard_map/ppermute | solution.py:589
  628.1 34.6 %collective-permute-start.66 = (bf16[352,1536]{1,0:T(8,128)(2,1)S(1)}, bf16[352,1536]{1,0:T(8,128)(2,1)S(1)}, u32[]{:S(2)}, u32[]{:S(2)}) collective-permute-start(bf16[352,1536]{1,0:T(8,128)(2,1)S(1)} %get-tuple-element.98.refs_0_), channel_id=1, source_target_pairs={{0,4},{1,5},{2,6},{3,7},{4,0},{5,1},{6,2},{7,3}} | collective-permute-start | bytes 3244040 | tf_op jit(solution)/shard_map/ppermute | solution.py:589
  637.5 25.8 %collective-permute-start.65 = (bf16[352,1536]{1,0:T(8,128)(2,1)S(1)}, bf16[352,1536]{1,0:T(8,128)(2,1)S(1)}, u32[]{:S(2)}, u32[]{:S(2)}) collective-permute-start(bf16[352,1536]{1,0:T(8,128)(2,1)S(1)} %get-tuple-element.97.refs_0_), channel_id=1, source_target_pairs={{0,1},{1,0},{2,3},{3,2},{4,5},{5,4},{6,7},{7,6}} | collective-permute-start | bytes 3244040 | tf_op jit(solution)/shard_map/ppermute | solution.py:589
  638.6 43.8 %collective-permute-start.48 = (bf16[352,1536]{1,0:T(8,128)(2,1)S(1)}, bf16[352,1536]{1,0:T(8,128)(2,1)S(1)}, u32[]{:S(2)}, u32[]{:S(2)}) collective-permute-start(bf16[352,1536]{1,0:T(8,128)(2,1)S(1)} %get-tuple-element.97.refs_0_), channel_id=1, source_target_pairs={{0,4},{1,5},{2,6},{3,7},{4,0},{5,1},{6,2},{7,3}} | collective-permute-start | bytes 3244040 | tf_op jit(solution)/shard_map/ppermute | solution.py:589
  640.4 43.2 %collective-permute-start.62 = (bf16[352,1536]{1,0:T(8,128)(2,1)S(1)}, bf16[352,1536]{1,0:T(8,128)(2,1)S(1)}, u32[]{:S(2)}, u32[]{:S(2)}) collective-permute-start(bf16[352,1536]{1,0:T(8,128)(2,1)S(1)} %get-tuple-element.97.refs_0_), channel_id=1, source_target_pairs={{0,2},{1,3},{2,0},{3,1},{4,6},{5,7},{6,4},{7,5}} | collective-permute-start | bytes 3244040 | tf_op jit(solution)/shard_map/ppermute | solution.py:589
  661.9 23.8 %collective-permute-start.59 = (bf16[176,1536]{1,0:T(8,128)(2,1)S(1)}, bf16[176,1536]{1,0:T(8,128)(2,1)S(1)}, u32[]{:S(2)}, u32[]{:S(2)}) collective-permute-start(bf16[176,1536]{1,0:T(8,128)(2,1)S(1)} %collective-permute-done.58.refs_0_), channel_id=1, source_target_pairs={{0,1},{1,0},{2,3},{3,2},{4,5},{5,4},{6,7},{7,6}} | collective-permute-start | bytes 1622024 | tf_op jit(solution)/shard_map/ppermute | solution.py:589
  662.7 29.7 %collective-permute-start.60 = (bf16[176,1536]{1,0:T(8,128)(2,1)S(1)}, bf16[176,1536]{1,0:T(8,128)(2,1)S(1)}, u32[]{:S(2)}, u32[]{:S(2)}) collective-permute-start(bf16[176,1536]{1,0:T(8,128)(2,1)S(1)} %collective-permute-done.45.refs_1_), channel_id=1, source_target_pairs={{0,1},{1,0},{2,3},{3,2},{4,5},{5,4},{6,7},{7,6}} | collective-permute-start | bytes 1622024 | tf_op jit(solution)/shard_map/ppermute | solution.py:589
  664.2 28.3 %collective-permute-start.55 = (bf16[176,1536]{1,0:T(8,128)(2,1)S(1)}, bf16[176,1536]{1,0:T(8,128)(2,1)S(1)}, u32[]{:S(2)}, u32[]{:S(2)}) collective-permute-start(bf16[176,1536]{1,0:T(8,128)(2,1)S(1)} %collective-permute-done.42.refs_0_), channel_id=1, source_target_pairs={{0,1},{1,0},{2,3},{3,2},{4,5},{5,4},{6,7},{7,6}} | collective-permute-start | bytes 1622024 | tf_op jit(solution)/shard_map/ppermute | solution.py:589
  692.5 19.2 %collective-permute-start.19 = (bf16[128,4224]{1,0:T(8,128)(2,1)}, bf16[128,4224]{1,0:T(8,128)(2,1)S(1)}, u32[]{:S(2)}, u32[]{:S(2)}) collective-permute-start(bf16[128,4224]{1,0:T(8,128)(2,1)} %get-tuple-element.78.refs_0_), channel_id=1, source_target_pairs={{0,1},{1,0},{2,3},{3,2},{4,5},{5,4},{6,7},{7,6}} | collective-permute-start | bytes 3244040 | tf_op jit(solution)/shard_map/ppermute | solution.py:589
  698.0 27.0 %collective-permute-start.16 = (bf16[128,4224]{1,0:T(8,128)(2,1)}, bf16[128,4224]{1,0:T(8,128)(2,1)}, u32[]{:S(2)}, u32[]{:S(2)}) collective-permute-start(bf16[128,4224]{1,0:T(8,128)(2,1)} %get-tuple-element.78.refs_0_), channel_id=1, source_target_pairs={{0,4},{1,5},{2,6},{3,7},{4,0},{5,1},{6,2},{7,3}} | collective-permute-start | bytes 3244040 | tf_op jit(solution)/shard_map/ppermute | solution.py:589
  702.2 32.9 %collective-permute-start.3 = (bf16[128,4224]{1,0:T(8,128)(2,1)}, bf16[128,4224]{1,0:T(8,128)(2,1)}, u32[]{:S(2)}, u32[]{:S(2)}) collective-permute-start(bf16[128,4224]{1,0:T(8,128)(2,1)} %get-tuple-element.78.refs_0_), channel_id=1, source_target_pairs={{0,2},{1,3},{2,0},{3,1},{4,6},{5,7},{6,4},{7,5}} | collective-permute-start | bytes 3244040 | tf_op jit(solution)/shard_map/ppermute | solution.py:589
  710.1 29.2 %collective-permute-start.15 = (bf16[128,4224]{1,0:T(8,128)(2,1)}, bf16[128,4224]{1,0:T(8,128)(2,1)}, u32[]{:S(2)}, u32[]{:S(2)}) collective-permute-start(bf16[128,4224]{1,0:T(8,128)(2,1)} %get-tuple-element.77.refs_0_), channel_id=1, source_target_pairs={{0,1},{1,0},{2,3},{3,2},{4,5},{5,4},{6,7},{7,6}} | collective-permute-start | bytes 3244040 | tf_op jit(solution)/shard_map/ppermute | solution.py:589
  710.9 37.3 %collective-permute-start = (bf16[128,4224]{1,0:T(8,128)(2,1)}, bf16[128,4224]{1,0:T(8,128)(2,1)}, u32[]{:S(2)}, u32[]{:S(2)}) collective-permute-start(bf16[128,4224]{1,0:T(8,128)(2,1)} %get-tuple-element.77.refs_0_), channel_id=1, source_target_pairs={{0,4},{1,5},{2,6},{3,7},{4,0},{5,1},{6,2},{7,3}} | collective-permute-start | bytes 3244040 | tf_op jit(solution)/shard_map/ppermute | solution.py:589
  712.7 39.7 %collective-permute-start.12 = (bf16[128,4224]{1,0:T(8,128)(2,1)}, bf16[128,4224]{1,0:T(8,128)(2,1)}, u32[]{:S(2)}, u32[]{:S(2)}) collective-permute-start(bf16[128,4224]{1,0:T(8,128)(2,1)} %get-tuple-element.77.refs_0_), channel_id=1, source_target_pairs={{0,2},{1,3},{2,0},{3,1},{4,6},{5,7},{6,4},{7,5}} | collective-permute-start | bytes 3244040 | tf_op jit(solution)/shard_map/ppermute | solution.py:589
  725.0 33.2 %collective-permute-start.10 = (bf16[64,4224]{1,0:T(8,128)(2,1)}, bf16[64,4224]{1,0:T(8,128)(2,1)}, u32[]{:S(2)}, u32[]{:S(2)}) collective-permute-start(bf16[64,4224]{1,0:T(8,128)(2,1)} %collective-permute-done.9.refs_1_), channel_id=1, source_target_pairs={{0,4},{1,5},{2,6},{3,7},{4,0},{5,1},{6,2},{7,3}} | collective-permute-start | bytes 1622024 | tf_op jit(solution)/shard_map/ppermute | solution.py:589
  735.0 37.3 %collective-permute-start.41 = (bf16[192,4224]{1,0:T(8,128)(2,1)S(1)}, bf16[192,4224]{1,0:T(8,128)(2,1)}, u32[]{:S(2)}, u32[]{:S(2)}) collective-permute-start(bf16[192,4224]{1,0:T(8,128)(2,1)S(1)} %get-tuple-element.86.refs_0_), channel_id=1, source_target_pairs={{0,1},{1,0},{2,3},{3,2},{4,5},{5,4},{6,7},{7,6}} | collective-permute-start | bytes 4866056 | tf_op jit(solution)/shard_map/ppermute | solution.py:589
  739.4 24.9 %collective-permute-start.7 = (bf16[64,4224]{1,0:T(8,128)(2,1)S(1)}, bf16[64,4224]{1,0:T(8,128)(2,1)}, u32[]{:S(2)}, u32[]{:S(2)}) collective-permute-start(bf16[64,4224]{1,0:T(8,128)(2,1)S(1)} %copy-done.72), channel_id=1, source_target_pairs={{0,2},{1,3},{2,0},{3,1},{4,6},{5,7},{6,4},{7,5}} | collective-permute-start | bytes 1622024 | tf_op jit(solution)/shard_map/ppermute | solution.py:589
  748.2 25.6 %collective-permute-start.68 = (bf16[352,1536]{1,0:T(8,128)(2,1)}, bf16[352,1536]{1,0:T(8,128)(2,1)S(1)}, u32[]{:S(2)}, u32[]{:S(2)}) collective-permute-start(bf16[352,1536]{1,0:T(8,128)(2,1)} %collective-permute-done.51.refs_1_), channel_id=1, source_target_pairs={{0,1},{1,0},{2,3},{3,2},{4,5},{5,4},{6,7},{7,6}} | collective-permute-start | bytes 3244040 | tf_op jit(solution)/shard_map/ppermute | solution.py:589
  752.4 22.0 %collective-permute-start.67 = (bf16[352,1536]{1,0:T(8,128)(2,1)S(1)}, bf16[352,1536]{1,0:T(8,128)(2,1)S(1)}, u32[]{:S(2)}, u32[]{:S(2)}) collective-permute-start(bf16[352,1536]{1,0:T(8,128)(2,1)S(1)} %copy-done.35), channel_id=1, source_target_pairs={{0,1},{1,0},{2,3},{3,2},{4,5},{5,4},{6,7},{7,6}} | collective-permute-start | bytes 3244040 | tf_op jit(solution)/shard_map/ppermute | solution.py:589
  772.3 37.8 %collective-permute-start.31 = (bf16[192,4224]{1,0:T(8,128)(2,1)S(1)}, bf16[192,4224]{1,0:T(8,128)(2,1)S(1)}, u32[]{:S(2)}, u32[]{:S(2)}) collective-permute-start(bf16[192,4224]{1,0:T(8,128)(2,1)S(1)} %get-tuple-element.86.refs_0_), channel_id=1, source_target_pairs={{0,2},{1,3},{2,0},{3,1},{4,6},{5,7},{6,4},{7,5}} | collective-permute-start | bytes 4866056 | tf_op jit(solution)/shard_map/ppermute | solution.py:589
  773.8 38.3 %collective-permute-start.38 = (bf16[192,4224]{1,0:T(8,128)(2,1)S(1)}, bf16[192,4224]{1,0:T(8,128)(2,1)S(1)}, u32[]{:S(2)}, u32[]{:S(2)}) collective-permute-start(bf16[192,4224]{1,0:T(8,128)(2,1)S(1)} %get-tuple-element.86.refs_0_), channel_id=1, source_target_pairs={{0,4},{1,5},{2,6},{3,7},{4,0},{5,1},{6,2},{7,3}} | collective-permute-start | bytes 4866056 | tf_op jit(solution)/shard_map/ppermute | solution.py:589
  774.4 72.4 %collective-permute-start.28 = (bf16[192,4224]{1,0:T(8,128)(2,1)S(1)}, bf16[192,4224]{1,0:T(8,128)(2,1)S(1)}, u32[]{:S(2)}, u32[]{:S(2)}) collective-permute-start(bf16[192,4224]{1,0:T(8,128)(2,1)S(1)} %get-tuple-element.85.refs_0_), channel_id=1, source_target_pairs={{0,4},{1,5},{2,6},{3,7},{4,0},{5,1},{6,2},{7,3}} | collective-permute-start | bytes 4866056 | tf_op jit(solution)/shard_map/ppermute | solution.py:589
  781.0 70.6 %collective-permute-start.13 = (bf16[128,4224]{1,0:T(8,128)(2,1)}, bf16[128,4224]{1,0:T(8,128)(2,1)}, u32[]{:S(2)}, u32[]{:S(2)}) collective-permute-start(bf16[128,4224]{1,0:T(8,128)(2,1)} %collective-permute-done.refs_0_), channel_id=1, source_target_pairs={{0,1},{1,0},{2,3},{3,2},{4,5},{5,4},{6,7},{7,6}} | collective-permute-start | bytes 3244040 | tf_op jit(solution)/shard_map/ppermute | solution.py:589
  781.0 71.1 %collective-permute-start.14 = (bf16[128,4224]{1,0:T(8,128)(2,1)}, bf16[128,4224]{1,0:T(8,128)(2,1)}, u32[]{:S(2)}, u32[]{:S(2)}) collective-permute-start(bf16[128,4224]{1,0:T(8,128)(2,1)} %collective-permute-done.12.refs_1_), channel_id=1, source_target_pairs={{0,1},{1,0},{2,3},{3,2},{4,5},{5,4},{6,7},{7,6}} | collective-permute-start | bytes 3244040 | tf_op jit(solution)/shard_map/ppermute | solution.py:589
  810.2 59.6 %collective-permute-start.52 = (bf16[352,1536]{1,0:T(8,128)(2,1)}, bf16[352,1536]{1,0:T(8,128)(2,1)S(1)}, u32[]{:S(2)}, u32[]{:S(2)}) collective-permute-start(bf16[352,1536]{1,0:T(8,128)(2,1)} %collective-permute-done.51.refs_1_), channel_id=1, source_target_pairs={{0,4},{1,5},{2,6},{3,7},{4,0},{5,1},{6,2},{7,3}} | collective-permute-start | bytes 3244040 | tf_op jit(solution)/shard_map/ppermute | solution.py:589
  812.1 54.7 %collective-permute-start.63 = (bf16[352,1536]{1,0:T(8,128)(2,1)S(1)}, bf16[352,1536]{1,0:T(8,128)(2,1)S(1)}, u32[]{:S(2)}, u32[]{:S(2)}) collective-permute-start(bf16[352,1536]{1,0:T(8,128)(2,1)S(1)} %copy-done.30), channel_id=1, source_target_pairs={{0,1},{1,0},{2,3},{3,2},{4,5},{5,4},{6,7},{7,6}} | collective-permute-start | bytes 3244040 | tf_op jit(solution)/shard_map/ppermute | solution.py:589
  846.8 21.6 %collective-permute-start.64 = (bf16[352,1536]{1,0:T(8,128)(2,1)S(1)}, bf16[352,1536]{1,0:T(8,128)(2,1)}, u32[]{:S(2)}, u32[]{:S(2)}) collective-permute-start(bf16[352,1536]{1,0:T(8,128)(2,1)S(1)} %copy-done.32), channel_id=1, source_target_pairs={{0,1},{1,0},{2,3},{3,2},{4,5},{5,4},{6,7},{7,6}} | collective-permute-start | bytes 3244040 | tf_op jit(solution)/shard_map/ppermute | solution.py:589
  860.3 85.4 %collective-permute-start.34 = (bf16[192,4224]{1,0:T(8,128)(2,1)S(1)}, bf16[192,4224]{1,0:T(8,128)(2,1)S(1)}, u32[]{:S(2)}, u32[]{:S(2)}) collective-permute-start(bf16[192,4224]{1,0:T(8,128)(2,1)S(1)} %get-tuple-element.85.refs_0_), channel_id=1, source_target_pairs={{0,2},{1,3},{2,0},{3,1},{4,6},{5,7},{6,4},{7,5}} | collective-permute-start | bytes 4866056 | tf_op jit(solution)/shard_map/ppermute | solution.py:589
  863.3 58.4 %collective-permute-start.49 = (bf16[352,1536]{1,0:T(8,128)(2,1)S(1)}, bf16[352,1536]{1,0:T(8,128)(2,1)S(1)}, u32[]{:S(2)}, u32[]{:S(2)}) collective-permute-start(bf16[352,1536]{1,0:T(8,128)(2,1)S(1)} %copy-done.30), channel_id=1, source_target_pairs={{0,2},{1,3},{2,0},{3,1},{4,6},{5,7},{6,4},{7,5}} | collective-permute-start | bytes 3244040 | tf_op jit(solution)/shard_map/ppermute | solution.py:589
  867.8 56.7 %collective-permute-start.4 = (bf16[128,4224]{1,0:T(8,128)(2,1)}, bf16[128,4224]{1,0:T(8,128)(2,1)}, u32[]{:S(2)}, u32[]{:S(2)}) collective-permute-start(bf16[128,4224]{1,0:T(8,128)(2,1)} %collective-permute-done.3.refs_1_), channel_id=1, source_target_pairs={{0,4},{1,5},{2,6},{3,7},{4,0},{5,1},{6,2},{7,3}} | collective-permute-start | bytes 3244040 | tf_op jit(solution)/shard_map/ppermute | solution.py:589
  868.4 76.0 %collective-permute-start.1 = (bf16[128,4224]{1,0:T(8,128)(2,1)}, bf16[128,4224]{1,0:T(8,128)(2,1)S(1)}, u32[]{:S(2)}, u32[]{:S(2)}) collective-permute-start(bf16[128,4224]{1,0:T(8,128)(2,1)} %collective-permute-done.refs_0_), channel_id=1, source_target_pairs={{0,2},{1,3},{2,0},{3,1},{4,6},{5,7},{6,4},{7,5}} | collective-permute-start | bytes 3244040 | tf_op jit(solution)/shard_map/ppermute | solution.py:589
  869.8 76.1 %collective-permute-start.53 = (bf16[352,1536]{1,0:T(8,128)(2,1)S(1)}, bf16[352,1536]{1,0:T(8,128)(2,1)}, u32[]{:S(2)}, u32[]{:S(2)}) collective-permute-start(bf16[352,1536]{1,0:T(8,128)(2,1)S(1)} %collective-permute-done.52.refs_0_), channel_id=1, source_target_pairs={{0,1},{1,0},{2,3},{3,2},{4,5},{5,4},{6,7},{7,6}} | collective-permute-start | bytes 3244040 | tf_op jit(solution)/shard_map/ppermute | solution.py:589
  921.8 33.8 %collective-permute-start.50 = (bf16[352,1536]{1,0:T(8,128)(2,1)S(1)}, bf16[352,1536]{1,0:T(8,128)(2,1)S(1)}, u32[]{:S(2)}, u32[]{:S(2)}) collective-permute-start(bf16[352,1536]{1,0:T(8,128)(2,1)S(1)} %collective-permute-done.49.refs_0_), channel_id=1, source_target_pairs={{0,1},{1,0},{2,3},{3,2},{4,5},{5,4},{6,7},{7,6}} | collective-permute-start | bytes 3244040 | tf_op jit(solution)/shard_map/ppermute | solution.py:589
  924.5 33.2 %collective-permute-start.5 = (bf16[128,4224]{1,0:T(8,128)(2,1)}, bf16[128,4224]{1,0:T(8,128)(2,1)}, u32[]{:S(2)}, u32[]{:S(2)}) collective-permute-start(bf16[128,4224]{1,0:T(8,128)(2,1)} %collective-permute-done.4.refs_0_), channel_id=1, source_target_pairs={{0,1},{1,0},{2,3},{3,2},{4,5},{5,4},{6,7},{7,6}} | collective-permute-start | bytes 3244040 | tf_op jit(solution)/shard_map/ppermute | solution.py:589
  945.7 22.7 %collective-permute-start.40 = (bf16[192,4224]{1,0:T(8,128)(2,1)S(1)}, bf16[192,4224]{1,0:T(8,128)(2,1)}, u32[]{:S(2)}, u32[]{:S(2)}) collective-permute-start(bf16[192,4224]{1,0:T(8,128)(2,1)S(1)} %copy-done.11), channel_id=1, source_target_pairs={{0,1},{1,0},{2,3},{3,2},{4,5},{5,4},{6,7},{7,6}} | collective-permute-start | bytes 4866056 | tf_op jit(solution)/shard_map/ppermute | solution.py:589
  945.9 22.5 %collective-permute-start.39 = (bf16[192,4224]{1,0:T(8,128)(2,1)S(1)}, bf16[192,4224]{1,0:T(8,128)(2,1)S(1)}, u32[]{:S(2)}, u32[]{:S(2)}) collective-permute-start(bf16[192,4224]{1,0:T(8,128)(2,1)S(1)} %copy-done.13), channel_id=1, source_target_pairs={{0,1},{1,0},{2,3},{3,2},{4,5},{5,4},{6,7},{7,6}} | collective-permute-start | bytes 4866056 | tf_op jit(solution)/shard_map/ppermute | solution.py:589
  956.5 22.0 %collective-permute-start.37 = (bf16[192,4224]{1,0:T(8,128)(2,1)S(1)}, bf16[192,4224]{1,0:T(8,128)(2,1)S(1)}, u32[]{:S(2)}, u32[]{:S(2)}) collective-permute-start(bf16[192,4224]{1,0:T(8,128)(2,1)S(1)} %copy-done.5), channel_id=1, source_target_pairs={{0,1},{1,0},{2,3},{3,2},{4,5},{5,4},{6,7},{7,6}} | collective-permute-start | bytes 4866056 | tf_op jit(solution)/shard_map/ppermute | solution.py:589
  957.7 37.7 %collective-permute-start.32 = (bf16[192,4224]{1,0:T(8,128)(2,1)S(1)}, bf16[192,4224]{1,0:T(8,128)(2,1)S(1)}, u32[]{:S(2)}, u32[]{:S(2)}) collective-permute-start(bf16[192,4224]{1,0:T(8,128)(2,1)S(1)} %copy-done.11), channel_id=1, source_target_pairs={{0,4},{1,5},{2,6},{3,7},{4,0},{5,1},{6,2},{7,3}} | collective-permute-start | bytes 4866056 | tf_op jit(solution)/shard_map/ppermute | solution.py:589
  958.4 37.5 %collective-permute-start.29 = (bf16[192,4224]{1,0:T(8,128)(2,1)S(1)}, bf16[192,4224]{1,0:T(8,128)(2,1)S(1)}, u32[]{:S(2)}, u32[]{:S(2)}) collective-permute-start(bf16[192,4224]{1,0:T(8,128)(2,1)S(1)} %copy-done.9), channel_id=1, source_target_pairs={{0,2},{1,3},{2,0},{3,1},{4,6},{5,7},{6,4},{7,5}} | collective-permute-start | bytes 4866056 | tf_op jit(solution)/shard_map/ppermute | solution.py:589
  968.3 31.7 %collective-permute-start.35 = (bf16[192,4224]{1,0:T(8,128)(2,1)S(1)}, bf16[192,4224]{1,0:T(8,128)(2,1)}, u32[]{:S(2)}, u32[]{:S(2)}) collective-permute-start(bf16[192,4224]{1,0:T(8,128)(2,1)S(1)} %copy-done.9), channel_id=1, source_target_pairs={{0,1},{1,0},{2,3},{3,2},{4,5},{5,4},{6,7},{7,6}} | collective-permute-start | bytes 4866056 | tf_op jit(solution)/shard_map/ppermute | solution.py:589
  968.3 31.7 %collective-permute-start.36 = (bf16[192,4224]{1,0:T(8,128)(2,1)S(1)}, bf16[192,4224]{1,0:T(8,128)(2,1)}, u32[]{:S(2)}, u32[]{:S(2)}) collective-permute-start(bf16[192,4224]{1,0:T(8,128)(2,1)S(1)} %collective-permute-done.34.refs_1_), channel_id=1, source_target_pairs={{0,1},{1,0},{2,3},{3,2},{4,5},{5,4},{6,7},{7,6}} | collective-permute-start | bytes 4866056 | tf_op jit(solution)/shard_map/ppermute | solution.py:589
  978.5 20.7 %collective-permute-start.44 = (bf16[176,1536]{1,0:T(8,128)(2,1)}, bf16[176,1536]{1,0:T(8,128)(2,1)S(1)}, u32[]{:S(2)}, u32[]{:S(2)}) collective-permute-start(bf16[176,1536]{1,0:T(8,128)(2,1)} %collective-permute-done.43.refs_0_), channel_id=1, source_target_pairs={{0,1},{1,0},{2,3},{3,2},{4,5},{5,4},{6,7},{7,6}} | collective-permute-start | bytes 1622024 | tf_op jit(solution)/shard_map/ppermute | solution.py:589
  995.8 18.0 %collective-permute-start.30 = (bf16[192,4224]{1,0:T(8,128)(2,1)S(1)}, bf16[192,4224]{1,0:T(8,128)(2,1)S(1)}, u32[]{:S(2)}, u32[]{:S(2)}) collective-permute-start(bf16[192,4224]{1,0:T(8,128)(2,1)S(1)} %collective-permute-done.29.refs_0_), channel_id=1, source_target_pairs={{0,1},{1,0},{2,3},{3,2},{4,5},{5,4},{6,7},{7,6}} | collective-permute-start | bytes 4866056 | tf_op jit(solution)/shard_map/ppermute | solution.py:589
  (113 other events, 1343.0 us)

commit v3 on v2

v3 whole, which is shorter than its diff:
```python
import functools

import jax
import jax.numpy as jnp
from jax import lax
from jax.experimental import pallas as pl
from jax.experimental.pallas import tpu as pltpu
from jax.sharding import PartitionSpec as P


BF = jnp.bfloat16
F32 = jnp.float32
MESH = pl.DeviceIdType.MESH
TOKENS, D, FF, LAYERS = 2048, 1536, 4224, 2
BLOCK = 256
STEPS = -(-FF // BLOCK)
LAST = FF - (STEPS - 1) * BLOCK
PART = D // 8
SUB = BLOCK // 8
OWN_DOWN = FF // 8
LAST_SUB = OWN_DOWN - (STEPS - 1) * SUB
HALF = PART // 2
CHUNK = PART + HALF
COUNT = 3 * LAYERS * D * FF
THIRD = FF // 3
GATE, UP, DOWN = range(3)
AHEAD = 2 * THIRD
TILES = AHEAD // BLOCK
SPREAD = 13
VMEM_LIMIT = 67043328
SMALL_LIMIT = 48 << 20


ANY = pl.BlockSpec(memory_space=pl.ANY)
SQUEEZED = pl.Squeezed()
FACTOR = (8, 128)
FIRST = pl.BlockSpec(FACTOR, lambda *_: (0, 0))
GROUPS = {"own": (0, 1), "near": (4, 2, 5, 3), "across": (6,), "last": (7,), "ahead_own": (4, 2, 6), "ahead_partner": (5, 3, 7)}


def dot(a, b, dims="nn"):
    ca, cb = ("tn".index(dims[0]), "nt".index(dims[1]))
    return lax.dot_general(a, b, (((ca,), (cb,)), ((), ())), preferred_element_type=F32)


def resident(shape):
    return pl.BlockSpec(shape, lambda *_: (0,) * len(shape), pipeline_mode=pl.Buffered(1))


def cost(units, bytes_accessed):
    return pl.CostEstimate(flops=int(units * 2 * TOKENS * D * FF), bytes_accessed=int(bytes_accessed), transcendentals=0)


def normed(h):
    wide = h.astype(F32)
    scale = lax.rsqrt(jnp.mean(wide * wide, -1, keepdims=True) + 1e-6)
    return (wide * scale).astype(BF)


def neighbours():
    me = lax.axis_index("dp")
    x, y, c = lax.div(me, 4), lax.rem(lax.div(me, 2), 2), lax.rem(me, 2)
    return (me, x, y, c), [{"dp": me + k * (1 - 2 * t)} for k, t in ((1, c), (4, x), (2, y))]


def remote(src, dst, send, recv, to):
    return pltpu.make_async_remote_copy(src_ref=src, dst_ref=dst, send_sem=send, recv_sem=recv, device_id=to, device_id_type=MESH)


class Weights:
    def __init__(self, l, wg, wu, wd, gu_ref, down_ref, sems):
        self.l, self.wg, self.wu, self.wd, self.gu_ref, self.down_ref, self.sems = l, wg, wu, wd, gu_ref, down_ref, sems

    def copies(self, j, last):
        slot, block, l = lax.rem(j, 2), lax.rem(j, STEPS), self.l
        if l is None:
            l = lax.div(j, STEPS)
        width = LAST if last else BLOCK
        start = (STEPS - 1) * BLOCK if last else pl.multiple_of(block * BLOCK, BLOCK)
        columns = pl.ds(start, width)
        pairs = [
            (self.wg.at[l, :, columns], self.gu_ref.at[slot, :, pl.ds(0, width)]),
            (self.wu.at[l, :, columns], self.gu_ref.at[slot, :, pl.ds(BLOCK, width)]),
        ]
        if self.wd is not None:
            pairs.append((self.wd.at[l, columns], self.down_ref.at[slot, pl.ds(0, width)]))
        return [pltpu.make_async_copy(src, dst, self.sems.at[slot, n]) for n, (src, dst) in enumerate(pairs)]

    def each(self, j, act):
        block = lax.rem(j, STEPS)

        @pl.when(block < STEPS - 1)
        def _():
            for copy in self.copies(j, False):
                act(copy)

        @pl.when(block == STEPS - 1)
        def _():
            for copy in self.copies(j, True):
                act(copy)

    def start(self, j):
        self.each(j, lambda copy: copy.start())

    def wait(self, j):
        self.each(j, lambda copy: copy.wait())


def forward_kernel(x_ref, wg, wu, wd, m_in, v_in, *refs):
    a_out, ht_ref, sl_ref, q_ref, h_out, mv_out, *refs = refs
    a_ref, h_ref, gu_ref, down_ref, hid_ref, acc_ref, w_sems, sems, near_send, near_recv, far_send, far_recv = refs
    j = pl.program_id(0)
    block = lax.rem(j, STEPS)
    weights = Weights(None, wg, wu, wd, gu_ref, down_ref, w_sems)
    _, (_, to_x, to_y) = neighbours()
    barrier = pltpu.get_barrier_semaphore()
    keep = [pltpu.make_async_copy(a_ref, a_out.at[l], sems.at[l]) for l in range(LAYERS)]
    keep_h = pltpu.make_async_copy(h_ref, h_out, sems.at[2])

    def near(k):
        src = (m_in, v_in)[k].at[1, :, pl.ds(0, AHEAD)]
        return [remote(src, mv_out.at[k, n], near_send.at[k, n], near_recv.at[k, n], to) for n, to in enumerate((to_x, to_y))]

    def far(k):
        return [
            remote(mv_out.at[k, n, rows], mv_out.at[k, 2, rows], far_send.at[k, n], far_recv.at[k, n], to)
            for n, (rows, to) in enumerate(((pl.ds(0, HALF), to_y), (pl.ds(HALF, HALF), to_x)))
        ]

    @pl.when(j == 0)
    def _():
        for to in (to_x, to_y):
            pl.semaphore_signal(barrier, inc=1, device_id=to, device_id_type=MESH)
        weights.start(j)

        @pl.loop(0, TOKENS // 256)
        def _(i):
            r = pl.ds(pl.multiple_of(i * 256, 256), 256)
            a_ref[r, :] = normed(x_ref[r, :])
            acc_ref[r, :] = jnp.zeros((256, D), F32)

        keep[0].start()

    @pl.when(j == 2)
    def _():
        pl.semaphore_wait(barrier, 2)
        for k in range(2):
            for copy in near(k):
                copy.start()

    @pl.when(j == STEPS)
    def _():
        keep[0].wait()

        @pl.loop(0, TOKENS // 256)
        def _(i):
            r = pl.ds(pl.multiple_of(i * 256, 256), 256)
            h = x_ref[r, :] + acc_ref[r, :].astype(BF)
            h_ref[r, :] = h
            a_ref[r, :] = normed(h)

        keep[1].start()
        keep_h.start()

    @pl.when(j == STEPS + 4)
    def _():
        for k in range(2):
            for copy in near(k):
                copy.wait()
            for copy in far(k):
                copy.start()

    pl.when(j + 1 < LAYERS * STEPS)(lambda: weights.start(j + 1))
    weights.wait(j)
    slot = lax.rem(j, 2)
    for i in range(8):
        r = slice(256 * i, 256 * i + 256)
        gu = dot(a_ref[r, :], gu_ref[slot])
        g, u = gu[:, :BLOCK], gu[:, BLOCK:]
        s = jax.nn.sigmoid(g)
        sl = g * s
        sl_ref[0, r, :] = sl
        q_ref[0, r, :] = u * (s * (1.0 + g * (1.0 - s)))
        hid = (sl * u).astype(BF)
        hid_ref[r, :] = hid
        ht_ref[0, :, r] = hid.T

    @pl.when(j < STEPS)
    def _():
        @pl.when(block == STEPS - 1)
        def _():
            hid_ref[:, LAST:] = jnp.zeros((TOKENS, BLOCK - LAST), BF)

        acc_ref[...] += dot(hid_ref[...], down_ref[slot])

    @pl.when(j == LAYERS * STEPS - 1)
    def _():
        keep[1].wait()
        keep_h.wait()
        for k in range(2):
            for copy in far(k):
                copy.wait()


def forward(x, wg, wu, wd, m, v):
    layer = lambda j: lax.div(j, STEPS)
    block = lambda j: lax.rem(j, STEPS)
    wide = pl.BlockSpec((1, TOKENS, BLOCK), lambda j: (layer(j), 0, block(j)))
    shape = jax.ShapeDtypeStruct
    return pl.pallas_call(
        forward_kernel,
        grid=(LAYERS * STEPS,),
        in_specs=[resident((TOKENS, D))] + [ANY] * 5,
        out_specs=[ANY, pl.BlockSpec((1, BLOCK, TOKENS), lambda j: (layer(j), block(j), 0)), wide, wide, ANY, ANY],
        out_shape=[
            shape((LAYERS, TOKENS, D), BF),
            shape((LAYERS, FF, TOKENS), BF),
            *[shape((LAYERS, TOKENS, FF), F32)] * 2,
            shape((TOKENS, D), BF),
            shape((2, 3, PART, AHEAD), F32),
        ],
        scratch_shapes=[
            pltpu.VMEM((TOKENS, D), BF),
            pltpu.VMEM((TOKENS, D), BF),
            pltpu.VMEM((2, D, 2 * BLOCK), BF),
            pltpu.VMEM((2, BLOCK, D), BF),
            pltpu.VMEM((TOKENS, BLOCK), BF),
            pltpu.VMEM((TOKENS, D), F32),
            pltpu.SemaphoreType.DMA((2, 3)),
            pltpu.SemaphoreType.DMA((3,)),
            *[pltpu.SemaphoreType.DMA((2, 2))] * 4,
        ],
        compiler_params=pltpu.CompilerParams(vmem_limit_bytes=VMEM_LIMIT, collective_id=2, has_side_effects=True),
        cost_estimate=cost(5, 260e6),
        name="forward",
    )(x, wg, wu, wd, m, v)


def bits(o):
    return o // 4, o // 2 % 2, o % 2


class Lags:
    def __init__(self, second, third, b, e):
        self.second, self.third, self.b, self.e = second, third, b, e
        self.s = third + 1
        self.a = third + 2
        self.c = second + third
        self.d = 2 * (third - second)


def backward_kernel(l, lags, a_in, dy_ref, wd_ref, sl_ref, q_ref, ht_ref, *refs):
    with_da = l == 1
    if with_da:
        wg, wu, h_in, g_gate, g_up, g_down, sq_ref, dh_out, far_out, acc_ref, gu_ref, w_sems, *refs = refs
        near_send, near_recv, far_send, far_recv, *refs = refs
        weights = Weights(l, wg, wu, None, gu_ref, None, w_sems)
    else:
        other_ref, g_gate, g_up, g_down, f_ref, sq_ref, every_ref, f_send, f_recv, *refs = refs
    a_ref, dgu_ref, s_ref, a2_ref, bx, by, cx, cy, ex, ey, dx, dy2, og, ou, od, *sems = refs
    s_send, a_recv, bx_send, by_send, cx_recv, cy_recv, ex_send, ey_send, dx_recv, dy_recv, out_sem, a_sem = sems
    j = pl.program_id(0)
    (me, x, y, c), (to_core, to_x, to_y) = neighbours()
    xn, yn, cn = (1 - k for k in (x, y, c))
    others = [{"dp": lax.rem(me + k, 8)} for k in range(1, 8)]

    def columns(last):
        return pl.ds(0, LAST if last else BLOCK)

    def pair(i, last, which=(0, 1)):
        s, a, w = lax.rem(i, lags.s), lax.rem(i, lags.a), columns(last)
        return [
            remote(s_ref.at[s, n, :, :, cn, :, w], a2_ref.at[a, n, :, :, :, w], s_send.at[s, k], a_recv.at[a, k], to_core)
            for k, n in ((k, (pl.ds(0, 2), pl.ds(2, 1))[k]) for k in which)
        ]

    def first(i, last):
        b, k, w = lax.rem(i, lags.b), lax.rem(i, lags.c), columns(last)
        return [
            remote(bx.at[b, :, :, w], cx.at[k, :, :, w], bx_send.at[b], cx_recv.at[k], to_x),
            remote(by.at[b, :, :, w], cy.at[k, :, :, w], by_send.at[b], cy_recv.at[k], to_y),
        ]

    def second(i, last):
        e, k, w = lax.rem(i, lags.e), lax.rem(i, lags.d), columns(last)
        return [
            remote(ex.at[e, :, w], dx.at[k, :, w], ex_send.at[e], dx_recv.at[k], to_x),
            remote(ey.at[e, :, w], dy2.at[k, :, w], ey_send.at[e], dy_recv.at[k], to_y),
        ]

    def outs(i, last):
        o, p = lax.rem(i, 2), lax.rem(i, og.shape[0])
        if last:
            wide, deep = pl.ds((STEPS - 1) * BLOCK, LAST), pl.ds((STEPS - 1) * SUB, LAST_SUB)
            srcs = og.at[p, :, pl.ds(0, LAST)], ou.at[o, :, pl.ds(0, LAST)], od.at[o, pl.ds(0, LAST_SUB)]
        else:
            wide, deep = pl.ds(pl.multiple_of(i * BLOCK, BLOCK), BLOCK), pl.ds(pl.multiple_of(i * SUB, SUB), SUB)
            srcs = og.at[p], ou.at[o], od.at[o]
        dsts = g_gate.at[:, wide], g_up.at[:, wide], g_down.at[deep]
        return [pltpu.make_async_copy(s, d, out_sem.at[o, n]) for n, (s, d) in enumerate(zip(srcs, dsts))]

    def each(i, copies, act):
        @pl.when(i < STEPS - 1)
        def _():
            for copy in copies(i, False):
                act(copy)

        @pl.when(i == STEPS - 1)
        def _():
            for copy in copies(i, True):
                act(copy)

    def start(copy):
        copy.start()

    def total(*terms):
        return functools.reduce(lambda p, q: p + q, [t.astype(F32) for t in terms])

    def take_first(i):
        each(i, pair, lambda copy: copy.wait())
        s, a, b = lax.rem(i, lags.s), lax.rem(i, lags.a), lax.rem(i, lags.b)

        @pl.when(i >= lags.b)
        def _():
            for copy in first(i - lags.b, False):
                copy.wait_send()

        for t in range(2):
            bx[b, t, :PART] = total(s_ref[s, GATE, xn, t, c], a2_ref[a, GATE, xn, t]).astype(BF)
            bx[b, t, PART:] = total(s_ref[s, DOWN, xn, t, c, :HALF], a2_ref[a, DOWN, xn, t, :HALF]).astype(BF)
            by[b, t, :PART] = total(s_ref[s, UP, t, yn, c], a2_ref[a, UP, t, yn]).astype(BF)
            by[b, t, PART:] = total(s_ref[s, DOWN, t, yn, c, HALF:], a2_ref[a, DOWN, t, yn, HALF:]).astype(BF)
        each(i, first, start)

    def take_second(i):
        each(i, first, lambda copy: copy.wait_recv())
        s, a, k, e = lax.rem(i, lags.s), lax.rem(i, lags.a), lax.rem(i, lags.c), lax.rem(i, lags.e)

        @pl.when(i >= lags.e)
        def _():
            for copy in second(i - lags.e, False):
                copy.wait_send()

        ey[e, :PART] = total(s_ref[s, GATE, x, yn, c], a2_ref[a, GATE, x, yn], cx[k, yn, :PART]).astype(BF)
        ey[e, PART:] = total(s_ref[s, DOWN, x, yn, c, :HALF], a2_ref[a, DOWN, x, yn, :HALF], cx[k, yn, PART:]).astype(BF)
        ex[e, :PART] = total(s_ref[s, UP, xn, y, c], a2_ref[a, UP, xn, y], cy[k, xn, :PART]).astype(BF)
        ex[e, PART:] = total(s_ref[s, DOWN, xn, y, c, HALF:], a2_ref[a, DOWN, xn, y, HALF:], cy[k, xn, PART:]).astype(BF)
        each(i, second, start)

    def take_third(i):
        each(i, second, lambda copy: copy.wait_recv())
        s, a, k, d, o = (lax.rem(i, n) for n in (lags.s, lags.a, lags.c, lags.d, 2))

        @pl.when(i >= 1)
        def _():
            for copy in outs(i - 1, False):
                copy.wait()

        gate = total(s_ref[s, GATE, x, y, c], a2_ref[a, GATE, x, y], cx[k, y, :PART], dy2[d, :PART]).astype(BF)
        up = total(s_ref[s, UP, x, y, c], a2_ref[a, UP, x, y], cy[k, x, :PART], dx[d, :PART]).astype(BF)
        og[lax.rem(i, og.shape[0])] = gate
        ou[o] = up
        low = total(s_ref[s, DOWN, x, y, c, :HALF], a2_ref[a, DOWN, x, y, :HALF], cx[k, y, PART:], dy2[d, PART:]).astype(BF)
        high = total(s_ref[s, DOWN, x, y, c, HALF:], a2_ref[a, DOWN, x, y, HALF:], cy[k, x, PART:], dx[d, PART:]).astype(BF)
        downs = [half[SUB * n : SUB * n + SUB] for half in (low, high) for n in range(HALF // SUB)]

        def squares(t):
            wide = t.astype(F32)
            return jnp.sum((wide * wide).reshape(-1, 8, t.shape[-1]), 0)

        @pl.when(i < STEPS - 1)
        def _():
            for n, one in enumerate(downs):
                od[o, :, BLOCK * n : BLOCK * n + BLOCK] = one
            sq_ref[...] += squares(gate) + squares(up) + squares(low) + squares(high)

        @pl.when(i == STEPS - 1)
        def _():
            for n, one in enumerate(downs):
                od[o, :LAST_SUB, BLOCK * n : BLOCK * n + LAST] = one[:LAST_SUB, :LAST]
                od[o, :LAST_SUB, BLOCK * n + LAST : BLOCK * n + BLOCK] = one[LAST_SUB:, :LAST]
            sq_ref[:, :LAST] += sum(squares(t[:, :LAST]) for t in (gate, up, low, high))

        each(i, outs, start)

    def near(t):
        k = lax.rem(t, 4)
        src = og.at[lax.rem(t, og.shape[0])]
        return [remote(src, far_out.at[n, t], near_send.at[k, n], near_recv.at[k, n], to) for n, to in enumerate((to_x, to_y))]

    def far(t):
        k = lax.rem(t, 4)
        return [
            remote(far_out.at[n, t, rows], far_out.at[2, t, rows], far_send.at[k, n], far_recv.at[k, n], to)
            for n, (rows, to) in enumerate(((pl.ds(0, HALF), to_y), (pl.ds(HALF, HALF), to_x)))
        ]

    def at_step(n, act):
        t = lax.div(n * TILES, SPREAD)

        @pl.when((n >= 0) & (n < SPREAD) & ((n == 0) | (t > lax.div((n - 1) * TILES, SPREAD))))
        def _():
            act(t)

    def pass_on(t):
        for copy in near(t):
            copy.wait()
        for copy in far(t):
            copy.start()

    take_a = pltpu.make_async_copy(a_in.at[l], a_ref, a_sem.at[0])

    barrier = pltpu.get_barrier_semaphore()
    greeted = (to_core, to_x, to_y) if with_da else others

    @pl.when(j == 0)
    def _():
        take_a.start()
        for to in greeted:
            pl.semaphore_signal(barrier, inc=1, device_id=to, device_id_type=MESH)
        sq_ref[...] = jnp.zeros_like(sq_ref)
        if with_da:
            weights.start(j)

            @pl.loop(0, TOKENS // 256)
            def _(i):
                acc_ref[pl.ds(pl.multiple_of(i * 256, 256), 256), :] = jnp.zeros((256, D), F32)

    @pl.when(j < STEPS)
    def _():
        if with_da:
            pl.when(j + 1 < STEPS)(lambda: weights.start(j + 1))
        s = lax.rem(j, lags.s)
        for i in range(4):
            r = slice(512 * i, 512 * i + 512)
            dh = dot(dy_ref[r, :], wd_ref[0], "nt").astype(BF).astype(F32)
            dgu_ref[r, :BLOCK] = (dh * q_ref[0, r, :]).astype(BF)
            dgu_ref[r, BLOCK:] = (dh * sl_ref[0, r, :]).astype(BF)

        pl.when(j == 0)(lambda: take_a.wait())

        @pl.when(j == STEPS - 1)
        def _():
            dgu_ref[:, LAST:BLOCK] = jnp.zeros((TOKENS, BLOCK - LAST), BF)
            dgu_ref[:, BLOCK + LAST :] = jnp.zeros((TOKENS, BLOCK - LAST), BF)

        for h in range(2):
            gu = dot(a_ref[:, D // 2 * h : D // 2 * (h + 1)], dgu_ref[...], "tn")
            for o in range(4):
                for t in range(2):
                    s_ref[s, t, h, o // 2, o % 2] = gu[PART * o : PART * o + PART, BLOCK * t : BLOCK * t + BLOCK].astype(BF)
        pl.when(j == 0)(lambda: pl.semaphore_wait(barrier, len(greeted)))
        each(j, functools.partial(pair, which=(0,)), start)
        for h in range(2):
            down = dot(ht_ref[...].reshape(BLOCK, TOKENS), dy_ref[:, D // 2 * h : D // 2 * (h + 1)])
            for o in range(8):
                for n in range(3):
                    s_ref[(s, DOWN, *bits(o), slice(SUB * (3 * h + n), SUB * (3 * h + n + 1)))] = down[
                        SUB * o : SUB * o + SUB, BLOCK * n : BLOCK * n + BLOCK
                    ].astype(BF)

        @pl.when(j == STEPS - 1)
        def _():
            for o in range(8):
                for n in range(6):
                    half = SUB * n + LAST_SUB
                    s_ref[(s, DOWN, *bits(o), slice(half, SUB * n + SUB), slice(LAST))] = s_ref[
                        (s, DOWN, *bits(o), slice(SUB * n, half), slice(LAST, BLOCK))
                    ]

        each(j, functools.partial(pair, which=(1,)), start)
        if with_da:
            weights.wait(j)
            for i in range(4):
                r = slice(512 * i, 512 * i + 512)
                acc_ref[r, :] += dot(dgu_ref[r, :], gu_ref[lax.rem(j, 2)], "nt")

    if with_da:
        take_h = pltpu.make_async_copy(h_in, a_ref, a_sem.at[1])
        give_dh = pltpu.make_async_copy(a_ref, dh_out, a_sem.at[2])
        pl.when(j == STEPS - 1)(lambda: take_h.start())

        @pl.when(j == STEPS)
        def _():
            take_h.wait()

            @pl.loop(0, TOKENS // 128)
            def _(i):
                r = pl.ds(pl.multiple_of(i * 128, 128), 128)
                h = a_ref[r, :].astype(F32)
                da = acc_ref[r, :].astype(BF).astype(F32)
                scale = lax.rsqrt(jnp.mean(h * h, -1, keepdims=True) + 1e-6)
                along = jnp.sum(da * h, -1, keepdims=True) * (scale * scale * scale) * (1.0 / D)
                a_ref[r, :] = dy_ref[r, :] + (da * scale - h * along).astype(BF)

            give_dh.start()

    pl.when((j >= lags.third) & (j < STEPS + lags.third))(lambda: take_third(j - lags.third))
    pl.when((j >= lags.second) & (j < STEPS + lags.second))(lambda: take_second(j - lags.second))
    pl.when(j < STEPS)(lambda: take_first(j))
    if with_da:
        soonest = lags.third
        at_step(j - soonest - 4, lambda t: [copy.wait() for copy in far(t)])
        at_step(j - soonest - 2, pass_on)
        at_step(j - soonest, lambda t: [copy.start() for copy in near(t)])

    @pl.when(j == STEPS + lags.third - 1)
    def _():
        if not with_da:
            both = sq_ref[...] + other_ref[...]
            every_ref[me] = both[:, :128] + both[:, 128:]
            for n, to in enumerate(others):
                remote(every_ref.at[me], every_ref.at[me], f_send.at[n], f_recv.at[n], to).start()
        for i in range(STEPS - lags.b, STEPS):
            for copy in first(jnp.int32(i), i == STEPS - 1):
                copy.wait_send()
        for i in range(STEPS - lags.e, STEPS):
            for copy in second(jnp.int32(i), i == STEPS - 1):
                copy.wait_send()
        for copy in outs(jnp.int32(STEPS - 1), True):
            copy.wait()
        if with_da:
            give_dh.wait()
        else:
            for n, to in enumerate(others):
                remote(every_ref.at[me], every_ref.at[me], f_send.at[n], f_recv.at[n], to).wait()
            squares = functools.reduce(lambda p, q: p + q, [every_ref[n] for n in range(8)])
            squares = jnp.sum(jnp.sum(squares, axis=1, keepdims=True), axis=0, keepdims=True)
            f_ref[...] = jnp.broadcast_to(jnp.minimum(1.0, 0.5 * lax.rsqrt(squares / COUNT + 1e-30)), FACTOR)


def backward(l, lags, a, dy, wd, sl, q, ht, *more):
    with_da = l == 1
    at = lambda j: jnp.minimum(j, STEPS - 1)
    wide = pl.BlockSpec((1, TOKENS, BLOCK), lambda j: (l, 0, at(j)))
    sums = pl.BlockSpec((8, BLOCK), lambda j: (0, 0))
    in_specs = [
        ANY,
        resident((TOKENS, D)),
        pl.BlockSpec((1, BLOCK, D), lambda j: (l, at(j), 0)),
        wide,
        wide,
        pl.BlockSpec((8, SUB, TOKENS), lambda j: (l, at(j), 0)),
    ]
    args = [a, dy, wd, sl, q, ht.reshape(LAYERS * 8, OWN_DOWN, TOKENS), *more]
    out_shape = [jax.ShapeDtypeStruct((PART, FF), BF)] * 2 + [jax.ShapeDtypeStruct((OWN_DOWN, D), BF)]
    if with_da:
        in_specs += [ANY] * 3
        out_shape += [jax.ShapeDtypeStruct(*t) for t in (((8, BLOCK), F32), ((TOKENS, D), BF), ((3, TILES) + (PART, BLOCK), BF))]
        out_specs = [ANY] * 3 + [sums, ANY, ANY]
        scratch = [pltpu.VMEM((TOKENS, D), F32), pltpu.VMEM((2, D, 2 * BLOCK), BF), pltpu.SemaphoreType.DMA((2, 3))]
        scratch += [pltpu.SemaphoreType.DMA((4, 2))] * 4
    else:
        in_specs += [sums]
        out_shape += [jax.ShapeDtypeStruct(FACTOR, F32)]
        out_specs = [ANY] * 3 + [FIRST]
        scratch = [pltpu.VMEM((8, BLOCK), F32), pltpu.VMEM((8, 8, 128), F32), *[pltpu.SemaphoreType.DMA((7,))] * 2]
    piece = (PART, BLOCK)
    scratch += [
        pltpu.VMEM((TOKENS, D), BF),
        pltpu.VMEM((TOKENS, 2 * BLOCK), BF),
        pltpu.VMEM((lags.s, 3, 2, 2, 2) + piece, BF),
        pltpu.VMEM((lags.a, 3, 2, 2) + piece, BF),
        *[pltpu.VMEM((lags.b, 2, CHUNK, BLOCK), BF)] * 2,
        *[pltpu.VMEM((lags.c, 2, CHUNK, BLOCK), BF)] * 2,
        *[pltpu.VMEM((lags.e, CHUNK, BLOCK), BF)] * 2,
        *[pltpu.VMEM((lags.d, CHUNK, BLOCK), BF)] * 2,
        pltpu.VMEM((6 if with_da else 2,) + piece, BF),
        pltpu.VMEM((2,) + piece, BF),
        pltpu.VMEM((2, SUB, D), BF),
    ]
    scratch += [pltpu.SemaphoreType.DMA((n, 2)) for n in (lags.s, lags.a)]
    scratch += [pltpu.SemaphoreType.DMA((n,)) for n in (lags.b, lags.b, lags.c, lags.c, lags.e, lags.e, lags.d, lags.d)]
    scratch += [pltpu.SemaphoreType.DMA((2, 3)), pltpu.SemaphoreType.DMA((3,))]
    return pl.pallas_call(
        functools.partial(backward_kernel, l, lags),
        grid=(STEPS + lags.third,),
        in_specs=in_specs,
        out_specs=out_specs,
        out_shape=out_shape,
        scratch_shapes=scratch,
        compiler_params=pltpu.CompilerParams(vmem_limit_bytes=VMEM_LIMIT, collective_id=l, has_side_effects=True),
        cost_estimate=cost(6 if with_da else 4, 150e6),
    )(*args)


def stepped(factor, g, w, m, v):
    g, w = g.astype(F32) * factor, w.astype(F32)
    m = 0.9 * m + 0.1 * g
    v = 0.95 * v + 0.05 * g * g
    return (w - 0.02 * (m * lax.rsqrt(v + 1e-8) + 0.1 * w)).astype(BF), m, v


def adamw_kernel(at_ref, f_ref, g_ref, w_ref, m_ref, v_ref, *refs):
    nw_ref, nm_ref, nv_ref = refs[-3:]
    factor = f_ref[:1, :1]

    @pl.loop(0, g_ref.shape[0] // 16)
    def _(i):
        r = pl.ds(pl.multiple_of(i * 16, 16), 16)
        nw_ref[r, :], nm_ref[0, r, :], nv_ref[0, r, :] = stepped(factor, g_ref[r, :], w_ref[0, r, :], m_ref[0, r, :], v_ref[0, r, :])


def thirds(shape, axis):
    return tuple(n // 3 if k == axis else n for k, n in enumerate(shape))


def spot(axis, i, other=0):
    return (i, other) if axis == 0 else (other, i)


def adamw(piece, at, factor, g, w, m, v, so_far=None):
    _, l, axis, skip, count = piece
    block = thirds(g.shape, axis)
    moment = pl.BlockSpec((1, *block), lambda i, at: (l, *spot(axis, skip + i)))
    in_specs = [
        FIRST,
        pl.BlockSpec(block, lambda i, at: spot(axis, skip + i)),
        pl.BlockSpec((1, *block), lambda i, at: (l, 3 * at[0] + skip + i, 0) if axis == 0 else (l, at[0], skip + i)),
        moment,
        moment,
    ]
    args = [factor, g, w, m, v]
    aliases = {}
    if so_far is not None:
        in_specs += [ANY, ANY]
        args += so_far
        aliases = {6: 1, 7: 2}
    new = tuple(n * count if k == axis else n for k, n in enumerate(block))
    return pl.pallas_call(
        adamw_kernel,
        grid_spec=pltpu.PrefetchScalarGridSpec(
            num_scalar_prefetch=1,
            grid=(count,),
            in_specs=in_specs,
            out_specs=[pl.BlockSpec(block, lambda i, at: spot(axis, i)), moment, moment],
        ),
        out_shape=[jax.ShapeDtypeStruct(new, BF)] + [jax.ShapeDtypeStruct(m.shape, F32)] * 2,
        input_output_aliases=aliases,
        compiler_params=pltpu.CompilerParams(vmem_limit_bytes=SMALL_LIMIT),
        cost_estimate=cost(0.1, m.size),
    )(at, *args)


def adamw_ahead_kernel(owners_ref, f_ref, g_ref, w_ref, m_ref, v_ref, nw_ref):
    factor = f_ref[:1, :1]

    @pl.loop(0, PART // 32)
    def _(i):
        r = pl.ds(pl.multiple_of(i * 32, 32), 32)
        nw_ref[0, r, :], _, _ = stepped(factor, g_ref[r, :], w_ref[0, r, :], m_ref[r, :], v_ref[r, :])


def adamw_ahead(owners, factor, g, w, mv):
    block = (PART, BLOCK)
    return pl.pallas_call(
        adamw_ahead_kernel,
        grid_spec=pltpu.PrefetchScalarGridSpec(
            num_scalar_prefetch=1,
            grid=(3, TILES),
            in_specs=[
                FIRST,
                pl.BlockSpec((SQUEEZED, SQUEEZED, *block), lambda s, t, own: (s, t, 0, 0)),
                pl.BlockSpec((1, *block), lambda s, t, own: (1, own[s], t)),
                *[pl.BlockSpec((SQUEEZED, SQUEEZED, *block), lambda s, t, own, k=k: (k, s, 0, t)) for k in range(2)],
            ],
            out_specs=pl.BlockSpec((1, *block), lambda s, t, own: (s, 0, t)),
        ),
        out_shape=jax.ShapeDtypeStruct((3, PART, AHEAD), BF),
        compiler_params=pltpu.CompilerParams(vmem_limit_bytes=SMALL_LIMIT),
        cost_estimate=cost(0.1, 14 * 3 * PART * AHEAD),
        name="adamw_ahead",
    )(owners, factor, g, w, mv, mv)


def place_kernel(n, owners_ref, *refs):
    out_ref = refs[-1]
    s = pl.program_id(0)
    for k in range(n):

        @pl.when(s == k)
        def _():
            out_ref[0] = refs[k][...]


def place(piece, owners, pieces, so_far, whole):
    _, l, axis, skip, count = piece
    n = len(pieces)
    block = tuple(m // count if k == axis else m for k, m in enumerate(pieces[0].shape))

    def of(k):
        return lambda s, i, own: spot(axis, jnp.where(s == k, i, jnp.where(s < k, 0, count - 1)))

    in_specs = [pl.BlockSpec(block, of(k)) for k in range(n)]
    args = list(pieces)
    aliases = {}
    if so_far is not None:
        in_specs.append(ANY)
        args.append(so_far)
        aliases = {n + 1: 0}
    return pl.pallas_call(
        functools.partial(place_kernel, n),
        grid_spec=pltpu.PrefetchScalarGridSpec(
            num_scalar_prefetch=1,
            grid=(n, count),
            in_specs=in_specs,
            out_specs=pl.BlockSpec(
                (1, *block), lambda s, i, own: (l, 3 * own[s] + skip + i, 0) if axis == 0 else (l, own[s], skip + i)
            ),
        ),
        out_shape=jax.ShapeDtypeStruct(whole.shape, BF),
        input_output_aliases=aliases,
        compiler_params=pltpu.CompilerParams(vmem_limit_bytes=SMALL_LIMIT),
        cost_estimate=cost(0.1, whole.size),
    )(owners, *args)


def place_ahead_kernel(owners_ref, new_ref, so_far, out_ref):
    out_ref[...] = new_ref[...]


def place_ahead(owners, new, so_far):
    block = (1, PART, THIRD)
    return pl.pallas_call(
        place_ahead_kernel,
        grid_spec=pltpu.PrefetchScalarGridSpec(
            num_scalar_prefetch=1,
            grid=(3, 2),
            in_specs=[pl.BlockSpec(block, lambda s, i, own: (s, 0, i)), ANY],
            out_specs=pl.BlockSpec(block, lambda s, i, own: (1, own[s], i)),
        ),
        out_shape=jax.ShapeDtypeStruct(so_far.shape, BF),
        input_output_aliases={2: 0},
        compiler_params=pltpu.CompilerParams(vmem_limit_bytes=SMALL_LIMIT),
        cost_estimate=cost(0.1, 4 * 3 * PART * AHEAD),
        name="place_ahead",
    )(owners, new, so_far)


PIECES = [(GATE, 1, 1, 2, 1)] + [(GATE, 0, 1, n, 1) for n in range(3)]
PIECES += [(n, l, 0, *part) for n, part in ((UP, (0, 3)), (DOWN, (0, 2)), (DOWN, (2, 1))) for l in range(LAYERS)]
KNOWN = (0, 1, 1, 0, 2)


def solution(mesh):
    def swap(t, mask):
        return lax.ppermute(t, "dp", [(i, i ^ mask) for i in range(8)])

    def step(x, dy, wg, wu, wd, mg, mu, md, vg, vu, vd):
        x, dy = x[0], dy[0]
        me = lax.axis_index("dp")
        a, ht, sl, q, h1, mv = forward(x, wg, wu, wd, mg, vg)
        *g1, squares, dh1, g_ahead = backward(1, Lags(1, 2, 2, 2), a, dy, wd, sl, q, ht, wg, wu, h1)
        *g0, factor = backward(0, Lags(2, 4, 3, 3), a, dh1, wd, sl, q, ht, squares)
        at = me[None].astype(jnp.int32)
        groups = {name: jnp.stack([me ^ k for k in group]).astype(jnp.int32) for name, group in GROUPS.items()}
        mats = ((wg, mg, vg), (wu, mu, vu), (wd, md, vd))
        moments, whole = [None] * 3, [None] * 3

        def put(kind, piece, have):
            n = piece[0]
            whole[n] = place(piece, groups[kind], [have[k] for k in GROUPS[kind]], whole[n], mats[n][0])

        def new_rows(piece):
            n, l = piece[:2]
            new, *moments[n] = adamw(piece, at, factor, (g0, g1)[l][n], *mats[n], moments[n])
            return new

        everything = []
        for number, piece in enumerate(PIECES):
            have = {}
            everything.append(have)
            have[0] = new_rows(piece)
            have[4] = swap(have[0], 4)
            have[2] = swap(have[0], 2)
            have[6] = swap(have[4], 2) if number % 2 else swap(have[2], 4)
            for k in (0, 4, 2, 6):
                have[k + 1] = swap(have[k], 1)
            put("own", piece, have)
            put("near", piece, have)
        have = {0: new_rows(KNOWN)}
        have[1] = swap(have[0], 1)
        put("own", KNOWN, have)
        ahead = adamw_ahead(groups["ahead_own"], factor, g_ahead, wg, mv)
        for kind, new in (("ahead_own", ahead), ("ahead_partner", swap(ahead, 1))):
            whole[0] = place_ahead(groups[kind], new, whole[0])
        for piece, have in zip(PIECES, everything):
            put("across", piece, have)
            put("last", piece, have)
        return tuple(whole + [m[0] for m in moments] + [m[1] for m in moments])

    whole, rows = P(), P(None, "dp")
    return jax.shard_map(
        step,
        mesh=mesh,
        in_specs=(P(("rep", "dp")),) * 2 + (whole,) * 3 + (rows,) * 6,
        out_specs=(P("rep"),) * 3 + (P("rep", "dp"),) * 6,
        check_vma=False,
    )
```

time: 1020 us -> 1010 us (level)
  waiting for transfers between devices: 216 us -> 175 us
  Pallas kernels: 734 us -> 771 us
    ppermute x70 -> x72, waiting for transfers between devices: 216 us -> 175 us  [swap(): return lax.ppermute(t, 'dp', [(i, i ^ mask) for i in range(8)])]
    pallas_call x2 -> x4, Pallas kernels: 170 us -> 208 us  [the longest x1 169 us: forward(): pl.pallas_call(forward_kernel, grid=(LAYERS * STEPS,), in_specs=[resident...]
    pallas_call x40 -> x41, Pallas kernels: 111 us -> 98.5 us  [place(): pl.pallas_call(functools.partial(place_kernel, n), grid_spec=pltpu.Prefet...]
    pallas_call x10 -> x11, Pallas kernels: 56.9 us -> 59.9 us  [adamw(): pl.pallas_call(adamw_kernel, grid_spec=pltpu.PrefetchScalarGridSpec(num_s...]
    ppermute x70 -> x72, starting transfers between devices: 37.4 us -> 38.9 us  [swap(): return lax.ppermute(t, 'dp', [(i, i ^ mask) for i in range(8)])]
  transfers between devices with their start and end apart: 70 -> 72, of which waited for: 22 -> 19; matrix products, arithmetic and copies ran while one was open for 0% -> 0% of each run, Pallas kernels for 15% -> 18%
where the time goes in v3:
time: 1010 us
  Pallas kernels  771 us (76%)
  waiting for transfers between devices  175 us (17%)
  starting transfers between devices  38.9 us (4%)
  local copies, waits for them, and re-layouts  20.2 us (2%)
    pallas_call x2, Pallas kernels, backward(): pl.pallas_call(functools.partial(backward_kernel, l, lags), grid=(STEPS +...  406 us
    ppermute x72, waiting for transfers between devices, swap(): return lax.ppermute(t, 'dp', [(i, i ^ mask) for i in range(8)])  175 us
    pallas_call x1, Pallas kernels, forward(): pl.pallas_call(forward_kernel, grid=(LAYERS * STEPS,), in_specs=[resident...  169 us
    pallas_call x41, Pallas kernels, place(): pl.pallas_call(functools.partial(place_kernel, n), grid_spec=pltpu.Prefet...  98.5 us
    pallas_call x11, Pallas kernels, adamw(): pl.pallas_call(adamw_kernel, grid_spec=pltpu.PrefetchScalarGridSpec(num_s...  59.9 us
    ppermute x72, starting transfers between devices, swap(): return lax.ppermute(t, 'dp', [(i, i ^ mask) for i in range(8)])  38.9 us
    pallas_call x1, Pallas kernels, adamw_ahead(): pl.pallas_call(adamw_ahead_kernel, grid_spec=pltpu.PrefetchScalarGridSpec...  26.3 us
    unnamed x182, local copies, waits for them, and re-layouts  20.2 us
  transfers between devices with their start and end apart: 72, of which 19 were waited for; matrix products, arithmetic and copies ran while one was open for 0% of the time, Pallas kernels for 18%

profile of v3, /device:TPU:0, one launch (start us, length us, event | category | flops | bytes accessed | tf_op | source)
XLA Modules:
  0.0 1007.0 jit_solution(13139562536047171816)
XLA Ops:
  0.6 169.3 %forward.1 = (bf16[2,2048,1536]{2,1,0:T(8,128)(2,1)}, bf16[2,4224,2048]{2,1,0:T(8,128)(2,1)}, f32[2,2048,4224]{2,1,0:T(8,128)}, f32[2,2048,4224]{2,1,0:T(8,128)}...) custom-call(bf16[2048,1536]{1,0:T(8,128)(2,1)} %bitcast.11, bf16[2,1536,4224]{2,1,0:T(8,128)(2,1)} %w_ref.17, ...), custom_call_target="tpu_custom_call" | custom-call | flops 132875550720 | bytes 260000000 | tf_op jit(solution)/shard_map/forward/pallas_call | solution.py:210
  170.0 223.2 %shard_map.178 = (bf16[192,4224]{1,0:T(8,128)(2,1)}, bf16[192,4224]{1,0:T(8,128)(2,1)}, bf16[528,1536]{1,0:T(8,128)(2,1)}, f32[8,256]{1,0:T(8,128)}, bf16[2048,1...) custom-call(bf16[2,2048,1536]{2,1,0:T(8,128)(2,1)} %get-tuple-element.58.a_in, bf16[2048,1536]{1,0:T(8,128)(2,1)} %bitcast.12, ...), custom_call_target="tpu_custom_call" | custom-call | flops 159450660864 | bytes 150000000 | tf_op jit(solution)/shard_map/pallas_call | solution.py:575
  393.2 182.4 %shard_map.179 = (bf16[192,4224]{1,0:T(8,128)(2,1)}, bf16[192,4224]{1,0:T(8,128)(2,1)}, bf16[528,1536]{1,0:T(8,128)(2,1)}, f32[8,128]{1,0:T(8,128)}) custom-call(bf16[2,2048,1536]{2,1,0:T(8,128)(2,1)} %get-tuple-element.58.a_in, bf16[2048,1536]{1,0:T(8,128)(2,1)} %get-tuple-element.63.dy_ref, bf16[2,4224,1536]{2,1,0:T(8,128)(2,1)} %w_ref.23, ...), custom_call_target="tpu_custom_call" | custom-call | flops 106300440576 | bytes 150000000 | tf_op jit(solution)/shard_map/pallas_call | solution.py:575
  577.7 5.4 shard_map.212
  583.0 5.6 shard_map.213
  588.7 4.5 shard_map.214
  595.4 4.2 shard_map.215
  600.5 4.3 shard_map.180
  605.9 2.6 collective-permute-done.60.refs_0_
  611.5 4.2 shard_map.181
  615.7 4.4 collective-permute-done.44.refs_0_
  623.9 4.2 shard_map.182
  628.0 4.3 collective-permute-done.9.refs_1_
  633.6 4.2 shard_map.183
  638.8 4.5 collective-permute-done.6.refs_0_
  646.3 8.5 collective-permute-done.18.refs_0_
  659.5 6.9 collective-permute-done.refs_0_
  666.4 3.7 collective-permute-done.14.refs_1_
  673.1 20.1 %collective-permute-done.53.refs_1_ = bf16[352,1536]{1,0:T(8,128)(2,1)} collective-permute-done((bf16[352,1536]{1,0:T(8,128)(2,1)S(1)}, bf16[352,1536]{1,0:T(8,128)(2,1)}, u32[]{:S(2)}, u32[]{:S(2)}) %collective-permute-start.53) | collective-permute-done | bytes 1081376 | tf_op jit(solution)/shard_map/ppermute | solution.py:747
  694.8 17.3 %collective-permute-done.50.refs_0_ = bf16[352,1536]{1,0:T(8,128)(2,1)S(1)} collective-permute-done((bf16[352,1536]{1,0:T(8,128)(2,1)S(1)}, bf16[352,1536]{1,0:T(8,128)(2,1)S(1)}, u32[]{:S(2)}, u32[]{:S(2)}) %collective-permute-start.50) | collective-permute-done | bytes 1081376 | tf_op jit(solution)/shard_map/ppermute | solution.py:747
  713.1 5.7 shard_map.184
  721.1 8.9 shard_map.202
  730.0 8.9 shard_map.203
  741.1 26.3 %adamw_ahead.1.new_ref = bf16[3,192,2816]{2,1,0:T(8,128)(2,1)} custom-call(s32[3]{0:T(128)S(1)} %pad_add_fusion.1.owners_ref, f32[8,128]{1,0:T(8,128)S(1)} %copy-done.23, bf16[3,11,192,256]{3,2,1,0:T(8,128)(2,1)} %get-tuple-element.78.g_ref, bf16[2,1536,4224]{2,1,0:T(8,128)(2,1)} %w_ref.17, f32[2,3,192,2816]{3,2,1,0:T(8,128)} %get-tuple-element.79.m_ref.v_ref, ...), custom_call_target="tpu_custom_call" | custom-call | flops 2657510912 | bytes 22708224 | tf_op jit(solution)/shard_map/adamw_ahead/pallas_call | solution.py:656
  774.7 2.4 shard_map.186.refs_2_
  780.0 4.6 collective-permute-done.10.refs_0_
  785.8 3.5 shard_map.188.refs_2_
  791.9 30.8 %collective-permute-done.7.refs_0_ = bf16[192,1408]{1,0:T(8,128)(2,1)S(1)} collective-permute-done((bf16[192,1408]{1,0:T(8,128)(2,1)}, bf16[192,1408]{1,0:T(8,128)(2,1)S(1)}, u32[]{:S(2)}, u32[]{:S(2)}) %collective-permute-start.7) | collective-permute-done | bytes 540704 | tf_op jit(solution)/shard_map/ppermute | solution.py:747
  826.1 2.4 shard_map.190.refs_2_
  832.4 3.5 shard_map.192.refs_2_
  836.2 2.7 shard_map.193.so_far
  838.9 6.0 place_ahead.2.so_far
  846.2 2.7 shard_map.216.refs_4_
  848.9 3.3 shard_map.204.refs_4_
  853.5 7.9 shard_map.217.refs_2_
  862.2 2.4 shard_map.218.refs_4_
  864.7 7.9 shard_map.219.refs_2_
  874.2 4.0 shard_map.221.refs_2_
  881.1 3.8 shard_map.223.refs_1_
  884.9 2.2 shard_map.224.refs_1_
  887.1 19.2 %collective-permute-done.30.refs_0_ = bf16[192,4224]{1,0:T(8,128)(2,1)S(1)} collective-permute-done((bf16[192,4224]{1,0:T(8,128)(2,1)S(1)}, bf16[192,4224]{1,0:T(8,128)(2,1)S(1)}, u32[]{:S(2)}, u32[]{:S(2)}) %collective-permute-start.30) | collective-permute-done | bytes 1622048 | tf_op jit(solution)/shard_map/ppermute | solution.py:747
  911.0 5.1 collective-permute-done.36.refs_1_
  916.6 5.9 place_ahead.3.refs_1_
  927.8 7.8 shard_map.205.refs_2_
  935.6 3.3 shard_map.206.refs_4_
  939.7 31.8 %collective-permute-done.4.refs_0_ = bf16[192,1408]{1,0:T(8,128)(2,1)S(1)} collective-permute-done((bf16[192,1408]{1,0:T(8,128)(2,1)S(1)}, bf16[192,1408]{1,0:T(8,128)(2,1)S(1)}, u32[]{:S(2)}, u32[]{:S(2)}) %collective-permute-start.4) | collective-permute-done | bytes 540704 | tf_op jit(solution)/shard_map/ppermute | solution.py:747
  974.4 9.5 shard_map.207.refs_1_
  987.5 8.9 collective-permute-done.1.refs_0_
  (340 shorter events, 91.1 us)
Async XLA Ops:
  599.6 20.4 %collective-permute-start.44 = (bf16[176,1536]{1,0:T(8,128)(2,1)S(1)}, bf16[176,1536]{1,0:T(8,128)(2,1)S(1)}, u32[]{:S(2)}, u32[]{:S(2)}) collective-permute-start(bf16[176,1536]{1,0:T(8,128)(2,1)S(1)} %get-tuple-element.97.refs_0_), channel_id=1, source_target_pairs={{0,4},{1,5},{2,6},{3,7},{4,0},{5,1},{6,2},{7,3}} | collective-permute-start | bytes 1622024 | tf_op jit(solution)/shard_map/ppermute | solution.py:747
  609.3 23.1 %collective-permute-start.9 = (bf16[192,1408]{1,0:T(8,128)(2,1)S(1)}, bf16[192,1408]{1,0:T(8,128)(2,1)S(1)}, u32[]{:S(2)}, u32[]{:S(2)}) collective-permute-start(bf16[192,1408]{1,0:T(8,128)(2,1)S(1)} %get-tuple-element.77.refs_0_), channel_id=1, source_target_pairs={{0,2},{1,3},{2,0},{3,1},{4,6},{5,7},{6,4},{7,5}} | collective-permute-start | bytes 1622024 | tf_op jit(solution)/shard_map/ppermute | solution.py:747
  610.7 21.7 %collective-permute-start.26 = (bf16[192,1408]{1,0:T(8,128)(2,1)S(1)}, bf16[192,1408]{1,0:T(8,128)(2,1)S(1)}, u32[]{:S(2)}, u32[]{:S(2)}) collective-permute-start(bf16[192,1408]{1,0:T(8,128)(2,1)S(1)} %get-tuple-element.77.refs_0_), channel_id=1, source_target_pairs={{0,4},{1,5},{2,6},{3,7},{4,0},{5,1},{6,2},{7,3}} | collective-permute-start | bytes 1622024 | tf_op jit(solution)/shard_map/ppermute | solution.py:747
  620.9 22.4 %collective-permute-start.6 = (bf16[192,1408]{1,0:T(8,128)(2,1)S(1)}, bf16[192,1408]{1,0:T(8,128)(2,1)}, u32[]{:S(2)}, u32[]{:S(2)}) collective-permute-start(bf16[192,1408]{1,0:T(8,128)(2,1)S(1)} %get-tuple-element.76.refs_0_), channel_id=1, source_target_pairs={{0,4},{1,5},{2,6},{3,7},{4,0},{5,1},{6,2},{7,3}} | collective-permute-start | bytes 1622024 | tf_op jit(solution)/shard_map/ppermute | solution.py:747
  622.9 21.3 %collective-permute-start.22 = (bf16[192,1408]{1,0:T(8,128)(2,1)S(1)}, bf16[192,1408]{1,0:T(8,128)(2,1)S(1)}, u32[]{:S(2)}, u32[]{:S(2)}) collective-permute-start(bf16[192,1408]{1,0:T(8,128)(2,1)S(1)} %get-tuple-element.76.refs_0_), channel_id=1, source_target_pairs={{0,2},{1,3},{2,0},{3,1},{4,6},{5,7},{6,4},{7,5}} | collective-permute-start | bytes 1622024 | tf_op jit(solution)/shard_map/ppermute | solution.py:747
  632.4 22.4 %collective-permute-start.18 = (bf16[192,1408]{1,0:T(8,128)(2,1)S(1)}, bf16[192,1408]{1,0:T(8,128)(2,1)S(1)}, u32[]{:S(2)}, u32[]{:S(2)}) collective-permute-start(bf16[192,1408]{1,0:T(8,128)(2,1)S(1)} %get-tuple-element.75.refs_0_), channel_id=1, source_target_pairs={{0,4},{1,5},{2,6},{3,7},{4,0},{5,1},{6,2},{7,3}} | collective-permute-start | bytes 1622024 | tf_op jit(solution)/shard_map/ppermute | solution.py:747
  638.6 32.2 %collective-permute-start.71 = (bf16[352,1536]{1,0:T(8,128)(2,1)S(1)}, bf16[352,1536]{1,0:T(8,128)(2,1)S(1)}, u32[]{:S(2)}, u32[]{:S(2)}) collective-permute-start(bf16[352,1536]{1,0:T(8,128)(2,1)S(1)} %get-tuple-element.100.refs_0_), channel_id=1, source_target_pairs={{0,1},{1,0},{2,3},{3,2},{4,5},{5,4},{6,7},{7,6}} | collective-permute-start | bytes 3244040 | tf_op jit(solution)/shard_map/ppermute | solution.py:747
  645.1 21.3 %collective-permute-start = (bf16[192,1408]{1,0:T(8,128)(2,1)S(1)}, bf16[192,1408]{1,0:T(8,128)(2,1)S(1)}, u32[]{:S(2)}, u32[]{:S(2)}) collective-permute-start(bf16[192,1408]{1,0:T(8,128)(2,1)S(1)} %get-tuple-element.74.refs_0_), channel_id=1, source_target_pairs={{0,4},{1,5},{2,6},{3,7},{4,0},{5,1},{6,2},{7,3}} | collective-permute-start | bytes 1622024 | tf_op jit(solution)/shard_map/ppermute | solution.py:747
  656.6 36.7 %collective-permute-start.53 = (bf16[352,1536]{1,0:T(8,128)(2,1)S(1)}, bf16[352,1536]{1,0:T(8,128)(2,1)}, u32[]{:S(2)}, u32[]{:S(2)}) collective-permute-start(bf16[352,1536]{1,0:T(8,128)(2,1)S(1)} %get-tuple-element.100.refs_0_), channel_id=1, source_target_pairs={{0,2},{1,3},{2,0},{3,1},{4,6},{5,7},{6,4},{7,5}} | collective-permute-start | bytes 3244040 | tf_op jit(solution)/shard_map/ppermute | solution.py:747
  658.4 34.8 %collective-permute-start.68 = (bf16[352,1536]{1,0:T(8,128)(2,1)S(1)}, bf16[352,1536]{1,0:T(8,128)(2,1)S(1)}, u32[]{:S(2)}, u32[]{:S(2)}) collective-permute-start(bf16[352,1536]{1,0:T(8,128)(2,1)S(1)} %get-tuple-element.100.refs_0_), channel_id=1, source_target_pairs={{0,4},{1,5},{2,6},{3,7},{4,0},{5,1},{6,2},{7,3}} | collective-permute-start | bytes 3244040 | tf_op jit(solution)/shard_map/ppermute | solution.py:747
  666.4 27.4 %collective-permute-start.67 = (bf16[352,1536]{1,0:T(8,128)(2,1)S(1)}, bf16[352,1536]{1,0:T(8,128)(2,1)S(1)}, u32[]{:S(2)}, u32[]{:S(2)}) collective-permute-start(bf16[352,1536]{1,0:T(8,128)(2,1)S(1)} %get-tuple-element.99.refs_0_), channel_id=1, source_target_pairs={{0,1},{1,0},{2,3},{3,2},{4,5},{5,4},{6,7},{7,6}} | collective-permute-start | bytes 3244040 | tf_op jit(solution)/shard_map/ppermute | solution.py:747
  670.0 42.1 %collective-permute-start.50 = (bf16[352,1536]{1,0:T(8,128)(2,1)S(1)}, bf16[352,1536]{1,0:T(8,128)(2,1)S(1)}, u32[]{:S(2)}, u32[]{:S(2)}) collective-permute-start(bf16[352,1536]{1,0:T(8,128)(2,1)S(1)} %get-tuple-element.99.refs_0_), channel_id=1, source_target_pairs={{0,4},{1,5},{2,6},{3,7},{4,0},{5,1},{6,2},{7,3}} | collective-permute-start | bytes 3244040 | tf_op jit(solution)/shard_map/ppermute | solution.py:747
  671.8 48.0 %collective-permute-start.64 = (bf16[352,1536]{1,0:T(8,128)(2,1)S(1)}, bf16[352,1536]{1,0:T(8,128)(2,1)}, u32[]{:S(2)}, u32[]{:S(2)}) collective-permute-start(bf16[352,1536]{1,0:T(8,128)(2,1)S(1)} %get-tuple-element.99.refs_0_), channel_id=1, source_target_pairs={{0,2},{1,3},{2,0},{3,1},{4,6},{5,7},{6,4},{7,5}} | collective-permute-start | bytes 3244040 | tf_op jit(solution)/shard_map/ppermute | solution.py:747
  693.2 27.4 %collective-permute-start.61 = (bf16[176,1536]{1,0:T(8,128)(2,1)}, bf16[176,1536]{1,0:T(8,128)(2,1)}, u32[]{:S(2)}, u32[]{:S(2)}) collective-permute-start(bf16[176,1536]{1,0:T(8,128)(2,1)} %collective-permute-done.60.refs_0_), channel_id=1, source_target_pairs={{0,1},{1,0},{2,3},{3,2},{4,5},{5,4},{6,7},{7,6}} | collective-permute-start | bytes 1622024 | tf_op jit(solution)/shard_map/ppermute | solution.py:747
  693.2 27.4 %collective-permute-start.62 = (bf16[176,1536]{1,0:T(8,128)(2,1)}, bf16[176,1536]{1,0:T(8,128)(2,1)}, u32[]{:S(2)}, u32[]{:S(2)}) collective-permute-start(bf16[176,1536]{1,0:T(8,128)(2,1)} %collective-permute-done.47.refs_1_), channel_id=1, source_target_pairs={{0,1},{1,0},{2,3},{3,2},{4,5},{5,4},{6,7},{7,6}} | collective-permute-start | bytes 1622024 | tf_op jit(solution)/shard_map/ppermute | solution.py:747
  694.7 35.2 %collective-permute-start.57 = (bf16[176,1536]{1,0:T(8,128)(2,1)S(1)}, bf16[176,1536]{1,0:T(8,128)(2,1)}, u32[]{:S(2)}, u32[]{:S(2)}) collective-permute-start(bf16[176,1536]{1,0:T(8,128)(2,1)S(1)} %collective-permute-done.44.refs_0_), channel_id=1, source_target_pairs={{0,1},{1,0},{2,3},{3,2},{4,5},{5,4},{6,7},{7,6}} | collective-permute-start | bytes 1622024 | tf_op jit(solution)/shard_map/ppermute | solution.py:747
  712.1 26.8 %collective-permute-start.58 = (bf16[176,1536]{1,0:T(8,128)(2,1)}, bf16[176,1536]{1,0:T(8,128)(2,1)}, u32[]{:S(2)}, u32[]{:S(2)}) collective-permute-start(bf16[176,1536]{1,0:T(8,128)(2,1)} %collective-permute-done.56.refs_1_), channel_id=1, source_target_pairs={{0,1},{1,0},{2,3},{3,2},{4,5},{5,4},{6,7},{7,6}} | collective-permute-start | bytes 1622024 | tf_op jit(solution)/shard_map/ppermute | solution.py:747
  719.8 19.7 %collective-permute-start.48 = (bf16[176,1536]{1,0:T(8,128)(2,1)}, bf16[176,1536]{1,0:T(8,128)(2,1)S(1)}, u32[]{:S(2)}, u32[]{:S(2)}) collective-permute-start(bf16[176,1536]{1,0:T(8,128)(2,1)} %collective-permute-done.47.refs_1_), channel_id=1, source_target_pairs={{0,4},{1,5},{2,6},{3,7},{4,0},{5,1},{6,2},{7,3}} | collective-permute-start | bytes 1622024 | tf_op jit(solution)/shard_map/ppermute | solution.py:747
  730.0 37.4 %collective-permute-start.23 = (bf16[192,1408]{1,0:T(8,128)(2,1)}, bf16[192,1408]{1,0:T(8,128)(2,1)S(1)}, u32[]{:S(2)}, u32[]{:S(2)}) collective-permute-start(bf16[192,1408]{1,0:T(8,128)(2,1)} %collective-permute-done.6.refs_0_), channel_id=1, source_target_pairs={{0,1},{1,0},{2,3},{3,2},{4,5},{5,4},{6,7},{7,6}} | collective-permute-start | bytes 1622024 | tf_op jit(solution)/shard_map/ppermute | solution.py:747
  738.9 29.0 %collective-permute-start.24 = (bf16[192,1408]{1,0:T(8,128)(2,1)S(1)}, bf16[192,1408]{1,0:T(8,128)(2,1)S(1)}, u32[]{:S(2)}, u32[]{:S(2)}) collective-permute-start(bf16[192,1408]{1,0:T(8,128)(2,1)S(1)} %copy-done.68), channel_id=1, source_target_pairs={{0,1},{1,0},{2,3},{3,2},{4,5},{5,4},{6,7},{7,6}} | collective-permute-start | bytes 1622024 | tf_op jit(solution)/shard_map/ppermute | solution.py:747
  739.5 38.8 %collective-permute-start.13 = (bf16[192,2816]{1,0:T(8,128)(2,1)S(1)}, bf16[192,2816]{1,0:T(8,128)(2,1)S(1)}, u32[]{:S(2)}, u32[]{:S(2)}) collective-permute-start(bf16[192,2816]{1,0:T(8,128)(2,1)S(1)} %copy-done.17), channel_id=1, source_target_pairs={{0,1},{1,0},{2,3},{3,2},{4,5},{5,4},{6,7},{7,6}} | collective-permute-start | bytes 3244040 | tf_op jit(solution)/shard_map/ppermute | solution.py:747
  739.6 29.4 %collective-permute-start.19 = (bf16[192,1408]{1,0:T(8,128)(2,1)S(1)}, bf16[192,1408]{1,0:T(8,128)(2,1)S(1)}, u32[]{:S(2)}, u32[]{:S(2)}) collective-permute-start(bf16[192,1408]{1,0:T(8,128)(2,1)S(1)} %copy-done.61), channel_id=1, source_target_pairs={{0,1},{1,0},{2,3},{3,2},{4,5},{5,4},{6,7},{7,6}} | collective-permute-start | bytes 1622024 | tf_op jit(solution)/shard_map/ppermute | solution.py:747
  740.9 28.5 %collective-permute-start.20 = (bf16[192,1408]{1,0:T(8,128)(2,1)S(1)}, bf16[192,1408]{1,0:T(8,128)(2,1)S(1)}, u32[]{:S(2)}, u32[]{:S(2)}) collective-permute-start(bf16[192,1408]{1,0:T(8,128)(2,1)S(1)} %copy-done.49), channel_id=1, source_target_pairs={{0,1},{1,0},{2,3},{3,2},{4,5},{5,4},{6,7},{7,6}} | collective-permute-start | bytes 1622024 | tf_op jit(solution)/shard_map/ppermute | solution.py:747
  769.0 63.2 %collective-permute-start.43 = (bf16[192,4224]{1,0:T(8,128)(2,1)S(1)}, bf16[192,4224]{1,0:T(8,128)(2,1)S(1)}, u32[]{:S(2)}, u32[]{:S(2)}) collective-permute-start(bf16[192,4224]{1,0:T(8,128)(2,1)S(1)} %get-tuple-element.88.refs_0_), channel_id=1, source_target_pairs={{0,1},{1,0},{2,3},{3,2},{4,5},{5,4},{6,7},{7,6}} | collective-permute-start | bytes 4866056 | tf_op jit(solution)/shard_map/ppermute | solution.py:747
  773.8 62.1 %collective-permute-start.33 = (bf16[192,4224]{1,0:T(8,128)(2,1)S(1)}, bf16[192,4224]{1,0:T(8,128)(2,1)S(1)}, u32[]{:S(2)}, u32[]{:S(2)}) collective-permute-start(bf16[192,4224]{1,0:T(8,128)(2,1)S(1)} %get-tuple-element.88.refs_0_), channel_id=1, source_target_pairs={{0,2},{1,3},{2,0},{3,1},{4,6},{5,7},{6,4},{7,5}} | collective-permute-start | bytes 4866056 | tf_op jit(solution)/shard_map/ppermute | solution.py:747
  777.2 45.5 %collective-permute-start.7 = (bf16[192,1408]{1,0:T(8,128)(2,1)}, bf16[192,1408]{1,0:T(8,128)(2,1)S(1)}, u32[]{:S(2)}, u32[]{:S(2)}) collective-permute-start(bf16[192,1408]{1,0:T(8,128)(2,1)} %collective-permute-done.6.refs_0_), channel_id=1, source_target_pairs={{0,2},{1,3},{2,0},{3,1},{4,6},{5,7},{6,4},{7,5}} | collective-permute-start | bytes 1622024 | tf_op jit(solution)/shard_map/ppermute | solution.py:747
  778.3 45.1 %collective-permute-start.49 = (bf16[176,1536]{1,0:T(8,128)(2,1)S(1)}, bf16[176,1536]{1,0:T(8,128)(2,1)S(1)}, u32[]{:S(2)}, u32[]{:S(2)}) collective-permute-start(bf16[176,1536]{1,0:T(8,128)(2,1)S(1)} %collective-permute-done.48.refs_0_), channel_id=1, source_target_pairs={{0,1},{1,0},{2,3},{3,2},{4,5},{5,4},{6,7},{7,6}} | collective-permute-start | bytes 1622024 | tf_op jit(solution)/shard_map/ppermute | solution.py:747
  784.5 60.3 %collective-permute-start.40 = (bf16[192,4224]{1,0:T(8,128)(2,1)S(1)}, bf16[192,4224]{1,0:T(8,128)(2,1)S(1)}, u32[]{:S(2)}, u32[]{:S(2)}) collective-permute-start(bf16[192,4224]{1,0:T(8,128)(2,1)S(1)} %get-tuple-element.88.refs_0_), channel_id=1, source_target_pairs={{0,4},{1,5},{2,6},{3,7},{4,0},{5,1},{6,2},{7,3}} | collective-permute-start | bytes 4866056 | tf_op jit(solution)/shard_map/ppermute | solution.py:747
  823.4 21.6 %collective-permute-start.70 = (bf16[352,1536]{1,0:T(8,128)(2,1)}, bf16[352,1536]{1,0:T(8,128)(2,1)}, u32[]{:S(2)}, u32[]{:S(2)}) collective-permute-start(bf16[352,1536]{1,0:T(8,128)(2,1)} %collective-permute-done.53.refs_1_), channel_id=1, source_target_pairs={{0,1},{1,0},{2,3},{3,2},{4,5},{5,4},{6,7},{7,6}} | collective-permute-start | bytes 3244040 | tf_op jit(solution)/shard_map/ppermute | solution.py:747
  823.5 21.9 %collective-permute-start.69 = (bf16[352,1536]{1,0:T(8,128)(2,1)S(1)}, bf16[352,1536]{1,0:T(8,128)(2,1)}, u32[]{:S(2)}, u32[]{:S(2)}) collective-permute-start(bf16[352,1536]{1,0:T(8,128)(2,1)S(1)} %copy-done.21), channel_id=1, source_target_pairs={{0,1},{1,0},{2,3},{3,2},{4,5},{5,4},{6,7},{7,6}} | collective-permute-start | bytes 3244040 | tf_op jit(solution)/shard_map/ppermute | solution.py:747
  832.2 19.9 %collective-permute-start.65 = (bf16[352,1536]{1,0:T(8,128)(2,1)S(1)}, bf16[352,1536]{1,0:T(8,128)(2,1)}, u32[]{:S(2)}, u32[]{:S(2)}) collective-permute-start(bf16[352,1536]{1,0:T(8,128)(2,1)S(1)} %copy-done.19), channel_id=1, source_target_pairs={{0,1},{1,0},{2,3},{3,2},{4,5},{5,4},{6,7},{7,6}} | collective-permute-start | bytes 3244040 | tf_op jit(solution)/shard_map/ppermute | solution.py:747
  835.9 25.5 %collective-permute-start.66 = (bf16[352,1536]{1,0:T(8,128)(2,1)}, bf16[352,1536]{1,0:T(8,128)(2,1)}, u32[]{:S(2)}, u32[]{:S(2)}) collective-permute-start(bf16[352,1536]{1,0:T(8,128)(2,1)} %collective-permute-done.64.refs_1_), channel_id=1, source_target_pairs={{0,1},{1,0},{2,3},{3,2},{4,5},{5,4},{6,7},{7,6}} | collective-permute-start | bytes 3244040 | tf_op jit(solution)/shard_map/ppermute | solution.py:747
  844.9 71.3 %collective-permute-start.12 = (bf16[3,192,2816]{2,1,0:T(8,128)(2,1)}, bf16[3,192,2816]{2,1,0:T(8,128)(2,1)}, u32[]{:S(2)}, u32[]{:S(2)}) collective-permute-start(bf16[3,192,2816]{2,1,0:T(8,128)(2,1)} %adamw_ahead.1.new_ref), channel_id=1, source_target_pairs={{0,1},{1,0},{2,3},{3,2},{4,5},{5,4},{6,7},{7,6}} | collective-permute-start | bytes 9732104 | tf_op jit(solution)/shard_map/ppermute | solution.py:747
  845.1 33.1 %collective-permute-start.39 = (bf16[192,4224]{1,0:T(8,128)(2,1)S(1)}, bf16[192,4224]{1,0:T(8,128)(2,1)S(1)}, u32[]{:S(2)}, u32[]{:S(2)}) collective-permute-start(bf16[192,4224]{1,0:T(8,128)(2,1)S(1)} %get-tuple-element.87.refs_0_), channel_id=1, source_target_pairs={{0,1},{1,0},{2,3},{3,2},{4,5},{5,4},{6,7},{7,6}} | collective-permute-start | bytes 4866056 | tf_op jit(solution)/shard_map/ppermute | solution.py:747
  845.4 27.2 %collective-permute-start.54 = (bf16[352,1536]{1,0:T(8,128)(2,1)}, bf16[352,1536]{1,0:T(8,128)(2,1)}, u32[]{:S(2)}, u32[]{:S(2)}) collective-permute-start(bf16[352,1536]{1,0:T(8,128)(2,1)} %collective-permute-done.53.refs_1_), channel_id=1, source_target_pairs={{0,4},{1,5},{2,6},{3,7},{4,0},{5,1},{6,2},{7,3}} | collective-permute-start | bytes 3244040 | tf_op jit(solution)/shard_map/ppermute | solution.py:747
  852.2 27.1 %collective-permute-start.51 = (bf16[352,1536]{1,0:T(8,128)(2,1)S(1)}, bf16[352,1536]{1,0:T(8,128)(2,1)S(1)}, u32[]{:S(2)}, u32[]{:S(2)}) collective-permute-start(bf16[352,1536]{1,0:T(8,128)(2,1)S(1)} %copy-done.19), channel_id=1, source_target_pairs={{0,2},{1,3},{2,0},{3,1},{4,6},{5,7},{6,4},{7,5}} | collective-permute-start | bytes 3244040 | tf_op jit(solution)/shard_map/ppermute | solution.py:747
  861.4 44.9 %collective-permute-start.30 = (bf16[192,4224]{1,0:T(8,128)(2,1)S(1)}, bf16[192,4224]{1,0:T(8,128)(2,1)S(1)}, u32[]{:S(2)}, u32[]{:S(2)}) collective-permute-start(bf16[192,4224]{1,0:T(8,128)(2,1)S(1)} %get-tuple-element.87.refs_0_), channel_id=1, source_target_pairs={{0,4},{1,5},{2,6},{3,7},{4,0},{5,1},{6,2},{7,3}} | collective-permute-start | bytes 4866056 | tf_op jit(solution)/shard_map/ppermute | solution.py:747
  872.6 33.8 %collective-permute-start.55 = (bf16[352,1536]{1,0:T(8,128)(2,1)}, bf16[352,1536]{1,0:T(8,128)(2,1)S(1)}, u32[]{:S(2)}, u32[]{:S(2)}) collective-permute-start(bf16[352,1536]{1,0:T(8,128)(2,1)} %collective-permute-done.54.refs_0_), channel_id=1, source_target_pairs={{0,1},{1,0},{2,3},{3,2},{4,5},{5,4},{6,7},{7,6}} | collective-permute-start | bytes 3244040 | tf_op jit(solution)/shard_map/ppermute | solution.py:747
  878.2 38.0 %collective-permute-start.36 = (bf16[192,4224]{1,0:T(8,128)(2,1)S(1)}, bf16[192,4224]{1,0:T(8,128)(2,1)}, u32[]{:S(2)}, u32[]{:S(2)}) collective-permute-start(bf16[192,4224]{1,0:T(8,128)(2,1)S(1)} %get-tuple-element.87.refs_0_), channel_id=1, source_target_pairs={{0,2},{1,3},{2,0},{3,1},{4,6},{5,7},{6,4},{7,5}} | collective-permute-start | bytes 4866056 | tf_op jit(solution)/shard_map/ppermute | solution.py:747
  879.3 29.6 %collective-permute-start.52 = (bf16[352,1536]{1,0:T(8,128)(2,1)S(1)}, bf16[352,1536]{1,0:T(8,128)(2,1)S(1)}, u32[]{:S(2)}, u32[]{:S(2)}) collective-permute-start(bf16[352,1536]{1,0:T(8,128)(2,1)S(1)} %collective-permute-done.51.refs_0_), channel_id=1, source_target_pairs={{0,1},{1,0},{2,3},{3,2},{4,5},{5,4},{6,7},{7,6}} | collective-permute-start | bytes 3244040 | tf_op jit(solution)/shard_map/ppermute | solution.py:747
  906.3 20.3 %collective-permute-start.41 = (bf16[192,4224]{1,0:T(8,128)(2,1)S(1)}, bf16[192,4224]{1,0:T(8,128)(2,1)S(1)}, u32[]{:S(2)}, u32[]{:S(2)}) collective-permute-start(bf16[192,4224]{1,0:T(8,128)(2,1)S(1)} %collective-permute-done.40.refs_0_), channel_id=1, source_target_pairs={{0,1},{1,0},{2,3},{3,2},{4,5},{5,4},{6,7},{7,6}} | collective-permute-start | bytes 4866056 | tf_op jit(solution)/shard_map/ppermute | solution.py:747
  916.1 57.4 %collective-permute-start.37 = (bf16[192,4224]{1,0:T(8,128)(2,1)S(1)}, bf16[192,4224]{1,0:T(8,128)(2,1)}, u32[]{:S(2)}, u32[]{:S(2)}) collective-permute-start(bf16[192,4224]{1,0:T(8,128)(2,1)S(1)} %collective-permute-done.30.refs_0_), channel_id=1, source_target_pairs={{0,1},{1,0},{2,3},{3,2},{4,5},{5,4},{6,7},{7,6}} | collective-permute-start | bytes 4866056 | tf_op jit(solution)/shard_map/ppermute | solution.py:747
  916.1 58.2 %collective-permute-start.38 = (bf16[192,4224]{1,0:T(8,128)(2,1)}, bf16[192,4224]{1,0:T(8,128)(2,1)}, u32[]{:S(2)}, u32[]{:S(2)}) collective-permute-start(bf16[192,4224]{1,0:T(8,128)(2,1)} %collective-permute-done.36.refs_1_), channel_id=1, source_target_pairs={{0,1},{1,0},{2,3},{3,2},{4,5},{5,4},{6,7},{7,6}} | collective-permute-start | bytes 4866056 | tf_op jit(solution)/shard_map/ppermute | solution.py:747
  922.5 61.4 %collective-permute-start.34 = (bf16[192,4224]{1,0:T(8,128)(2,1)S(1)}, bf16[192,4224]{1,0:T(8,128)(2,1)S(1)}, u32[]{:S(2)}, u32[]{:S(2)}) collective-permute-start(bf16[192,4224]{1,0:T(8,128)(2,1)S(1)} %copy-done.7), channel_id=1, source_target_pairs={{0,4},{1,5},{2,6},{3,7},{4,0},{5,1},{6,2},{7,3}} | collective-permute-start | bytes 4866056 | tf_op jit(solution)/shard_map/ppermute | solution.py:747
  925.9 45.6 %collective-permute-start.4 = (bf16[192,1408]{1,0:T(8,128)(2,1)S(1)}, bf16[192,1408]{1,0:T(8,128)(2,1)S(1)}, u32[]{:S(2)}, u32[]{:S(2)}) collective-permute-start(bf16[192,1408]{1,0:T(8,128)(2,1)S(1)} %copy-done.51), channel_id=1, source_target_pairs={{0,4},{1,5},{2,6},{3,7},{4,0},{5,1},{6,2},{7,3}} | collective-permute-start | bytes 1622024 | tf_op jit(solution)/shard_map/ppermute | solution.py:747
  926.7 70.3 %collective-permute-start.31 = (bf16[192,4224]{1,0:T(8,128)(2,1)S(1)}, bf16[192,4224]{1,0:T(8,128)(2,1)S(1)}, u32[]{:S(2)}, u32[]{:S(2)}) collective-permute-start(bf16[192,4224]{1,0:T(8,128)(2,1)S(1)} %collective-permute-done.30.refs_0_), channel_id=1, source_target_pairs={{0,2},{1,3},{2,0},{3,1},{4,6},{5,7},{6,4},{7,5}} | collective-permute-start | bytes 4866056 | tf_op jit(solution)/shard_map/ppermute | solution.py:747
  973.5 22.9 %collective-permute-start.1 = (bf16[192,1408]{1,0:T(8,128)(2,1)S(1)}, bf16[192,1408]{1,0:T(8,128)(2,1)S(1)}, u32[]{:S(2)}, u32[]{:S(2)}) collective-permute-start(bf16[192,1408]{1,0:T(8,128)(2,1)S(1)} %copy-done.39), channel_id=1, source_target_pairs={{0,2},{1,3},{2,0},{3,1},{4,6},{5,7},{6,4},{7,5}} | collective-permute-start | bytes 1622024 | tf_op jit(solution)/shard_map/ppermute | solution.py:747
  974.4 22.0 %collective-permute-start.8 = (bf16[192,1408]{1,0:T(8,128)(2,1)S(1)}, bf16[192,1408]{1,0:T(8,128)(2,1)S(1)}, u32[]{:S(2)}, u32[]{:S(2)}) collective-permute-start(bf16[192,1408]{1,0:T(8,128)(2,1)S(1)} %copy-done.27), channel_id=1, source_target_pairs={{0,1},{1,0},{2,3},{3,2},{4,5},{5,4},{6,7},{7,6}} | collective-permute-start | bytes 1622024 | tf_op jit(solution)/shard_map/ppermute | solution.py:747
  (115 other events, 1480.7 us)

commit v4 on v3

--- a/solution.py
+++ b/solution.py
@@ -15,6 +15,7 @@
 BLOCK = 256
 STEPS = -(-FF // BLOCK)
 LAST = FF - (STEPS - 1) * BLOCK
+ALL = LAYERS * STEPS
 PART = D // 8
 SUB = BLOCK // 8
 OWN_DOWN = FF // 8
@@ -170,7 +171,7 @@
             for copy in far(k):
                 copy.start()
 
-    pl.when(j + 1 < LAYERS * STEPS)(lambda: weights.start(j + 1))
+    pl.when(j + 1 < ALL)(lambda: weights.start(j + 1))
     weights.wait(j)
     slot = lax.rem(j, 2)
     for i in range(8):
@@ -193,7 +194,7 @@
 
         acc_ref[...] += dot(hid_ref[...], down_ref[slot])
 
-    @pl.when(j == LAYERS * STEPS - 1)
+    @pl.when(j == ALL - 1)
     def _():
         keep[1].wait()
         keep_h.wait()
@@ -209,7 +210,7 @@
     shape = jax.ShapeDtypeStruct
     return pl.pallas_call(
         forward_kernel,
-        grid=(LAYERS * STEPS,),
+        grid=(ALL,),
         in_specs=[resident((TOKENS, D))] + [ANY] * 5,
         out_specs=[ANY, pl.BlockSpec((1, BLOCK, TOKENS), lambda j: (layer(j), block(j), 0)), wide, wide, ANY, ANY],
         out_shape=[
@@ -230,7 +231,7 @@
             pltpu.SemaphoreType.DMA((3,)),
             *[pltpu.SemaphoreType.DMA((2, 2))] * 4,
         ],
-        compiler_params=pltpu.CompilerParams(vmem_limit_bytes=VMEM_LIMIT, collective_id=2, has_side_effects=True),
+        compiler_params=pltpu.CompilerParams(vmem_limit_bytes=VMEM_LIMIT, collective_id=1, has_side_effects=True),
         cost_estimate=cost(5, 260e6),
         name="forward",
     )(x, wg, wu, wd, m, v)
@@ -249,17 +250,13 @@
         self.d = 2 * (third - second)
 
 
-def backward_kernel(l, lags, a_in, dy_ref, wd_ref, sl_ref, q_ref, ht_ref, *refs):
-    with_da = l == 1
-    if with_da:
-        wg, wu, h_in, g_gate, g_up, g_down, sq_ref, dh_out, far_out, acc_ref, gu_ref, w_sems, *refs = refs
-        near_send, near_recv, far_send, far_recv, *refs = refs
-        weights = Weights(l, wg, wu, None, gu_ref, None, w_sems)
-    else:
-        other_ref, g_gate, g_up, g_down, f_ref, sq_ref, every_ref, f_send, f_recv, *refs = refs
-    a_ref, dgu_ref, s_ref, a2_ref, bx, by, cx, cy, ex, ey, dx, dy2, og, ou, od, *sems = refs
-    s_send, a_recv, bx_send, by_send, cx_recv, cy_recv, ex_send, ey_send, dx_recv, dy_recv, out_sem, a_sem = sems
+def backward_kernel(lags, a_in, dy_in, wd_ref, sl_ref, q_ref, ht_ref, wg, wu, h_in, *refs):
+    g_gate, g_up, g_down, f_ref, far_out, acc_ref, gu_ref, w_sems, sq_ref, every_ref, f_send, f_recv, *refs = refs
+    near_send, near_recv, far_send, far_recv, a_ref, dy_ref, dgu_ref, s_ref, a2_ref, bx, by, cx, cy, ex, ey, dx, dy2, *refs = refs
+    og, ou, od, s_send, a_recv, bx_send, by_send, cx_recv, cy_recv, ex_send, ey_send, dx_recv, dy_recv, out_sem, a_sem = refs
+    weights = Weights(1, wg, wu, None, gu_ref, None, w_sems)
     j = pl.program_id(0)
+    block = lax.rem(j, STEPS)
     (me, x, y, c), (to_core, to_x, to_y) = neighbours()
     xn, yn, cn = (1 - k for k in (x, y, c))
     others = [{"dp": lax.rem(me + k, 8)} for k in range(1, 8)]
@@ -289,23 +286,23 @@
         ]
 
     def outs(i, last):
-        o, p = lax.rem(i, 2), lax.rem(i, og.shape[0])
-        if last:
-            wide, deep = pl.ds((STEPS - 1) * BLOCK, LAST), pl.ds((STEPS - 1) * SUB, LAST_SUB)
-            srcs = og.at[p, :, pl.ds(0, LAST)], ou.at[o, :, pl.ds(0, LAST)], od.at[o, pl.ds(0, LAST_SUB)]
-        else:
-            wide, deep = pl.ds(pl.multiple_of(i * BLOCK, BLOCK), BLOCK), pl.ds(pl.multiple_of(i * SUB, SUB), SUB)
-            srcs = og.at[p], ou.at[o], od.at[o]
-        dsts = g_gate.at[:, wide], g_up.at[:, wide], g_down.at[deep]
+        o, p, l, n = lax.rem(i, 2), lax.rem(i, og.shape[0]), 1 - lax.div(i, STEPS), lax.rem(i, STEPS)
+        w = columns(last)
+        wide = pl.ds(pl.multiple_of(n * BLOCK, BLOCK), w.size)
+        deep = pl.ds(pl.multiple_of(n * SUB, SUB), LAST_SUB if last else SUB)
+        srcs = og.at[p, :, w], ou.at[o, :, w], od.at[o, pl.ds(0, deep.size)]
+        dsts = g_gate.at[l, :, wide], g_up.at[l, :, wide], g_down.at[l, deep]
         return [pltpu.make_async_copy(s, d, out_sem.at[o, n]) for n, (s, d) in enumerate(zip(srcs, dsts))]
 
     def each(i, copies, act):
-        @pl.when(i < STEPS - 1)
+        last = lax.rem(i, STEPS) == STEPS - 1
+
+        @pl.when(jnp.logical_not(last))
         def _():
             for copy in copies(i, False):
                 act(copy)
 
-        @pl.when(i == STEPS - 1)
+        @pl.when(last)
         def _():
             for copy in copies(i, True):
                 act(copy)
@@ -320,10 +317,7 @@
         each(i, pair, lambda copy: copy.wait())
         s, a, b = lax.rem(i, lags.s), lax.rem(i, lags.a), lax.rem(i, lags.b)
 
-        @pl.when(i >= lags.b)
-        def _():
-            for copy in first(i - lags.b, False):
-                copy.wait_send()
+        pl.when(i >= lags.b)(lambda: each(i - lags.b, first, lambda copy: copy.wait_send()))
 
         for t in range(2):
             bx[b, t, :PART] = total(s_ref[s, GATE, xn, t, c], a2_ref[a, GATE, xn, t]).astype(BF)
@@ -336,10 +330,7 @@
         each(i, first, lambda copy: copy.wait_recv())
         s, a, k, e = lax.rem(i, lags.s), lax.rem(i, lags.a), lax.rem(i, lags.c), lax.rem(i, lags.e)
 
-        @pl.when(i >= lags.e)
-        def _():
-            for copy in second(i - lags.e, False):
-                copy.wait_send()
+        pl.when(i >= lags.e)(lambda: each(i - lags.e, second, lambda copy: copy.wait_send()))
 
         ey[e, :PART] = total(s_ref[s, GATE, x, yn, c], a2_ref[a, GATE, x, yn], cx[k, yn, :PART]).astype(BF)
         ey[e, PART:] = total(s_ref[s, DOWN, x, yn, c, :HALF], a2_ref[a, DOWN, x, yn, :HALF], cx[k, yn, PART:]).astype(BF)
@@ -351,10 +342,7 @@
         each(i, second, lambda copy: copy.wait_recv())
         s, a, k, d, o = (lax.rem(i, n) for n in (lags.s, lags.a, lags.c, lags.d, 2))
 
-        @pl.when(i >= 1)
-        def _():
-            for copy in outs(i - 1, False):
-                copy.wait()
+        pl.when(i >= 1)(lambda: each(i - 1, outs, lambda copy: copy.wait()))
 
         gate = total(s_ref[s, GATE, x, y, c], a2_ref[a, GATE, x, y], cx[k, y, :PART], dy2[d, :PART]).astype(BF)
         up = total(s_ref[s, UP, x, y, c], a2_ref[a, UP, x, y], cy[k, x, :PART], dx[d, :PART]).astype(BF)
@@ -368,13 +356,15 @@
             wide = t.astype(F32)
             return jnp.sum((wide * wide).reshape(-1, 8, t.shape[-1]), 0)
 
-        @pl.when(i < STEPS - 1)
+        last = lax.rem(i, STEPS) == STEPS - 1
+
+        @pl.when(jnp.logical_not(last))
         def _():
             for n, one in enumerate(downs):
                 od[o, :, BLOCK * n : BLOCK * n + BLOCK] = one
             sq_ref[...] += squares(gate) + squares(up) + squares(low) + squares(high)
 
-        @pl.when(i == STEPS - 1)
+        @pl.when(last)
         def _():
             for n, one in enumerate(downs):
                 od[o, :LAST_SUB, BLOCK * n : BLOCK * n + LAST] = one[:LAST_SUB, :LAST]
@@ -408,28 +398,44 @@
         for copy in far(t):
             copy.start()
 
-    take_a = pltpu.make_async_copy(a_in.at[l], a_ref, a_sem.at[0])
-
+    take_a1, take_a0 = (pltpu.make_async_copy(a_in.at[l], a_ref, a_sem.at[l]) for l in (1, 0))
+    take_h = pltpu.make_async_copy(h_in, a_ref, a_sem.at[2])
+    take_dy = pltpu.make_async_copy(dy_in, dy_ref, a_sem.at[3])
     barrier = pltpu.get_barrier_semaphore()
-    greeted = (to_core, to_x, to_y) if with_da else others
 
     @pl.when(j == 0)
     def _():
-        take_a.start()
-        for to in greeted:
+        take_dy.start()
+        take_a1.start()
+        weights.start(j)
+        for to in others:
             pl.semaphore_signal(barrier, inc=1, device_id=to, device_id_type=MESH)
         sq_ref[...] = jnp.zeros_like(sq_ref)
-        if with_da:
-            weights.start(j)
-
-            @pl.loop(0, TOKENS // 256)
-            def _(i):
-                acc_ref[pl.ds(pl.multiple_of(i * 256, 256), 256), :] = jnp.zeros((256, D), F32)
-
-    @pl.when(j < STEPS)
-    def _():
-        if with_da:
-            pl.when(j + 1 < STEPS)(lambda: weights.start(j + 1))
+
+        @pl.loop(0, TOKENS // 256)
+        def _(i):
+            acc_ref[pl.ds(pl.multiple_of(i * 256, 256), 256), :] = jnp.zeros((256, D), F32)
+
+        take_dy.wait()
+
+    @pl.when(j == STEPS)
+    def _():
+        take_h.wait()
+
+        @pl.loop(0, TOKENS // 128)
+        def _(i):
+            r = pl.ds(pl.multiple_of(i * 128, 128), 128)
+            h = a_ref[r, :].astype(F32)
+            da = acc_ref[r, :].astype(BF).astype(F32)
+            scale = lax.rsqrt(jnp.mean(h * h, -1, keepdims=True) + 1e-6)
+            along = jnp.sum(da * h, -1, keepdims=True) * (scale * scale * scale) * (1.0 / D)
+            dy_ref[r, :] = dy_ref[r, :] + (da * scale - h * along).astype(BF)
+
+        take_a0.start()
+
+    @pl.when(j < ALL)
+    def _():
+        pl.when(j + 1 < STEPS)(lambda: weights.start(j + 1))
         s = lax.rem(j, lags.s)
         for i in range(4):
             r = slice(512 * i, 512 * i + 512)
@@ -437,9 +443,10 @@
             dgu_ref[r, :BLOCK] = (dh * q_ref[0, r, :]).astype(BF)
             dgu_ref[r, BLOCK:] = (dh * sl_ref[0, r, :]).astype(BF)
 
-        pl.when(j == 0)(lambda: take_a.wait())
-
-        @pl.when(j == STEPS - 1)
+        pl.when(j == 0)(lambda: take_a1.wait())
+        pl.when(j == STEPS)(lambda: take_a0.wait())
+
+        @pl.when(block == STEPS - 1)
         def _():
             dgu_ref[:, LAST:BLOCK] = jnp.zeros((TOKENS, BLOCK - LAST), BF)
             dgu_ref[:, BLOCK + LAST :] = jnp.zeros((TOKENS, BLOCK - LAST), BF)
@@ -449,7 +456,8 @@
             for o in range(4):
                 for t in range(2):
                     s_ref[s, t, h, o // 2, o % 2] = gu[PART * o : PART * o + PART, BLOCK * t : BLOCK * t + BLOCK].astype(BF)
-        pl.when(j == 0)(lambda: pl.semaphore_wait(barrier, len(greeted)))
+        pl.when(j == STEPS - 1)(lambda: take_h.start())
+        pl.when(j == 0)(lambda: pl.semaphore_wait(barrier, len(others)))
         each(j, functools.partial(pair, which=(0,)), start)
         for h in range(2):
             down = dot(ht_ref[...].reshape(BLOCK, TOKENS), dy_ref[:, D // 2 * h : D // 2 * (h + 1)])
@@ -459,7 +467,7 @@
                         SUB * o : SUB * o + SUB, BLOCK * n : BLOCK * n + BLOCK
                     ].astype(BF)
 
-        @pl.when(j == STEPS - 1)
+        @pl.when(block == STEPS - 1)
         def _():
             for o in range(8):
                 for n in range(6):
@@ -469,119 +477,99 @@
                     ]
 
         each(j, functools.partial(pair, which=(1,)), start)
-        if with_da:
+
+        @pl.when(j < STEPS)
+        def _():
             weights.wait(j)
-            for i in range(4):
-                r = slice(512 * i, 512 * i + 512)
+            for i in range(8):
+                r = slice(256 * i, 256 * i + 256)
                 acc_ref[r, :] += dot(dgu_ref[r, :], gu_ref[lax.rem(j, 2)], "nt")
 
-    if with_da:
-        take_h = pltpu.make_async_copy(h_in, a_ref, a_sem.at[1])
-        give_dh = pltpu.make_async_copy(a_ref, dh_out, a_sem.at[2])
-        pl.when(j == STEPS - 1)(lambda: take_h.start())
-
-        @pl.when(j == STEPS)
-        def _():
-            take_h.wait()
-
-            @pl.loop(0, TOKENS // 128)
-            def _(i):
-                r = pl.ds(pl.multiple_of(i * 128, 128), 128)
-                h = a_ref[r, :].astype(F32)
-                da = acc_ref[r, :].astype(BF).astype(F32)
-                scale = lax.rsqrt(jnp.mean(h * h, -1, keepdims=True) + 1e-6)
-                along = jnp.sum(da * h, -1, keepdims=True) * (scale * scale * scale) * (1.0 / D)
-                a_ref[r, :] = dy_ref[r, :] + (da * scale - h * along).astype(BF)
-
-            give_dh.start()
-
-    pl.when((j >= lags.third) & (j < STEPS + lags.third))(lambda: take_third(j - lags.third))
-    pl.when((j >= lags.second) & (j < STEPS + lags.second))(lambda: take_second(j - lags.second))
-    pl.when(j < STEPS)(lambda: take_first(j))
-    if with_da:
-        soonest = lags.third
-        at_step(j - soonest - 4, lambda t: [copy.wait() for copy in far(t)])
-        at_step(j - soonest - 2, pass_on)
-        at_step(j - soonest, lambda t: [copy.start() for copy in near(t)])
-
-    @pl.when(j == STEPS + lags.third - 1)
-    def _():
-        if not with_da:
-            both = sq_ref[...] + other_ref[...]
-            every_ref[me] = both[:, :128] + both[:, 128:]
-            for n, to in enumerate(others):
-                remote(every_ref.at[me], every_ref.at[me], f_send.at[n], f_recv.at[n], to).start()
-        for i in range(STEPS - lags.b, STEPS):
-            for copy in first(jnp.int32(i), i == STEPS - 1):
+    pl.when((j >= lags.third) & (j < ALL + lags.third))(lambda: take_third(j - lags.third))
+    pl.when((j >= lags.second) & (j < ALL + lags.second))(lambda: take_second(j - lags.second))
+    pl.when(j < ALL)(lambda: take_first(j))
+    at_step(j - lags.third - 4, lambda t: [copy.wait() for copy in far(t)])
+    at_step(j - lags.third - 2, pass_on)
+    at_step(j - lags.third, lambda t: [copy.start() for copy in near(t)])
+
+    @pl.when(j == ALL + lags.third - 1)
+    def _():
+        both = sq_ref[...]
+        every_ref[me] = both[:, :128] + both[:, 128:]
+
+        def exchange():
+            return [remote(every_ref.at[me], every_ref.at[me], f_send.at[n], f_recv.at[n], to) for n, to in enumerate(others)]
+
+        for copy in exchange():
+            copy.start()
+        for i in range(ALL - lags.b, ALL):
+            for copy in first(jnp.int32(i), i == ALL - 1):
                 copy.wait_send()
-        for i in range(STEPS - lags.e, STEPS):
-            for copy in second(jnp.int32(i), i == STEPS - 1):
+        for i in range(ALL - lags.e, ALL):
+            for copy in second(jnp.int32(i), i == ALL - 1):
                 copy.wait_send()
-        for copy in outs(jnp.int32(STEPS - 1), True):
+        for copy in outs(jnp.int32(ALL - 1), True):
             copy.wait()
-        if with_da:
-            give_dh.wait()
-        else:
-            for n, to in enumerate(others):
-                remote(every_ref.at[me], every_ref.at[me], f_send.at[n], f_recv.at[n], to).wait()
-            squares = functools.reduce(lambda p, q: p + q, [every_ref[n] for n in range(8)])
-            squares = jnp.sum(jnp.sum(squares, axis=1, keepdims=True), axis=0, keepdims=True)
-            f_ref[...] = jnp.broadcast_to(jnp.minimum(1.0, 0.5 * lax.rsqrt(squares / COUNT + 1e-30)), FACTOR)
-
-
-def backward(l, lags, a, dy, wd, sl, q, ht, *more):
-    with_da = l == 1
-    at = lambda j: jnp.minimum(j, STEPS - 1)
-    wide = pl.BlockSpec((1, TOKENS, BLOCK), lambda j: (l, 0, at(j)))
-    sums = pl.BlockSpec((8, BLOCK), lambda j: (0, 0))
-    in_specs = [
-        ANY,
-        resident((TOKENS, D)),
-        pl.BlockSpec((1, BLOCK, D), lambda j: (l, at(j), 0)),
-        wide,
-        wide,
-        pl.BlockSpec((8, SUB, TOKENS), lambda j: (l, at(j), 0)),
-    ]
-    args = [a, dy, wd, sl, q, ht.reshape(LAYERS * 8, OWN_DOWN, TOKENS), *more]
-    out_shape = [jax.ShapeDtypeStruct((PART, FF), BF)] * 2 + [jax.ShapeDtypeStruct((OWN_DOWN, D), BF)]
-    if with_da:
-        in_specs += [ANY] * 3
-        out_shape += [jax.ShapeDtypeStruct(*t) for t in (((8, BLOCK), F32), ((TOKENS, D), BF), ((3, TILES) + (PART, BLOCK), BF))]
-        out_specs = [ANY] * 3 + [sums, ANY, ANY]
-        scratch = [pltpu.VMEM((TOKENS, D), F32), pltpu.VMEM((2, D, 2 * BLOCK), BF), pltpu.SemaphoreType.DMA((2, 3))]
-        scratch += [pltpu.SemaphoreType.DMA((4, 2))] * 4
-    else:
-        in_specs += [sums]
-        out_shape += [jax.ShapeDtypeStruct(FACTOR, F32)]
-        out_specs = [ANY] * 3 + [FIRST]
-        scratch = [pltpu.VMEM((8, BLOCK), F32), pltpu.VMEM((8, 8, 128), F32), *[pltpu.SemaphoreType.DMA((7,))] * 2]
+        for copy in exchange():
+            copy.wait()
+        squares = functools.reduce(lambda p, q: p + q, [every_ref[n] for n in range(8)])
+        squares = jnp.sum(jnp.sum(squares, axis=1, keepdims=True), axis=0, keepdims=True)
+        f_ref[...] = jnp.broadcast_to(jnp.minimum(1.0, 0.5 * lax.rsqrt(squares / COUNT + 1e-30)), FACTOR)
+
+
+def backward(lags, a, dy, wd, sl, q, ht, wg, wu, h):
+    layer = lambda j: 1 - lax.div(jnp.minimum(j, ALL - 1), STEPS)
+    block = lambda j: lax.rem(jnp.minimum(j, ALL - 1), STEPS)
+    wide = pl.BlockSpec((1, TOKENS, BLOCK), lambda j: (layer(j), 0, block(j)))
+    shape = jax.ShapeDtypeStruct
     piece = (PART, BLOCK)
-    scratch += [
-        pltpu.VMEM((TOKENS, D), BF),
-        pltpu.VMEM((TOKENS, 2 * BLOCK), BF),
-        pltpu.VMEM((lags.s, 3, 2, 2, 2) + piece, BF),
-        pltpu.VMEM((lags.a, 3, 2, 2) + piece, BF),
-        *[pltpu.VMEM((lags.b, 2, CHUNK, BLOCK), BF)] * 2,
-        *[pltpu.VMEM((lags.c, 2, CHUNK, BLOCK), BF)] * 2,
-        *[pltpu.VMEM((lags.e, CHUNK, BLOCK), BF)] * 2,
-        *[pltpu.VMEM((lags.d, CHUNK, BLOCK), BF)] * 2,
-        pltpu.VMEM((6 if with_da else 2,) + piece, BF),
-        pltpu.VMEM((2,) + piece, BF),
-        pltpu.VMEM((2, SUB, D), BF),
-    ]
-    scratch += [pltpu.SemaphoreType.DMA((n, 2)) for n in (lags.s, lags.a)]
-    scratch += [pltpu.SemaphoreType.DMA((n,)) for n in (lags.b, lags.b, lags.c, lags.c, lags.e, lags.e, lags.d, lags.d)]
-    scratch += [pltpu.SemaphoreType.DMA((2, 3)), pltpu.SemaphoreType.DMA((3,))]
+    dma = pltpu.SemaphoreType.DMA
     return pl.pallas_call(
-        functools.partial(backward_kernel, l, lags),
-        grid=(STEPS + lags.third,),
-        in_specs=in_specs,
-        out_specs=out_specs,
-        out_shape=out_shape,
-        scratch_shapes=scratch,
-        compiler_params=pltpu.CompilerParams(vmem_limit_bytes=VMEM_LIMIT, collective_id=l, has_side_effects=True),
-        cost_estimate=cost(6 if with_da else 4, 150e6),
-    )(*args)
+        functools.partial(backward_kernel, lags),
+        grid=(ALL + lags.third,),
+        in_specs=[
+            ANY,
+            ANY,
+            pl.BlockSpec((1, BLOCK, D), lambda j: (layer(j), block(j), 0)),
+            wide,
+            wide,
+            pl.BlockSpec((8, SUB, TOKENS), lambda j: (layer(j), block(j), 0)),
+            ANY,
+            ANY,
+            ANY,
+        ],
+        out_specs=[ANY, ANY, ANY, FIRST, ANY],
+        out_shape=[
+            *[shape((LAYERS, PART, FF), BF)] * 2,
+            shape((LAYERS, OWN_DOWN, D), BF),
+            shape(FACTOR, F32),
+            shape((3, TILES, *piece), BF),
+        ],
+        scratch_shapes=[
+            pltpu.VMEM((TOKENS, D), F32),
+            pltpu.VMEM((2, D, 2 * BLOCK), BF),
+            dma((2, 3)),
+            pltpu.VMEM((8, BLOCK), F32),
+            pltpu.VMEM((8, *FACTOR), F32),
+            *[dma((7,))] * 2,
+            *[dma((4, 2))] * 4,
+            *[pltpu.VMEM((TOKENS, D), BF)] * 2,
+            pltpu.VMEM((TOKENS, 2 * BLOCK), BF),
+            pltpu.VMEM((lags.s, 3, 2, 2, 2, *piece), BF),
+            pltpu.VMEM((lags.a, 3, 2, 2, *piece), BF),
+            *[pltpu.VMEM((n, 2, CHUNK, BLOCK), BF) for n in (lags.b, lags.b, lags.c, lags.c)],
+            *[pltpu.VMEM((n, CHUNK, BLOCK), BF) for n in (lags.e, lags.e, lags.d, lags.d)],
+            *[pltpu.VMEM((n, *piece), BF) for n in (5, 2)],
+            pltpu.VMEM((2, SUB, D), BF),
+            *[dma((n, 2)) for n in (lags.s, lags.a)],
+            *[dma((n,)) for n in (lags.b, lags.b, lags.c, lags.c, lags.e, lags.e, lags.d, lags.d)],
+            dma((2, 3)),
+            dma((4,)),
+        ],
+        compiler_params=pltpu.CompilerParams(vmem_limit_bytes=VMEM_LIMIT, collective_id=0, has_side_effects=True),
+        cost_estimate=cost(10, 300e6),
+        name="backward",
+    )(a, dy, wd, sl, q, ht.reshape(LAYERS * 8, OWN_DOWN, TOKENS), wg, wu, h)
 
 
 def stepped(factor, g, w, m, v):
@@ -611,11 +599,11 @@
 
 def adamw(piece, at, factor, g, w, m, v, so_far=None):
     _, l, axis, skip, count = piece
-    block = thirds(g.shape, axis)
+    block = thirds(g.shape[1:], axis)
     moment = pl.BlockSpec((1, *block), lambda i, at: (l, *spot(axis, skip + i)))
     in_specs = [
         FIRST,
-        pl.BlockSpec(block, lambda i, at: spot(axis, skip + i)),
+        pl.BlockSpec((SQUEEZED, *block), lambda i, at: (l, *spot(axis, skip + i))),
         pl.BlockSpec((1, *block), lambda i, at: (l, 3 * at[0] + skip + i, 0) if axis == 0 else (l, at[0], skip + i)),
         moment,
         moment,
@@ -750,8 +738,7 @@
         x, dy = x[0], dy[0]
         me = lax.axis_index("dp")
         a, ht, sl, q, h1, mv = forward(x, wg, wu, wd, mg, vg)
-        *g1, squares, dh1, g_ahead = backward(1, Lags(1, 2, 2, 2), a, dy, wd, sl, q, ht, wg, wu, h1)
-        *g0, factor = backward(0, Lags(2, 4, 3, 3), a, dh1, wd, sl, q, ht, squares)
+        *gradients, factor, g_ahead = backward(Lags(2, 3, 2, 2), a, dy, wd, sl, q, ht, wg, wu, h1)
         at = me[None].astype(jnp.int32)
         groups = {name: jnp.stack([me ^ k for k in group]).astype(jnp.int32) for name, group in GROUPS.items()}
         mats = ((wg, mg, vg), (wu, mu, vu), (wd, md, vd))
@@ -762,8 +749,8 @@
             whole[n] = place(piece, groups[kind], [have[k] for k in GROUPS[kind]], whole[n], mats[n][0])
 
         def new_rows(piece):
-            n, l = piece[:2]
-            new, *moments[n] = adamw(piece, at, factor, (g0, g1)[l][n], *mats[n], moments[n])
+            n = piece[0]
+            new, *moments[n] = adamw(piece, at, factor, gradients[n], *mats[n], moments[n])
             return new
 
         everything = []

time: 1010 us -> 995 us (0.985)
  Pallas kernels: 771 us -> 755 us
    pallas_call x3 -> x2, Pallas kernels: 575 us -> 557 us  [the longest x1 388 us: backward(): pl.pallas_call(functools.partial(backward_kernel, lags), grid=(ALL + lags...]
    unnamed x182 -> x172, local copies, waits for them, and re-layouts: 20.2 us -> 25.6 us
where the time goes in v4:
time: 995 us; the launch traced here: 992 us
  Pallas kernels  755 us (76%)
  waiting for transfers between devices  172 us (17%)
  starting transfers between devices  38.7 us (4%)
  local copies, waits for them, and re-layouts  25.6 us (3%)
    pallas_call x1, Pallas kernels, backward(): pl.pallas_call(functools.partial(backward_kernel, lags), grid=(ALL + lags...  388 us
    ppermute x72, waiting for transfers between devices, swap(): return lax.ppermute(t, 'dp', [(i, i ^ mask) for i in range(8)])  172 us
    pallas_call x1, Pallas kernels, forward(): pl.pallas_call(forward_kernel, grid=(ALL,), in_specs=[resident((TOKENS, D...  169 us
    pallas_call x41, Pallas kernels, place(): pl.pallas_call(functools.partial(place_kernel, n), grid_spec=pltpu.Prefet...  99.4 us
    pallas_call x11, Pallas kernels, adamw(): pl.pallas_call(adamw_kernel, grid_spec=pltpu.PrefetchScalarGridSpec(num_s...  59.4 us
    ppermute x72, starting transfers between devices, swap(): return lax.ppermute(t, 'dp', [(i, i ^ mask) for i in range(8)])  38.7 us
    pallas_call x1, Pallas kernels, adamw_ahead(): pl.pallas_call(adamw_ahead_kernel, grid_spec=pltpu.PrefetchScalarGridSpec...  26.5 us
    unnamed x172, local copies, waits for them, and re-layouts  25.6 us
  transfers between devices with their start and end apart: 72, of which 19 were waited for; matrix products, arithmetic and copies ran while one was open for 0% of the time, Pallas kernels for 18%

profile of v4, /device:TPU:0, one launch (start us, length us, event | category | flops | bytes accessed | tf_op | source)
XLA Modules:
  0.0 992.2 jit_solution(14412601419162761658)
XLA Ops:
  0.6 169.3 %forward.1 = (bf16[2,2048,1536]{2,1,0:T(8,128)(2,1)}, bf16[2,4224,2048]{2,1,0:T(8,128)(2,1)}, f32[2,2048,4224]{2,1,0:T(8,128)}, f32[2,2048,4224]{2,1,0:T(8,128)}...) custom-call(bf16[2048,1536]{1,0:T(8,128)(2,1)} %bitcast.11, bf16[2,1536,4224]{2,1,0:T(8,128)(2,1)} %w_ref.17, ...), custom_call_target="tpu_custom_call" | custom-call | flops 132875550720 | bytes 260000000 | tf_op jit(solution)/shard_map/forward/pallas_call | solution.py:211
  169.9 388.0 %backward.1 = (bf16[2,192,4224]{2,1,0:T(8,128)(2,1)}, bf16[2,192,4224]{2,1,0:T(8,128)(2,1)}, bf16[2,528,1536]{2,1,0:T(8,128)(2,1)}, f32[8,128]{1,0:T(8,128)}, bf16[3,11,192,256]{3,2,1,0:T(8,128)(2,1)}) custom-call(bf16[2,2048,1536]{2,1,0:T(8,128)(2,1)} %get-tuple-element.53.a_in, bf16[2048,1536]{1,0:T(8,128)(2,1)} %bitcast.12, ...), custom_call_target="tpu_custom_call" | custom-call | flops 265751101440 | bytes 300000000 | tf_op jit(solution)/shard_map/backward/pallas_call | solution.py:527
  560.6 5.2 shard_map.210
  565.8 5.8 shard_map.211
  571.7 4.1 shard_map.212
  578.0 4.2 shard_map.213
  583.0 4.2 shard_map.178
  588.4 2.7 collective-permute-done.60.refs_0_
  593.9 4.2 shard_map.179
  598.1 4.6 collective-permute-done.44.refs_0_
  606.3 4.2 shard_map.180
  610.5 4.4 collective-permute-done.9.refs_1_
  616.3 4.3 shard_map.181
  621.6 4.3 collective-permute-done.6.refs_0_
  628.8 8.5 collective-permute-done.18.refs_0_
  642.1 6.9 collective-permute-done.refs_0_
  649.8 2.7 collective-permute-done.14.refs_1_
  655.6 20.2 %collective-permute-done.53.refs_1_ = bf16[352,1536]{1,0:T(8,128)(2,1)} collective-permute-done((bf16[352,1536]{1,0:T(8,128)(2,1)S(1)}, bf16[352,1536]{1,0:T(8,128)(2,1)}, u32[]{:S(2)}, u32[]{:S(2)}) %collective-permute-start.53) | collective-permute-done | bytes 1081376 | tf_op jit(solution)/shard_map/ppermute | solution.py:735
  677.4 17.3 %collective-permute-done.50.refs_0_ = bf16[352,1536]{1,0:T(8,128)(2,1)S(1)} collective-permute-done((bf16[352,1536]{1,0:T(8,128)(2,1)}, bf16[352,1536]{1,0:T(8,128)(2,1)S(1)}, u32[]{:S(2)}, u32[]{:S(2)}) %collective-permute-start.50) | collective-permute-done | bytes 1081376 | tf_op jit(solution)/shard_map/ppermute | solution.py:735
  695.7 8.8 shard_map.200
  706.9 1.9 copy-done.3
  708.8 8.7 shard_map.201
  717.5 5.7 shard_map.182
  726.0 26.5 %adamw_ahead.1.new_ref = bf16[3,192,2816]{2,1,0:T(8,128)(2,1)} custom-call(s32[3]{0:T(128)S(1)} %pad_add_fusion.1.owners_ref, f32[8,128]{1,0:T(8,128)S(1)} %copy-done.19, bf16[3,11,192,256]{3,2,1,0:T(8,128)(2,1)} %get-tuple-element.70.g_ref, bf16[2,1536,4224]{2,1,0:T(8,128)(2,1)} %w_ref.17, f32[2,3,192,2816]{3,2,1,0:T(8,128)} %get-tuple-element.71.m_ref.v_ref, ...), custom_call_target="tpu_custom_call" | custom-call | flops 2657510912 | bytes 22708224 | tf_op jit(solution)/shard_map/adamw_ahead/pallas_call | solution.py:644
  760.0 3.5 shard_map.184.refs_2_
  767.1 2.6 collective-permute-done.10.refs_0_
  771.0 3.5 shard_map.186.refs_2_
  777.2 30.8 %collective-permute-done.7.refs_0_ = bf16[192,1408]{1,0:T(8,128)(2,1)S(1)} collective-permute-done((bf16[192,1408]{1,0:T(8,128)(2,1)}, bf16[192,1408]{1,0:T(8,128)(2,1)S(1)}, u32[]{:S(2)}, u32[]{:S(2)}) %collective-permute-start.7) | collective-permute-done | bytes 540704 | tf_op jit(solution)/shard_map/ppermute | solution.py:735
  811.3 2.4 shard_map.188.refs_2_
  818.0 2.4 shard_map.190.refs_2_
  820.6 2.7 shard_map.191.so_far
  823.3 6.0 place_ahead.2.so_far
  830.5 2.4 shard_map.214.refs_4_
  832.9 3.3 shard_map.202.refs_4_
  837.6 7.9 shard_map.215.refs_2_
  846.2 3.5 shard_map.216.refs_4_
  849.7 7.9 shard_map.217.refs_2_
  859.2 4.0 shard_map.219.refs_2_
  866.2 4.0 shard_map.221.refs_1_
  870.2 2.2 shard_map.222.refs_1_
  872.4 18.4 %collective-permute-done.30.refs_0_ = bf16[192,4224]{1,0:T(8,128)(2,1)S(1)} collective-permute-done((bf16[192,4224]{1,0:T(8,128)(2,1)S(1)}, bf16[192,4224]{1,0:T(8,128)(2,1)S(1)}, u32[]{:S(2)}, u32[]{:S(2)}) %collective-permute-start.30) | collective-permute-done | bytes 1622048 | tf_op jit(solution)/shard_map/ppermute | solution.py:735
  895.5 5.6 collective-permute-done.36.refs_1_
  901.6 5.9 place_ahead.3.refs_1_
  912.9 7.8 shard_map.203.refs_2_
  920.7 3.3 shard_map.204.refs_4_
  924.8 31.7 %collective-permute-done.4.refs_0_ = bf16[192,1408]{1,0:T(8,128)(2,1)S(1)} collective-permute-done((bf16[192,1408]{1,0:T(8,128)(2,1)S(1)}, bf16[192,1408]{1,0:T(8,128)(2,1)S(1)}, u32[]{:S(2)}, u32[]{:S(2)}) %collective-permute-start.4) | collective-permute-done | bytes 540704 | tf_op jit(solution)/shard_map/ppermute | solution.py:735
  959.4 9.5 shard_map.205.refs_1_
  972.7 8.9 collective-permute-done.1.refs_0_
  (329 shorter events, 94.4 us)
Async XLA Ops:
  582.2 20.5 %collective-permute-start.44 = (bf16[176,1536]{1,0:T(8,128)(2,1)S(1)}, bf16[176,1536]{1,0:T(8,128)(2,1)}, u32[]{:S(2)}, u32[]{:S(2)}) collective-permute-start(bf16[176,1536]{1,0:T(8,128)(2,1)S(1)} %get-tuple-element.87.refs_0_), channel_id=1, source_target_pairs={{0,4},{1,5},{2,6},{3,7},{4,0},{5,1},{6,2},{7,3}} | collective-permute-start | bytes 1622024 | tf_op jit(solution)/shard_map/ppermute | solution.py:735
  591.8 23.1 %collective-permute-start.9 = (bf16[192,1408]{1,0:T(8,128)(2,1)S(1)}, bf16[192,1408]{1,0:T(8,128)(2,1)S(1)}, u32[]{:S(2)}, u32[]{:S(2)}) collective-permute-start(bf16[192,1408]{1,0:T(8,128)(2,1)S(1)} %get-tuple-element.69.refs_0_), channel_id=1, source_target_pairs={{0,2},{1,3},{2,0},{3,1},{4,6},{5,7},{6,4},{7,5}} | collective-permute-start | bytes 1622024 | tf_op jit(solution)/shard_map/ppermute | solution.py:735
  593.2 21.7 %collective-permute-start.26 = (bf16[192,1408]{1,0:T(8,128)(2,1)S(1)}, bf16[192,1408]{1,0:T(8,128)(2,1)}, u32[]{:S(2)}, u32[]{:S(2)}) collective-permute-start(bf16[192,1408]{1,0:T(8,128)(2,1)S(1)} %get-tuple-element.69.refs_0_), channel_id=1, source_target_pairs={{0,4},{1,5},{2,6},{3,7},{4,0},{5,1},{6,2},{7,3}} | collective-permute-start | bytes 1622024 | tf_op jit(solution)/shard_map/ppermute | solution.py:735
  603.4 22.5 %collective-permute-start.6 = (bf16[192,1408]{1,0:T(8,128)(2,1)S(1)}, bf16[192,1408]{1,0:T(8,128)(2,1)}, u32[]{:S(2)}, u32[]{:S(2)}) collective-permute-start(bf16[192,1408]{1,0:T(8,128)(2,1)S(1)} %get-tuple-element.68.refs_0_), channel_id=1, source_target_pairs={{0,4},{1,5},{2,6},{3,7},{4,0},{5,1},{6,2},{7,3}} | collective-permute-start | bytes 1622024 | tf_op jit(solution)/shard_map/ppermute | solution.py:735
  605.5 21.1 %collective-permute-start.22 = (bf16[192,1408]{1,0:T(8,128)(2,1)S(1)}, bf16[192,1408]{1,0:T(8,128)(2,1)S(1)}, u32[]{:S(2)}, u32[]{:S(2)}) collective-permute-start(bf16[192,1408]{1,0:T(8,128)(2,1)S(1)} %get-tuple-element.68.refs_0_), channel_id=1, source_target_pairs={{0,2},{1,3},{2,0},{3,1},{4,6},{5,7},{6,4},{7,5}} | collective-permute-start | bytes 1622024 | tf_op jit(solution)/shard_map/ppermute | solution.py:735
  614.9 22.5 %collective-permute-start.18 = (bf16[192,1408]{1,0:T(8,128)(2,1)S(1)}, bf16[192,1408]{1,0:T(8,128)(2,1)S(1)}, u32[]{:S(2)}, u32[]{:S(2)}) collective-permute-start(bf16[192,1408]{1,0:T(8,128)(2,1)S(1)} %get-tuple-element.67.refs_0_), channel_id=1, source_target_pairs={{0,4},{1,5},{2,6},{3,7},{4,0},{5,1},{6,2},{7,3}} | collective-permute-start | bytes 1622024 | tf_op jit(solution)/shard_map/ppermute | solution.py:735
  621.4 31.8 %collective-permute-start.71 = (bf16[352,1536]{1,0:T(8,128)(2,1)S(1)}, bf16[352,1536]{1,0:T(8,128)(2,1)S(1)}, u32[]{:S(2)}, u32[]{:S(2)}) collective-permute-start(bf16[352,1536]{1,0:T(8,128)(2,1)S(1)} %get-tuple-element.90.refs_0_), channel_id=1, source_target_pairs={{0,1},{1,0},{2,3},{3,2},{4,5},{5,4},{6,7},{7,6}} | collective-permute-start | bytes 3244040 | tf_op jit(solution)/shard_map/ppermute | solution.py:735
  627.5 21.4 %collective-permute-start = (bf16[192,1408]{1,0:T(8,128)(2,1)S(1)}, bf16[192,1408]{1,0:T(8,128)(2,1)S(1)}, u32[]{:S(2)}, u32[]{:S(2)}) collective-permute-start(bf16[192,1408]{1,0:T(8,128)(2,1)S(1)} %get-tuple-element.66.refs_0_), channel_id=1, source_target_pairs={{0,4},{1,5},{2,6},{3,7},{4,0},{5,1},{6,2},{7,3}} | collective-permute-start | bytes 1622024 | tf_op jit(solution)/shard_map/ppermute | solution.py:735
  639.1 36.7 %collective-permute-start.53 = (bf16[352,1536]{1,0:T(8,128)(2,1)S(1)}, bf16[352,1536]{1,0:T(8,128)(2,1)}, u32[]{:S(2)}, u32[]{:S(2)}) collective-permute-start(bf16[352,1536]{1,0:T(8,128)(2,1)S(1)} %get-tuple-element.90.refs_0_), channel_id=1, source_target_pairs={{0,2},{1,3},{2,0},{3,1},{4,6},{5,7},{6,4},{7,5}} | collective-permute-start | bytes 3244040 | tf_op jit(solution)/shard_map/ppermute | solution.py:735
  641.0 34.8 %collective-permute-start.68 = (bf16[352,1536]{1,0:T(8,128)(2,1)S(1)}, bf16[352,1536]{1,0:T(8,128)(2,1)S(1)}, u32[]{:S(2)}, u32[]{:S(2)}) collective-permute-start(bf16[352,1536]{1,0:T(8,128)(2,1)S(1)} %get-tuple-element.90.refs_0_), channel_id=1, source_target_pairs={{0,4},{1,5},{2,6},{3,7},{4,0},{5,1},{6,2},{7,3}} | collective-permute-start | bytes 3244040 | tf_op jit(solution)/shard_map/ppermute | solution.py:735
  649.8 26.5 %collective-permute-start.67 = (bf16[352,1536]{1,0:T(8,128)(2,1)}, bf16[352,1536]{1,0:T(8,128)(2,1)S(1)}, u32[]{:S(2)}, u32[]{:S(2)}) collective-permute-start(bf16[352,1536]{1,0:T(8,128)(2,1)} %get-tuple-element.89.refs_0_), channel_id=1, source_target_pairs={{0,1},{1,0},{2,3},{3,2},{4,5},{5,4},{6,7},{7,6}} | collective-permute-start | bytes 3244040 | tf_op jit(solution)/shard_map/ppermute | solution.py:735
  652.5 42.2 %collective-permute-start.50 = (bf16[352,1536]{1,0:T(8,128)(2,1)}, bf16[352,1536]{1,0:T(8,128)(2,1)S(1)}, u32[]{:S(2)}, u32[]{:S(2)}) collective-permute-start(bf16[352,1536]{1,0:T(8,128)(2,1)} %get-tuple-element.89.refs_0_), channel_id=1, source_target_pairs={{0,4},{1,5},{2,6},{3,7},{4,0},{5,1},{6,2},{7,3}} | collective-permute-start | bytes 3244040 | tf_op jit(solution)/shard_map/ppermute | solution.py:735
  654.2 51.4 %collective-permute-start.64 = (bf16[352,1536]{1,0:T(8,128)(2,1)}, bf16[352,1536]{1,0:T(8,128)(2,1)}, u32[]{:S(2)}, u32[]{:S(2)}) collective-permute-start(bf16[352,1536]{1,0:T(8,128)(2,1)} %get-tuple-element.89.refs_0_), channel_id=1, source_target_pairs={{0,2},{1,3},{2,0},{3,1},{4,6},{5,7},{6,4},{7,5}} | collective-permute-start | bytes 3244040 | tf_op jit(solution)/shard_map/ppermute | solution.py:735
  675.8 30.5 %collective-permute-start.61 = (bf16[176,1536]{1,0:T(8,128)(2,1)}, bf16[176,1536]{1,0:T(8,128)(2,1)}, u32[]{:S(2)}, u32[]{:S(2)}) collective-permute-start(bf16[176,1536]{1,0:T(8,128)(2,1)} %collective-permute-done.60.refs_0_), channel_id=1, source_target_pairs={{0,1},{1,0},{2,3},{3,2},{4,5},{5,4},{6,7},{7,6}} | collective-permute-start | bytes 1622024 | tf_op jit(solution)/shard_map/ppermute | solution.py:735
  675.8 30.5 %collective-permute-start.62 = (bf16[176,1536]{1,0:T(8,128)(2,1)}, bf16[176,1536]{1,0:T(8,128)(2,1)}, u32[]{:S(2)}, u32[]{:S(2)}) collective-permute-start(bf16[176,1536]{1,0:T(8,128)(2,1)} %collective-permute-done.47.refs_1_), channel_id=1, source_target_pairs={{0,1},{1,0},{2,3},{3,2},{4,5},{5,4},{6,7},{7,6}} | collective-permute-start | bytes 1622024 | tf_op jit(solution)/shard_map/ppermute | solution.py:735
  677.4 40.1 %collective-permute-start.57 = (bf16[176,1536]{1,0:T(8,128)(2,1)}, bf16[176,1536]{1,0:T(8,128)(2,1)}, u32[]{:S(2)}, u32[]{:S(2)}) collective-permute-start(bf16[176,1536]{1,0:T(8,128)(2,1)} %collective-permute-done.44.refs_0_), channel_id=1, source_target_pairs={{0,1},{1,0},{2,3},{3,2},{4,5},{5,4},{6,7},{7,6}} | collective-permute-start | bytes 1622024 | tf_op jit(solution)/shard_map/ppermute | solution.py:735
  694.7 28.5 %collective-permute-start.58 = (bf16[176,1536]{1,0:T(8,128)(2,1)}, bf16[176,1536]{1,0:T(8,128)(2,1)}, u32[]{:S(2)}, u32[]{:S(2)}) collective-permute-start(bf16[176,1536]{1,0:T(8,128)(2,1)} %collective-permute-done.56.refs_1_), channel_id=1, source_target_pairs={{0,1},{1,0},{2,3},{3,2},{4,5},{5,4},{6,7},{7,6}} | collective-permute-start | bytes 1622024 | tf_op jit(solution)/shard_map/ppermute | solution.py:735
  706.3 18.8 %collective-permute-start.27 = (bf16[192,1408]{1,0:T(8,128)(2,1)}, bf16[192,1408]{1,0:T(8,128)(2,1)S(1)}, u32[]{:S(2)}, u32[]{:S(2)}) collective-permute-start(bf16[192,1408]{1,0:T(8,128)(2,1)} %collective-permute-done.26.refs_0_), channel_id=1, source_target_pairs={{0,1},{1,0},{2,3},{3,2},{4,5},{5,4},{6,7},{7,6}} | collective-permute-start | bytes 1622024 | tf_op jit(solution)/shard_map/ppermute | solution.py:735
  717.5 35.1 %collective-permute-start.23 = (bf16[192,1408]{1,0:T(8,128)(2,1)}, bf16[192,1408]{1,0:T(8,128)(2,1)S(1)}, u32[]{:S(2)}, u32[]{:S(2)}) collective-permute-start(bf16[192,1408]{1,0:T(8,128)(2,1)} %collective-permute-done.6.refs_0_), channel_id=1, source_target_pairs={{0,1},{1,0},{2,3},{3,2},{4,5},{5,4},{6,7},{7,6}} | collective-permute-start | bytes 1622024 | tf_op jit(solution)/shard_map/ppermute | solution.py:735
  723.2 30.8 %collective-permute-start.24 = (bf16[192,1408]{1,0:T(8,128)(2,1)S(1)}, bf16[192,1408]{1,0:T(8,128)(2,1)S(1)}, u32[]{:S(2)}, u32[]{:S(2)}) collective-permute-start(bf16[192,1408]{1,0:T(8,128)(2,1)S(1)} %copy-done.61), channel_id=1, source_target_pairs={{0,1},{1,0},{2,3},{3,2},{4,5},{5,4},{6,7},{7,6}} | collective-permute-start | bytes 1622024 | tf_op jit(solution)/shard_map/ppermute | solution.py:735
  723.8 41.7 %collective-permute-start.13 = (bf16[192,2816]{1,0:T(8,128)(2,1)S(1)}, bf16[192,2816]{1,0:T(8,128)(2,1)S(1)}, u32[]{:S(2)}, u32[]{:S(2)}) collective-permute-start(bf16[192,2816]{1,0:T(8,128)(2,1)S(1)} %get-tuple-element.74.refs_0_), channel_id=1, source_target_pairs={{0,1},{1,0},{2,3},{3,2},{4,5},{5,4},{6,7},{7,6}} | collective-permute-start | bytes 3244040 | tf_op jit(solution)/shard_map/ppermute | solution.py:735
  724.7 29.5 %collective-permute-start.19 = (bf16[192,1408]{1,0:T(8,128)(2,1)S(1)}, bf16[192,1408]{1,0:T(8,128)(2,1)S(1)}, u32[]{:S(2)}, u32[]{:S(2)}) collective-permute-start(bf16[192,1408]{1,0:T(8,128)(2,1)S(1)} %copy-done.54), channel_id=1, source_target_pairs={{0,1},{1,0},{2,3},{3,2},{4,5},{5,4},{6,7},{7,6}} | collective-permute-start | bytes 1622024 | tf_op jit(solution)/shard_map/ppermute | solution.py:735
  725.9 29.5 %collective-permute-start.20 = (bf16[192,1408]{1,0:T(8,128)(2,1)S(1)}, bf16[192,1408]{1,0:T(8,128)(2,1)S(1)}, u32[]{:S(2)}, u32[]{:S(2)}) collective-permute-start(bf16[192,1408]{1,0:T(8,128)(2,1)S(1)} %copy-done.42), channel_id=1, source_target_pairs={{0,1},{1,0},{2,3},{3,2},{4,5},{5,4},{6,7},{7,6}} | collective-permute-start | bytes 1622024 | tf_op jit(solution)/shard_map/ppermute | solution.py:735
  755.0 62.5 %collective-permute-start.43 = (bf16[192,4224]{1,0:T(8,128)(2,1)S(1)}, bf16[192,4224]{1,0:T(8,128)(2,1)S(1)}, u32[]{:S(2)}, u32[]{:S(2)}) collective-permute-start(bf16[192,4224]{1,0:T(8,128)(2,1)S(1)} %copy-done.5), channel_id=1, source_target_pairs={{0,1},{1,0},{2,3},{3,2},{4,5},{5,4},{6,7},{7,6}} | collective-permute-start | bytes 4866056 | tf_op jit(solution)/shard_map/ppermute | solution.py:735
  759.2 61.2 %collective-permute-start.33 = (bf16[192,4224]{1,0:T(8,128)(2,1)S(1)}, bf16[192,4224]{1,0:T(8,128)(2,1)S(1)}, u32[]{:S(2)}, u32[]{:S(2)}) collective-permute-start(bf16[192,4224]{1,0:T(8,128)(2,1)S(1)} %copy-done.5), channel_id=1, source_target_pairs={{0,2},{1,3},{2,0},{3,1},{4,6},{5,7},{6,4},{7,5}} | collective-permute-start | bytes 4866056 | tf_op jit(solution)/shard_map/ppermute | solution.py:735
  764.3 43.7 %collective-permute-start.7 = (bf16[192,1408]{1,0:T(8,128)(2,1)}, bf16[192,1408]{1,0:T(8,128)(2,1)S(1)}, u32[]{:S(2)}, u32[]{:S(2)}) collective-permute-start(bf16[192,1408]{1,0:T(8,128)(2,1)} %collective-permute-done.6.refs_0_), channel_id=1, source_target_pairs={{0,2},{1,3},{2,0},{3,1},{4,6},{5,7},{6,4},{7,5}} | collective-permute-start | bytes 1622024 | tf_op jit(solution)/shard_map/ppermute | solution.py:735
  765.5 43.2 %collective-permute-start.49 = (bf16[176,1536]{1,0:T(8,128)(2,1)S(1)}, bf16[176,1536]{1,0:T(8,128)(2,1)S(1)}, u32[]{:S(2)}, u32[]{:S(2)}) collective-permute-start(bf16[176,1536]{1,0:T(8,128)(2,1)S(1)} %collective-permute-done.48.refs_0_), channel_id=1, source_target_pairs={{0,1},{1,0},{2,3},{3,2},{4,5},{5,4},{6,7},{7,6}} | collective-permute-start | bytes 1622024 | tf_op jit(solution)/shard_map/ppermute | solution.py:735
  769.7 59.5 %collective-permute-start.40 = (bf16[192,4224]{1,0:T(8,128)(2,1)S(1)}, bf16[192,4224]{1,0:T(8,128)(2,1)S(1)}, u32[]{:S(2)}, u32[]{:S(2)}) collective-permute-start(bf16[192,4224]{1,0:T(8,128)(2,1)S(1)} %copy-done.5), channel_id=1, source_target_pairs={{0,4},{1,5},{2,6},{3,7},{4,0},{5,1},{6,2},{7,3}} | collective-permute-start | bytes 4866056 | tf_op jit(solution)/shard_map/ppermute | solution.py:735
  808.7 20.9 %collective-permute-start.70 = (bf16[352,1536]{1,0:T(8,128)(2,1)}, bf16[352,1536]{1,0:T(8,128)(2,1)}, u32[]{:S(2)}, u32[]{:S(2)}) collective-permute-start(bf16[352,1536]{1,0:T(8,128)(2,1)} %collective-permute-done.53.refs_1_), channel_id=1, source_target_pairs={{0,1},{1,0},{2,3},{3,2},{4,5},{5,4},{6,7},{7,6}} | collective-permute-start | bytes 3244040 | tf_op jit(solution)/shard_map/ppermute | solution.py:735
  808.7 21.0 %collective-permute-start.69 = (bf16[352,1536]{1,0:T(8,128)(2,1)S(1)}, bf16[352,1536]{1,0:T(8,128)(2,1)}, u32[]{:S(2)}, u32[]{:S(2)}) collective-permute-start(bf16[352,1536]{1,0:T(8,128)(2,1)S(1)} %copy-done.17), channel_id=1, source_target_pairs={{0,1},{1,0},{2,3},{3,2},{4,5},{5,4},{6,7},{7,6}} | collective-permute-start | bytes 3244040 | tf_op jit(solution)/shard_map/ppermute | solution.py:735
  820.4 25.1 %collective-permute-start.66 = (bf16[352,1536]{1,0:T(8,128)(2,1)}, bf16[352,1536]{1,0:T(8,128)(2,1)}, u32[]{:S(2)}, u32[]{:S(2)}) collective-permute-start(bf16[352,1536]{1,0:T(8,128)(2,1)} %collective-permute-done.64.refs_1_), channel_id=1, source_target_pairs={{0,1},{1,0},{2,3},{3,2},{4,5},{5,4},{6,7},{7,6}} | collective-permute-start | bytes 3244040 | tf_op jit(solution)/shard_map/ppermute | solution.py:735
  829.2 71.9 %collective-permute-start.12 = (bf16[3,192,2816]{2,1,0:T(8,128)(2,1)}, bf16[3,192,2816]{2,1,0:T(8,128)(2,1)}, u32[]{:S(2)}, u32[]{:S(2)}) collective-permute-start(bf16[3,192,2816]{2,1,0:T(8,128)(2,1)} %adamw_ahead.1.new_ref), channel_id=1, source_target_pairs={{0,1},{1,0},{2,3},{3,2},{4,5},{5,4},{6,7},{7,6}} | collective-permute-start | bytes 9732104 | tf_op jit(solution)/shard_map/ppermute | solution.py:735
  829.6 33.6 %collective-permute-start.39 = (bf16[192,4224]{1,0:T(8,128)(2,1)S(1)}, bf16[192,4224]{1,0:T(8,128)(2,1)S(1)}, u32[]{:S(2)}, u32[]{:S(2)}) collective-permute-start(bf16[192,4224]{1,0:T(8,128)(2,1)S(1)} %get-tuple-element.78.refs_0_), channel_id=1, source_target_pairs={{0,1},{1,0},{2,3},{3,2},{4,5},{5,4},{6,7},{7,6}} | collective-permute-start | bytes 4866056 | tf_op jit(solution)/shard_map/ppermute | solution.py:735
  829.8 27.8 %collective-permute-start.54 = (bf16[352,1536]{1,0:T(8,128)(2,1)}, bf16[352,1536]{1,0:T(8,128)(2,1)}, u32[]{:S(2)}, u32[]{:S(2)}) collective-permute-start(bf16[352,1536]{1,0:T(8,128)(2,1)} %collective-permute-done.53.refs_1_), channel_id=1, source_target_pairs={{0,4},{1,5},{2,6},{3,7},{4,0},{5,1},{6,2},{7,3}} | collective-permute-start | bytes 3244040 | tf_op jit(solution)/shard_map/ppermute | solution.py:735
  836.2 28.2 %collective-permute-start.51 = (bf16[352,1536]{1,0:T(8,128)(2,1)S(1)}, bf16[352,1536]{1,0:T(8,128)(2,1)S(1)}, u32[]{:S(2)}, u32[]{:S(2)}) collective-permute-start(bf16[352,1536]{1,0:T(8,128)(2,1)S(1)} %copy-done.15), channel_id=1, source_target_pairs={{0,2},{1,3},{2,0},{3,1},{4,6},{5,7},{6,4},{7,5}} | collective-permute-start | bytes 3244040 | tf_op jit(solution)/shard_map/ppermute | solution.py:735
  845.5 45.3 %collective-permute-start.30 = (bf16[192,4224]{1,0:T(8,128)(2,1)S(1)}, bf16[192,4224]{1,0:T(8,128)(2,1)S(1)}, u32[]{:S(2)}, u32[]{:S(2)}) collective-permute-start(bf16[192,4224]{1,0:T(8,128)(2,1)S(1)} %get-tuple-element.78.refs_0_), channel_id=1, source_target_pairs={{0,4},{1,5},{2,6},{3,7},{4,0},{5,1},{6,2},{7,3}} | collective-permute-start | bytes 4866056 | tf_op jit(solution)/shard_map/ppermute | solution.py:735
  857.6 33.2 %collective-permute-start.55 = (bf16[352,1536]{1,0:T(8,128)(2,1)}, bf16[352,1536]{1,0:T(8,128)(2,1)S(1)}, u32[]{:S(2)}, u32[]{:S(2)}) collective-permute-start(bf16[352,1536]{1,0:T(8,128)(2,1)} %collective-permute-done.54.refs_0_), channel_id=1, source_target_pairs={{0,1},{1,0},{2,3},{3,2},{4,5},{5,4},{6,7},{7,6}} | collective-permute-start | bytes 3244040 | tf_op jit(solution)/shard_map/ppermute | solution.py:735
  863.2 37.9 %collective-permute-start.36 = (bf16[192,4224]{1,0:T(8,128)(2,1)S(1)}, bf16[192,4224]{1,0:T(8,128)(2,1)}, u32[]{:S(2)}, u32[]{:S(2)}) collective-permute-start(bf16[192,4224]{1,0:T(8,128)(2,1)S(1)} %get-tuple-element.78.refs_0_), channel_id=1, source_target_pairs={{0,2},{1,3},{2,0},{3,1},{4,6},{5,7},{6,4},{7,5}} | collective-permute-start | bytes 4866056 | tf_op jit(solution)/shard_map/ppermute | solution.py:735
  864.4 28.9 %collective-permute-start.52 = (bf16[352,1536]{1,0:T(8,128)(2,1)S(1)}, bf16[352,1536]{1,0:T(8,128)(2,1)S(1)}, u32[]{:S(2)}, u32[]{:S(2)}) collective-permute-start(bf16[352,1536]{1,0:T(8,128)(2,1)S(1)} %collective-permute-done.51.refs_0_), channel_id=1, source_target_pairs={{0,1},{1,0},{2,3},{3,2},{4,5},{5,4},{6,7},{7,6}} | collective-permute-start | bytes 3244040 | tf_op jit(solution)/shard_map/ppermute | solution.py:735
  890.8 19.7 %collective-permute-start.42 = (bf16[192,4224]{1,0:T(8,128)(2,1)S(1)}, bf16[192,4224]{1,0:T(8,128)(2,1)}, u32[]{:S(2)}, u32[]{:S(2)}) collective-permute-start(bf16[192,4224]{1,0:T(8,128)(2,1)S(1)} %copy-done.7), channel_id=1, source_target_pairs={{0,1},{1,0},{2,3},{3,2},{4,5},{5,4},{6,7},{7,6}} | collective-permute-start | bytes 4866056 | tf_op jit(solution)/shard_map/ppermute | solution.py:735
  890.8 20.8 %collective-permute-start.41 = (bf16[192,4224]{1,0:T(8,128)(2,1)S(1)}, bf16[192,4224]{1,0:T(8,128)(2,1)S(1)}, u32[]{:S(2)}, u32[]{:S(2)}) collective-permute-start(bf16[192,4224]{1,0:T(8,128)(2,1)S(1)} %collective-permute-done.40.refs_0_), channel_id=1, source_target_pairs={{0,1},{1,0},{2,3},{3,2},{4,5},{5,4},{6,7},{7,6}} | collective-permute-start | bytes 4866056 | tf_op jit(solution)/shard_map/ppermute | solution.py:735
  901.1 57.5 %collective-permute-start.37 = (bf16[192,4224]{1,0:T(8,128)(2,1)S(1)}, bf16[192,4224]{1,0:T(8,128)(2,1)}, u32[]{:S(2)}, u32[]{:S(2)}) collective-permute-start(bf16[192,4224]{1,0:T(8,128)(2,1)S(1)} %collective-permute-done.30.refs_0_), channel_id=1, source_target_pairs={{0,1},{1,0},{2,3},{3,2},{4,5},{5,4},{6,7},{7,6}} | collective-permute-start | bytes 4866056 | tf_op jit(solution)/shard_map/ppermute | solution.py:735
  901.1 58.2 %collective-permute-start.38 = (bf16[192,4224]{1,0:T(8,128)(2,1)}, bf16[192,4224]{1,0:T(8,128)(2,1)}, u32[]{:S(2)}, u32[]{:S(2)}) collective-permute-start(bf16[192,4224]{1,0:T(8,128)(2,1)} %collective-permute-done.36.refs_1_), channel_id=1, source_target_pairs={{0,1},{1,0},{2,3},{3,2},{4,5},{5,4},{6,7},{7,6}} | collective-permute-start | bytes 4866056 | tf_op jit(solution)/shard_map/ppermute | solution.py:735
  907.5 61.4 %collective-permute-start.34 = (bf16[192,4224]{1,0:T(8,128)(2,1)S(1)}, bf16[192,4224]{1,0:T(8,128)(2,1)S(1)}, u32[]{:S(2)}, u32[]{:S(2)}) collective-permute-start(bf16[192,4224]{1,0:T(8,128)(2,1)S(1)} %copy-done.7), channel_id=1, source_target_pairs={{0,4},{1,5},{2,6},{3,7},{4,0},{5,1},{6,2},{7,3}} | collective-permute-start | bytes 4866056 | tf_op jit(solution)/shard_map/ppermute | solution.py:735
  911.0 45.5 %collective-permute-start.4 = (bf16[192,1408]{1,0:T(8,128)(2,1)S(1)}, bf16[192,1408]{1,0:T(8,128)(2,1)S(1)}, u32[]{:S(2)}, u32[]{:S(2)}) collective-permute-start(bf16[192,1408]{1,0:T(8,128)(2,1)S(1)} %copy-done.44), channel_id=1, source_target_pairs={{0,4},{1,5},{2,6},{3,7},{4,0},{5,1},{6,2},{7,3}} | collective-permute-start | bytes 1622024 | tf_op jit(solution)/shard_map/ppermute | solution.py:735
  911.7 70.5 %collective-permute-start.31 = (bf16[192,4224]{1,0:T(8,128)(2,1)S(1)}, bf16[192,4224]{1,0:T(8,128)(2,1)S(1)}, u32[]{:S(2)}, u32[]{:S(2)}) collective-permute-start(bf16[192,4224]{1,0:T(8,128)(2,1)S(1)} %collective-permute-done.30.refs_0_), channel_id=1, source_target_pairs={{0,2},{1,3},{2,0},{3,1},{4,6},{5,7},{6,4},{7,5}} | collective-permute-start | bytes 4866056 | tf_op jit(solution)/shard_map/ppermute | solution.py:735
  958.6 23.0 %collective-permute-start.1 = (bf16[192,1408]{1,0:T(8,128)(2,1)S(1)}, bf16[192,1408]{1,0:T(8,128)(2,1)S(1)}, u32[]{:S(2)}, u32[]{:S(2)}) collective-permute-start(bf16[192,1408]{1,0:T(8,128)(2,1)S(1)} %copy-done.32), channel_id=1, source_target_pairs={{0,2},{1,3},{2,0},{3,1},{4,6},{5,7},{6,4},{7,5}} | collective-permute-start | bytes 1622024 | tf_op jit(solution)/shard_map/ppermute | solution.py:735
  959.4 22.3 %collective-permute-start.8 = (bf16[192,1408]{1,0:T(8,128)(2,1)S(1)}, bf16[192,1408]{1,0:T(8,128)(2,1)S(1)}, u32[]{:S(2)}, u32[]{:S(2)}) collective-permute-start(bf16[192,1408]{1,0:T(8,128)(2,1)S(1)} %copy-done.23), channel_id=1, source_target_pairs={{0,1},{1,0},{2,3},{3,2},{4,5},{5,4},{6,7},{7,6}} | collective-permute-start | bytes 1622024 | tf_op jit(solution)/shard_map/ppermute | solution.py:735
  (110 other events, 1306.6 us)

commit v5 on v4

--- a/solution.py
+++ b/solution.py
@@ -35,6 +35,7 @@
 ANY = pl.BlockSpec(memory_space=pl.ANY)
 SQUEEZED = pl.Squeezed()
 FACTOR = (8, 128)
+FEW = 16
 FIRST = pl.BlockSpec(FACTOR, lambda *_: (0, 0))
 GROUPS = {"own": (0, 1), "near": (4, 2, 5, 3), "across": (6,), "last": (7,), "ahead_own": (4, 2, 6), "ahead_partner": (5, 3, 7)}
 
@@ -42,6 +43,10 @@
 def dot(a, b, dims="nn"):
     ca, cb = ("tn".index(dims[0]), "nt".index(dims[1]))
     return lax.dot_general(a, b, (((ca,), (cb,)), ((), ())), preferred_element_type=F32)
+
+
+def band(i, n, start=0):
+    return pl.ds(pl.multiple_of(start + i * n, n), n)
 
 
 def resident(shape):
@@ -81,7 +86,7 @@
         columns = pl.ds(start, width)
         pairs = [
             (self.wg.at[l, :, columns], self.gu_ref.at[slot, :, pl.ds(0, width)]),
-            (self.wu.at[l, :, columns], self.gu_ref.at[slot, :, pl.ds(BLOCK, width)]),
+            (self.wu.at[l, :, columns], self.gu_ref.at[slot, :, pl.ds(width, width)]),
         ]
         if self.wd is not None:
             pairs.append((self.wd.at[l, columns], self.down_ref.at[slot, pl.ds(0, width)]))
@@ -134,11 +139,11 @@
             pl.semaphore_signal(barrier, inc=1, device_id=to, device_id_type=MESH)
         weights.start(j)
 
-        @pl.loop(0, TOKENS // 256)
+        @pl.loop(0, TOKENS // BLOCK)
         def _(i):
-            r = pl.ds(pl.multiple_of(i * 256, 256), 256)
+            r = band(i, BLOCK)
             a_ref[r, :] = normed(x_ref[r, :])
-            acc_ref[r, :] = jnp.zeros((256, D), F32)
+            acc_ref[r, :] = jnp.zeros((BLOCK, D), F32)
 
         keep[0].start()
 
@@ -153,9 +158,9 @@
     def _():
         keep[0].wait()
 
-        @pl.loop(0, TOKENS // 256)
+        @pl.loop(0, TOKENS // BLOCK)
         def _(i):
-            r = pl.ds(pl.multiple_of(i * 256, 256), 256)
+            r = band(i, BLOCK)
             h = x_ref[r, :] + acc_ref[r, :].astype(BF)
             h_ref[r, :] = h
             a_ref[r, :] = normed(h)
@@ -174,24 +179,29 @@
     pl.when(j + 1 < ALL)(lambda: weights.start(j + 1))
     weights.wait(j)
     slot = lax.rem(j, 2)
-    for i in range(8):
-        r = slice(256 * i, 256 * i + 256)
-        gu = dot(a_ref[r, :], gu_ref[slot])
-        g, u = gu[:, :BLOCK], gu[:, BLOCK:]
-        s = jax.nn.sigmoid(g)
-        sl = g * s
-        sl_ref[0, r, :] = sl
-        q_ref[0, r, :] = u * (s * (1.0 + g * (1.0 - s)))
-        hid = (sl * u).astype(BF)
-        hid_ref[r, :] = hid
-        ht_ref[0, :, r] = hid.T
+
+    def hidden(width):
+        for i in range(TOKENS // BLOCK):
+            r = slice(BLOCK * i, BLOCK * (i + 1))
+            gu = dot(a_ref[r, :], gu_ref[slot, :, : 2 * width])
+            g, u = gu[:, :width], gu[:, width:]
+            s = jax.nn.sigmoid(g)
+            sl = g * s
+            sl_ref[0, r, :width] = sl
+            q_ref[0, r, :width] = u * (s * (1.0 + g * (1.0 - s)))
+            hid = (sl * u).astype(BF)
+            hid_ref[r, :width] = hid
+            ht_ref[0, :width, r] = hid.T
+
+    pl.when(block < STEPS - 1)(lambda: hidden(BLOCK))
+
+    @pl.when(block == STEPS - 1)
+    def _():
+        hidden(LAST)
+        hid_ref[:, LAST:] = jnp.zeros((TOKENS, BLOCK - LAST), BF)
 
     @pl.when(j < STEPS)
     def _():
-        @pl.when(block == STEPS - 1)
-        def _():
-            hid_ref[:, LAST:] = jnp.zeros((TOKENS, BLOCK - LAST), BF)
-
         acc_ref[...] += dot(hid_ref[...], down_ref[slot])
 
     @pl.when(j == ALL - 1)
@@ -250,10 +260,10 @@
         self.d = 2 * (third - second)
 
 
-def backward_kernel(lags, a_in, dy_in, wd_ref, sl_ref, q_ref, ht_ref, wg, wu, h_in, *refs):
-    g_gate, g_up, g_down, f_ref, far_out, acc_ref, gu_ref, w_sems, sq_ref, every_ref, f_send, f_recv, *refs = refs
+def backward_kernel(lags, a_in, dy_in, wd_ref, sl_ref, q_ref, ht_ref, wg, wu, h_in, m_in, v_in, *refs):
+    g_gate, g_up, g_down, f_ref, far_out, new_out, acc_ref, gu_ref, w_sems, sq_ref, every_ref, f_send, f_recv, *refs = refs
     near_send, near_recv, far_send, far_recv, a_ref, dy_ref, dgu_ref, s_ref, a2_ref, bx, by, cx, cy, ex, ey, dx, dy2, *refs = refs
-    og, ou, od, s_send, a_recv, bx_send, by_send, cx_recv, cy_recv, ex_send, ey_send, dx_recv, dy_recv, out_sem, a_sem = refs
+    og, ou, od, s_send, a_recv, bx_send, by_send, cx_recv, cy_recv, ex_send, ey_send, dx_recv, dy_recv, out_sem, a_sem, new_sem = refs
     weights = Weights(1, wg, wu, None, gu_ref, None, w_sems)
     j = pl.program_id(0)
     block = lax.rem(j, STEPS)
@@ -412,9 +422,9 @@
             pl.semaphore_signal(barrier, inc=1, device_id=to, device_id_type=MESH)
         sq_ref[...] = jnp.zeros_like(sq_ref)
 
-        @pl.loop(0, TOKENS // 256)
+        @pl.loop(0, TOKENS // BLOCK)
         def _(i):
-            acc_ref[pl.ds(pl.multiple_of(i * 256, 256), 256), :] = jnp.zeros((256, D), F32)
+            acc_ref[band(i, BLOCK), :] = jnp.zeros((BLOCK, D), F32)
 
         take_dy.wait()
 
@@ -422,9 +432,9 @@
     def _():
         take_h.wait()
 
-        @pl.loop(0, TOKENS // 128)
+        @pl.loop(0, TOKENS // LAST)
         def _(i):
-            r = pl.ds(pl.multiple_of(i * 128, 128), 128)
+            r = band(i, LAST)
             h = a_ref[r, :].astype(F32)
             da = acc_ref[r, :].astype(BF).astype(F32)
             scale = lax.rsqrt(jnp.mean(h * h, -1, keepdims=True) + 1e-6)
@@ -438,7 +448,7 @@
         pl.when(j + 1 < STEPS)(lambda: weights.start(j + 1))
         s = lax.rem(j, lags.s)
         for i in range(4):
-            r = slice(512 * i, 512 * i + 512)
+            r = slice(2 * BLOCK * i, 2 * BLOCK * (i + 1))
             dh = dot(dy_ref[r, :], wd_ref[0], "nt").astype(BF).astype(F32)
             dgu_ref[r, :BLOCK] = (dh * q_ref[0, r, :]).astype(BF)
             dgu_ref[r, BLOCK:] = (dh * sl_ref[0, r, :]).astype(BF)
@@ -446,16 +456,20 @@
         pl.when(j == 0)(lambda: take_a1.wait())
         pl.when(j == STEPS)(lambda: take_a0.wait())
 
+        def gate_up(width):
+            for h in range(2):
+                gu = dot(a_ref[:, D // 2 * h : D // 2 * (h + 1)], dgu_ref[:, : 2 * width], "tn")
+                for o in range(4):
+                    for t in range(2):
+                        s_ref[s, t, h, o // 2, o % 2, :, :width] = gu[PART * o : PART * o + PART, width * t : width * t + width].astype(BF)
+
+        pl.when(block < STEPS - 1)(lambda: gate_up(BLOCK))
+
         @pl.when(block == STEPS - 1)
         def _():
-            dgu_ref[:, LAST:BLOCK] = jnp.zeros((TOKENS, BLOCK - LAST), BF)
-            dgu_ref[:, BLOCK + LAST :] = jnp.zeros((TOKENS, BLOCK - LAST), BF)
-
-        for h in range(2):
-            gu = dot(a_ref[:, D // 2 * h : D // 2 * (h + 1)], dgu_ref[...], "tn")
-            for o in range(4):
-                for t in range(2):
-                    s_ref[s, t, h, o // 2, o % 2] = gu[PART * o : PART * o + PART, BLOCK * t : BLOCK * t + BLOCK].astype(BF)
+            dgu_ref[:, LAST:BLOCK] = dgu_ref[:, BLOCK : BLOCK + LAST]
+            gate_up(LAST)
+
         pl.when(j == STEPS - 1)(lambda: take_h.start())
         pl.when(j == 0)(lambda: pl.semaphore_wait(barrier, len(others)))
         each(j, functools.partial(pair, which=(0,)), start)
@@ -478,12 +492,14 @@
 
         each(j, functools.partial(pair, which=(1,)), start)
 
-        @pl.when(j < STEPS)
-        def _():
+        def add_da(width):
             weights.wait(j)
             for i in range(8):
-                r = slice(256 * i, 256 * i + 256)
-                acc_ref[r, :] += dot(dgu_ref[r, :], gu_ref[lax.rem(j, 2)], "nt")
+                r = slice(BLOCK * i, BLOCK * (i + 1))
+                acc_ref[r, :] += dot(dgu_ref[r, : 2 * width], gu_ref[lax.rem(j, 2), :, : 2 * width], "nt")
+
+        pl.when(j < STEPS - 1)(lambda: add_da(BLOCK))
+        pl.when(j == STEPS - 1)(lambda: add_da(LAST))
 
     pl.when((j >= lags.third) & (j < ALL + lags.third))(lambda: take_third(j - lags.third))
     pl.when((j >= lags.second) & (j < ALL + lags.second))(lambda: take_second(j - lags.second))
@@ -492,8 +508,34 @@
     at_step(j - lags.third - 2, pass_on)
     at_step(j - lags.third, lambda t: [copy.start() for copy in near(t)])
 
+    chunks = [(k, start, min(2 * BLOCK, THIRD - start)) for k, start in enumerate(range(0, THIRD, 2 * BLOCK))]
+
+    def rows_of(k):
+        return pl.ds(PART * k, PART)
+
+    def gathered():
+        mine = band(me, PART)
+        copies = [(t.at[1, :, pl.ds(AHEAD, THIRD)], acc_ref.at[rows_of(k), pl.ds(0, THIRD)]) for k, t in enumerate((m_in, v_in))]
+        for k, start, width in chunks:
+            w, room = pl.ds(AHEAD + start, width), (rows_of(k), pl.ds(0, width))
+            copies += [(wg.at[1, mine, w], gu_ref.at[(0, *room)]), (g_gate.at[1, :, w], gu_ref.at[(1, *room)])]
+        return [pltpu.make_async_copy(src, dst, new_sem.at[n]) for n, (src, dst) in enumerate(copies)]
+
+    def given():
+        return [
+            pltpu.make_async_copy(gu_ref.at[0, rows_of(k), pl.ds(0, width)], new_out.at[:, pl.ds(start, width)], new_sem.at[k])
+            for k, start, width in chunks
+        ]
+
+    @pl.when(j == ALL)
+    def _():
+        for copy in gathered():
+            copy.start()
+
     @pl.when(j == ALL + lags.third - 1)
     def _():
+        for copy in gathered():
+            copy.wait()
         both = sq_ref[...]
         every_ref[me] = both[:, :128] + both[:, 128:]
 
@@ -514,10 +556,23 @@
             copy.wait()
         squares = functools.reduce(lambda p, q: p + q, [every_ref[n] for n in range(8)])
         squares = jnp.sum(jnp.sum(squares, axis=1, keepdims=True), axis=0, keepdims=True)
-        f_ref[...] = jnp.broadcast_to(jnp.minimum(1.0, 0.5 * lax.rsqrt(squares / COUNT + 1e-30)), FACTOR)
-
-
-def backward(lags, a, dy, wd, sl, q, ht, wg, wu, h):
+        factor = jnp.minimum(1.0, 0.5 * lax.rsqrt(squares / COUNT + 1e-30))
+        f_ref[...] = jnp.broadcast_to(factor, FACTOR)
+
+        @pl.loop(0, PART // FEW)
+        def _(i):
+            for k, start, width in chunks:
+                r, w = band(i, FEW, PART * k), pl.ds(start, width)
+                m, v = (acc_ref[band(i, FEW, PART * n), w] for n in range(2))
+                gu_ref[0, r, :width], _, _ = stepped(factor, gu_ref[1, r, :width], gu_ref[0, r, :width], m, v)
+
+        for copy in given():
+            copy.start()
+        for copy in given():
+            copy.wait()
+
+
+def backward(lags, a, dy, wd, sl, q, ht, wg, wu, h, m, v):
     layer = lambda j: 1 - lax.div(jnp.minimum(j, ALL - 1), STEPS)
     block = lambda j: lax.rem(jnp.minimum(j, ALL - 1), STEPS)
     wide = pl.BlockSpec((1, TOKENS, BLOCK), lambda j: (layer(j), 0, block(j)))
@@ -534,16 +589,15 @@
             wide,
             wide,
             pl.BlockSpec((8, SUB, TOKENS), lambda j: (layer(j), block(j), 0)),
-            ANY,
-            ANY,
-            ANY,
+            *[ANY] * 5,
         ],
-        out_specs=[ANY, ANY, ANY, FIRST, ANY],
+        out_specs=[ANY, ANY, ANY, FIRST, ANY, ANY],
         out_shape=[
             *[shape((LAYERS, PART, FF), BF)] * 2,
             shape((LAYERS, OWN_DOWN, D), BF),
             shape(FACTOR, F32),
             shape((3, TILES, *piece), BF),
+            shape((PART, THIRD), BF),
         ],
         scratch_shapes=[
             pltpu.VMEM((TOKENS, D), F32),
@@ -565,11 +619,12 @@
             *[dma((n,)) for n in (lags.b, lags.b, lags.c, lags.c, lags.e, lags.e, lags.d, lags.d)],
             dma((2, 3)),
             dma((4,)),
+            dma((8,)),
         ],
         compiler_params=pltpu.CompilerParams(vmem_limit_bytes=VMEM_LIMIT, collective_id=0, has_side_effects=True),
         cost_estimate=cost(10, 300e6),
         name="backward",
-    )(a, dy, wd, sl, q, ht.reshape(LAYERS * 8, OWN_DOWN, TOKENS), wg, wu, h)
+    )(a, dy, wd, sl, q, ht.reshape(LAYERS * 8, OWN_DOWN, TOKENS), wg, wu, h, m, v)
 
 
 def stepped(factor, g, w, m, v):
@@ -583,9 +638,9 @@
     nw_ref, nm_ref, nv_ref = refs[-3:]
     factor = f_ref[:1, :1]
 
-    @pl.loop(0, g_ref.shape[0] // 16)
+    @pl.loop(0, g_ref.shape[0] // FEW)
     def _(i):
-        r = pl.ds(pl.multiple_of(i * 16, 16), 16)
+        r = band(i, FEW)
         nw_ref[r, :], nm_ref[0, r, :], nv_ref[0, r, :] = stepped(factor, g_ref[r, :], w_ref[0, r, :], m_ref[0, r, :], v_ref[0, r, :])
 
 
@@ -633,9 +688,9 @@
 def adamw_ahead_kernel(owners_ref, f_ref, g_ref, w_ref, m_ref, v_ref, nw_ref):
     factor = f_ref[:1, :1]
 
-    @pl.loop(0, PART // 32)
+    @pl.loop(0, PART // SUB)
     def _(i):
-        r = pl.ds(pl.multiple_of(i * 32, 32), 32)
+        r = band(i, SUB)
         nw_ref[0, r, :], _, _ = stepped(factor, g_ref[r, :], w_ref[0, r, :], m_ref[r, :], v_ref[r, :])
 
 
@@ -671,9 +726,10 @@
             out_ref[0] = refs[k][...]
 
 
-def place(piece, owners, pieces, so_far, whole):
+def place(piece, owners, pieces, so_far, whole, both=False):
     _, l, axis, skip, count = piece
     n = len(pieces)
+    of_layer = lambda s: s if both else l
     block = tuple(m // count if k == axis else m for k, m in enumerate(pieces[0].shape))
 
     def of(k):
@@ -693,7 +749,7 @@
             grid=(n, count),
             in_specs=in_specs,
             out_specs=pl.BlockSpec(
-                (1, *block), lambda s, i, own: (l, 3 * own[s] + skip + i, 0) if axis == 0 else (l, own[s], skip + i)
+                (1, *block), lambda s, i, own: (of_layer(s), 3 * own[s] + skip + i, 0) if axis == 0 else (of_layer(s), own[s], skip + i)
             ),
         ),
         out_shape=jax.ShapeDtypeStruct(whole.shape, BF),
@@ -738,7 +794,7 @@
         x, dy = x[0], dy[0]
         me = lax.axis_index("dp")
         a, ht, sl, q, h1, mv = forward(x, wg, wu, wd, mg, vg)
-        *gradients, factor, g_ahead = backward(Lags(2, 3, 2, 2), a, dy, wd, sl, q, ht, wg, wu, h1)
+        *gradients, factor, g_ahead, early = backward(Lags(2, 3, 2, 2), a, dy, wd, sl, q, ht, wg, wu, h1, mg, vg)
         at = me[None].astype(jnp.int32)
         groups = {name: jnp.stack([me ^ k for k in group]).astype(jnp.int32) for name, group in GROUPS.items()}
         mats = ((wg, mg, vg), (wu, mu, vu), (wd, md, vd))
@@ -757,7 +813,7 @@
         for number, piece in enumerate(PIECES):
             have = {}
             everything.append(have)
-            have[0] = new_rows(piece)
+            have[0] = new_rows(piece) if number else early
             have[4] = swap(have[0], 4)
             have[2] = swap(have[0], 2)
             have[6] = swap(have[4], 2) if number % 2 else swap(have[2], 4)
@@ -766,14 +822,21 @@
             put("own", piece, have)
             put("near", piece, have)
         have = {0: new_rows(KNOWN)}
+        new_rows(PIECES[0])
         have[1] = swap(have[0], 1)
         put("own", KNOWN, have)
         ahead = adamw_ahead(groups["ahead_own"], factor, g_ahead, wg, mv)
         for kind, new in (("ahead_own", ahead), ("ahead_partner", swap(ahead, 1))):
             whole[0] = place_ahead(groups[kind], new, whole[0])
-        for piece, have in zip(PIECES, everything):
-            put("across", piece, have)
-            put("last", piece, have)
+        for number, (piece, have) in enumerate(zip(PIECES, everything)):
+            if piece[0] == GATE:
+                put("across", piece, have)
+                put("last", piece, have)
+            elif piece[1] == 0:
+                for kind in ("across", "last"):
+                    k, n = GROUPS[kind][0], piece[0]
+                    pair = [have[k], everything[number + 1][k]]
+                    whole[n] = place(piece, jnp.tile(groups[kind], 2), pair, whole[n], mats[n][0], both=True)
         return tuple(whole + [m[0] for m in moments] + [m[1] for m in moments])
 
     whole, rows = P(), P(None, "dp")

time: 995 us -> 970 us (0.975)
  waiting for transfers between devices: 172 us -> 153 us
    ppermute x72, waiting for transfers between devices: 172 us -> 153 us  [swap(): return lax.ppermute(t, 'dp', [(i, i ^ mask) for i in range(8)])]
    unnamed x172 -> x168, local copies, waits for them, and re-layouts: 25.6 us -> 16.4 us
    pallas_call x41 -> x35, Pallas kernels: 99.4 us -> 104 us  [place(): pl.pallas_call(functools.partial(place_kernel, n), grid_spec=pltpu.Prefet...]
  transfers between devices with their start and end apart: 72 -> 72, of which waited for: 19 -> 21; matrix products, arithmetic and copies ran while one was open for 0% -> 0% of each run, Pallas kernels for 18% -> 19%
where the time goes in v5:
time: 970 us; the launch traced here: 968 us
  Pallas kernels  759 us (78%)
  waiting for transfers between devices  153 us (16%)
  starting transfers between devices  37.6 us (4%)
  local copies, waits for them, and re-layouts  16.4 us (2%)
    pallas_call x1, Pallas kernels, backward(): pl.pallas_call(functools.partial(backward_kernel, lags), grid=(ALL + lags...  389 us
    pallas_call x1, Pallas kernels, forward(): pl.pallas_call(forward_kernel, grid=(ALL,), in_specs=[resident((TOKENS, D...  168 us
    ppermute x72, waiting for transfers between devices, swap(): return lax.ppermute(t, 'dp', [(i, i ^ mask) for i in range(8)])  153 us
    pallas_call x35, Pallas kernels, place(): pl.pallas_call(functools.partial(place_kernel, n), grid_spec=pltpu.Prefet...  104 us
    pallas_call x11, Pallas kernels, adamw(): pl.pallas_call(adamw_kernel, grid_spec=pltpu.PrefetchScalarGridSpec(num_s...  60 us
    ppermute x72, starting transfers between devices, swap(): return lax.ppermute(t, 'dp', [(i, i ^ mask) for i in range(8)])  37.6 us
    pallas_call x1, Pallas kernels, adamw_ahead(): pl.pallas_call(adamw_ahead_kernel, grid_spec=pltpu.PrefetchScalarGridSpec...  26.2 us
  transfers between devices with their start and end apart: 72, of which 21 were waited for; matrix products, arithmetic and copies ran while one was open for 0% of the time, Pallas kernels for 19%

profile of v5, /device:TPU:0, one launch (start us, length us, event | category | flops | bytes accessed | tf_op | source)
XLA Modules:
  0.0 968.1 jit_solution(297627085315163021)
XLA Ops:
  0.6 167.6 %forward.1 = (bf16[2,2048,1536]{2,1,0:T(8,128)(2,1)}, bf16[2,4224,2048]{2,1,0:T(8,128)(2,1)}, f32[2,2048,4224]{2,1,0:T(8,128)}, f32[2,2048,4224]{2,1,0:T(8,128)}...) custom-call(bf16[2048,1536]{1,0:T(8,128)(2,1)} %bitcast.11, bf16[2,1536,4224]{2,1,0:T(8,128)(2,1)} %w_ref.23, ...), custom_call_target="tpu_custom_call" | custom-call | flops 132875550720 | bytes 260000000 | tf_op jit(solution)/shard_map/forward/pallas_call | solution.py:221
  168.3 389.4 %backward.1 = (bf16[2,192,4224]{2,1,0:T(8,128)(2,1)}, bf16[2,192,4224]{2,1,0:T(8,128)(2,1)}, bf16[2,528,1536]{2,1,0:T(8,128)(2,1)}, f32[8,128]{1,0:T(8,128)}, bf...) custom-call(bf16[2,2048,1536]{2,1,0:T(8,128)(2,1)} %get-tuple-element.53.a_in, bf16[2048,1536]{1,0:T(8,128)(2,1)} %bitcast.12, ...), custom_call_target="tpu_custom_call" | custom-call | flops 265751101440 | bytes 300000000 | tf_op jit(solution)/shard_map/backward/pallas_call | solution.py:582
  560.3 5.2 shard_map.207
  565.6 5.6 shard_map.208
  571.2 4.5 shard_map.209
  577.9 4.2 shard_map.210
  585.0 6.0 collective-permute-done.60.refs_0_
  595.1 4.2 shard_map.178
  599.2 3.3 collective-permute-done.47.refs_0_
  602.6 4.4 shard_map.179
  609.9 5.4 collective-permute-done.9.refs_1_
  617.2 4.2 shard_map.180
  621.4 4.5 collective-permute-done.6.refs_0_
  628.8 8.6 collective-permute-done.18.refs_0_
  642.3 6.7 collective-permute-done.refs_0_
  649.0 3.7 collective-permute-done.14.refs_1_
  654.8 20.9 %collective-permute-done.50.refs_1_ = bf16[352,1536]{1,0:T(8,128)(2,1)S(1)} collective-permute-done((bf16[352,1536]{1,0:T(8,128)(2,1)S(1)}, bf16[352,1536]{1,0:T(8,128)(2,1)S(1)}, u32[]{:S(2)}, u32[]{:S(2)}) %collective-permute-start.50) | collective-permute-done | bytes 1081376 | tf_op jit(solution)/shard_map/ppermute | solution.py:791
  677.1 17.6 %collective-permute-done.53.refs_0_ = bf16[352,1536]{1,0:T(8,128)(2,1)S(1)} collective-permute-done((bf16[352,1536]{1,0:T(8,128)(2,1)S(1)}, bf16[352,1536]{1,0:T(8,128)(2,1)S(1)}, u32[]{:S(2)}, u32[]{:S(2)}) %collective-permute-start.53) | collective-permute-done | bytes 1081376 | tf_op jit(solution)/shard_map/ppermute | solution.py:791
  701.0 5.6 shard_map.181
  706.6 2.8 collective-permute-done.48.refs_1_
  710.2 4.5 shard_map.223
  716.9 8.9 shard_map.199
  726.9 8.7 shard_map.200
  738.1 26.2 %adamw_ahead.1.new_ref = bf16[3,192,2816]{2,1,0:T(8,128)(2,1)} custom-call(s32[3]{0:T(128)S(1)} %pad_add_fusion.1.owners_ref, f32[8,128]{1,0:T(8,128)S(1)} %copy-done.22, bf16[3,11,192,256]{3,2,1,0:T(8,128)(2,1)} %get-tuple-element.68.g_ref, bf16[2,1536,4224]{2,1,0:T(8,128)(2,1)} %w_ref.23, f32[2,3,192,2816]{3,2,1,0:T(8,128)} %get-tuple-element.69.m_ref.v_ref, ...), custom_call_target="tpu_custom_call" | custom-call | flops 2657510912 | bytes 22708224 | tf_op jit(solution)/shard_map/adamw_ahead/pallas_call | solution.py:699
  772.7 12.5 %collective-permute-done.7.refs_0_ = bf16[192,1408]{1,0:T(8,128)(2,1)S(1)} collective-permute-done((bf16[192,1408]{1,0:T(8,128)(2,1)}, bf16[192,1408]{1,0:T(8,128)(2,1)S(1)}, u32[]{:S(2)}, u32[]{:S(2)}) %collective-permute-start.7) | collective-permute-done | bytes 540704 | tf_op jit(solution)/shard_map/ppermute | solution.py:791
  788.0 3.5 shard_map.185.refs_2_
  793.7 4.0 shard_map.187.refs_2_
  797.7 5.2 collective-permute-done.40.refs_0_
  805.5 4.0 shard_map.189.refs_2_
  809.5 4.8 shard_map.190.so_far
  814.3 22.0 %collective-permute-done.33.refs_0_ = bf16[192,4224]{1,0:T(8,128)(2,1)S(1)} collective-permute-done((bf16[192,4224]{1,0:T(8,128)(2,1)S(1)}, bf16[192,4224]{1,0:T(8,128)(2,1)S(1)}, u32[]{:S(2)}, u32[]{:S(2)}) %collective-permute-start.33) | collective-permute-done | bytes 1622048 | tf_op jit(solution)/shard_map/ppermute | solution.py:791
  836.8 5.9 place_ahead.2.so_far
  845.2 5.2 shard_map.201.refs_4_
  851.5 6.4 shard_map.212.refs_2_
  861.7 7.1 shard_map.214.refs_2_
  873.0 3.3 collective-permute-done.54.refs_1_
  877.9 5.6 collective-permute-done.51.refs_0_
  886.5 4.7 shard_map.219.refs_2_
  891.2 5.9 place_ahead.3.refs_1_
  903.3 9.5 shard_map.202.refs_2_
  912.8 3.3 shard_map.203.refs_4_
  917.8 7.8 shard_map.204.refs_2_
  925.5 9.0 collective-permute-done.34.refs_1_
  937.7 3.3 shard_map.205.refs_2_
  940.9 7.2 collective-permute-done.4.refs_0_
  949.6 4.7 shard_map.220.refs_2_
  954.3 4.3 collective-permute-done.45.refs_0_
  964.8 3.3 shard_map.206
  (321 shorter events, 91.9 us)
Async XLA Ops:
  582.2 20.4 %collective-permute-start.47 = (bf16[176,1536]{1,0:T(8,128)(2,1)S(1)}, bf16[176,1536]{1,0:T(8,128)(2,1)S(1)}, u32[]{:S(2)}, u32[]{:S(2)}) collective-permute-start(bf16[176,1536]{1,0:T(8,128)(2,1)S(1)} %get-tuple-element.86.refs_0_), channel_id=1, source_target_pairs={{0,4},{1,5},{2,6},{3,7},{4,0},{5,1},{6,2},{7,3}} | collective-permute-start | bytes 1622024 | tf_op jit(solution)/shard_map/ppermute | solution.py:791
  584.2 22.7 %collective-permute-start.56 = (bf16[176,1536]{1,0:T(8,128)(2,1)S(1)}, bf16[176,1536]{1,0:T(8,128)(2,1)S(1)}, u32[]{:S(2)}, u32[]{:S(2)}) collective-permute-start(bf16[176,1536]{1,0:T(8,128)(2,1)S(1)} %get-tuple-element.86.refs_0_), channel_id=1, source_target_pairs={{0,2},{1,3},{2,0},{3,1},{4,6},{5,7},{6,4},{7,5}} | collective-permute-start | bytes 1622024 | tf_op jit(solution)/shard_map/ppermute | solution.py:791
  592.1 23.2 %collective-permute-start.9 = (bf16[192,1408]{1,0:T(8,128)(2,1)S(1)}, bf16[192,1408]{1,0:T(8,128)(2,1)S(1)}, u32[]{:S(2)}, u32[]{:S(2)}) collective-permute-start(bf16[192,1408]{1,0:T(8,128)(2,1)S(1)} %copy-done.46), channel_id=1, source_target_pairs={{0,2},{1,3},{2,0},{3,1},{4,6},{5,7},{6,4},{7,5}} | collective-permute-start | bytes 1622024 | tf_op jit(solution)/shard_map/ppermute | solution.py:791
  593.9 21.4 %collective-permute-start.26 = (bf16[192,1408]{1,0:T(8,128)(2,1)S(1)}, bf16[192,1408]{1,0:T(8,128)(2,1)S(1)}, u32[]{:S(2)}, u32[]{:S(2)}) collective-permute-start(bf16[192,1408]{1,0:T(8,128)(2,1)S(1)} %copy-done.46), channel_id=1, source_target_pairs={{0,4},{1,5},{2,6},{3,7},{4,0},{5,1},{6,2},{7,3}} | collective-permute-start | bytes 1622024 | tf_op jit(solution)/shard_map/ppermute | solution.py:791
  606.9 18.9 %collective-permute-start.6 = (bf16[192,1408]{1,0:T(8,128)(2,1)S(1)}, bf16[192,1408]{1,0:T(8,128)(2,1)}, u32[]{:S(2)}, u32[]{:S(2)}) collective-permute-start(bf16[192,1408]{1,0:T(8,128)(2,1)S(1)} %get-tuple-element.66.refs_0_), channel_id=1, source_target_pairs={{0,4},{1,5},{2,6},{3,7},{4,0},{5,1},{6,2},{7,3}} | collective-permute-start | bytes 1622024 | tf_op jit(solution)/shard_map/ppermute | solution.py:791
  615.3 22.1 %collective-permute-start.18 = (bf16[192,1408]{1,0:T(8,128)(2,1)S(1)}, bf16[192,1408]{1,0:T(8,128)(2,1)}, u32[]{:S(2)}, u32[]{:S(2)}) collective-permute-start(bf16[192,1408]{1,0:T(8,128)(2,1)S(1)} %get-tuple-element.65.refs_0_), channel_id=1, source_target_pairs={{0,4},{1,5},{2,6},{3,7},{4,0},{5,1},{6,2},{7,3}} | collective-permute-start | bytes 1622024 | tf_op jit(solution)/shard_map/ppermute | solution.py:791
  617.0 36.9 %collective-permute-start.71 = (bf16[352,1536]{1,0:T(8,128)(2,1)S(1)}, bf16[352,1536]{1,0:T(8,128)(2,1)S(1)}, u32[]{:S(2)}, u32[]{:S(2)}) collective-permute-start(bf16[352,1536]{1,0:T(8,128)(2,1)S(1)} %get-tuple-element.87.refs_0_), channel_id=1, source_target_pairs={{0,1},{1,0},{2,3},{3,2},{4,5},{5,4},{6,7},{7,6}} | collective-permute-start | bytes 3244040 | tf_op jit(solution)/shard_map/ppermute | solution.py:791
  627.9 21.1 %collective-permute-start = (bf16[192,1408]{1,0:T(8,128)(2,1)S(1)}, bf16[192,1408]{1,0:T(8,128)(2,1)}, u32[]{:S(2)}, u32[]{:S(2)}) collective-permute-start(bf16[192,1408]{1,0:T(8,128)(2,1)S(1)} %get-tuple-element.64.refs_0_), channel_id=1, source_target_pairs={{0,4},{1,5},{2,6},{3,7},{4,0},{5,1},{6,2},{7,3}} | collective-permute-start | bytes 1622024 | tf_op jit(solution)/shard_map/ppermute | solution.py:791
  639.5 36.2 %collective-permute-start.50 = (bf16[352,1536]{1,0:T(8,128)(2,1)S(1)}, bf16[352,1536]{1,0:T(8,128)(2,1)S(1)}, u32[]{:S(2)}, u32[]{:S(2)}) collective-permute-start(bf16[352,1536]{1,0:T(8,128)(2,1)S(1)} %get-tuple-element.87.refs_0_), channel_id=1, source_target_pairs={{0,2},{1,3},{2,0},{3,1},{4,6},{5,7},{6,4},{7,5}} | collective-permute-start | bytes 3244040 | tf_op jit(solution)/shard_map/ppermute | solution.py:791
  641.2 35.4 %collective-permute-start.68 = (bf16[352,1536]{1,0:T(8,128)(2,1)S(1)}, bf16[352,1536]{1,0:T(8,128)(2,1)}, u32[]{:S(2)}, u32[]{:S(2)}) collective-permute-start(bf16[352,1536]{1,0:T(8,128)(2,1)S(1)} %get-tuple-element.87.refs_0_), channel_id=1, source_target_pairs={{0,4},{1,5},{2,6},{3,7},{4,0},{5,1},{6,2},{7,3}} | collective-permute-start | bytes 3244040 | tf_op jit(solution)/shard_map/ppermute | solution.py:791
  649.0 28.1 %collective-permute-start.67 = (bf16[352,1536]{1,0:T(8,128)(2,1)S(1)}, bf16[352,1536]{1,0:T(8,128)(2,1)S(1)}, u32[]{:S(2)}, u32[]{:S(2)}) collective-permute-start(bf16[352,1536]{1,0:T(8,128)(2,1)S(1)} %get-tuple-element.88.refs_0_), channel_id=1, source_target_pairs={{0,1},{1,0},{2,3},{3,2},{4,5},{5,4},{6,7},{7,6}} | collective-permute-start | bytes 3244040 | tf_op jit(solution)/shard_map/ppermute | solution.py:791
  652.7 42.0 %collective-permute-start.53 = (bf16[352,1536]{1,0:T(8,128)(2,1)S(1)}, bf16[352,1536]{1,0:T(8,128)(2,1)S(1)}, u32[]{:S(2)}, u32[]{:S(2)}) collective-permute-start(bf16[352,1536]{1,0:T(8,128)(2,1)S(1)} %get-tuple-element.88.refs_0_), channel_id=1, source_target_pairs={{0,4},{1,5},{2,6},{3,7},{4,0},{5,1},{6,2},{7,3}} | collective-permute-start | bytes 3244040 | tf_op jit(solution)/shard_map/ppermute | solution.py:791
  653.8 43.1 %collective-permute-start.64 = (bf16[352,1536]{1,0:T(8,128)(2,1)S(1)}, bf16[352,1536]{1,0:T(8,128)(2,1)S(1)}, u32[]{:S(2)}, u32[]{:S(2)}) collective-permute-start(bf16[352,1536]{1,0:T(8,128)(2,1)S(1)} %get-tuple-element.88.refs_0_), channel_id=1, source_target_pairs={{0,2},{1,3},{2,0},{3,1},{4,6},{5,7},{6,4},{7,5}} | collective-permute-start | bytes 3244040 | tf_op jit(solution)/shard_map/ppermute | solution.py:791
  675.7 22.5 %collective-permute-start.61 = (bf16[176,1536]{1,0:T(8,128)(2,1)S(1)}, bf16[176,1536]{1,0:T(8,128)(2,1)S(1)}, u32[]{:S(2)}, u32[]{:S(2)}) collective-permute-start(bf16[176,1536]{1,0:T(8,128)(2,1)S(1)} %collective-permute-done.60.refs_0_), channel_id=1, source_target_pairs={{0,1},{1,0},{2,3},{3,2},{4,5},{5,4},{6,7},{7,6}} | collective-permute-start | bytes 1622024 | tf_op jit(solution)/shard_map/ppermute | solution.py:791
  676.6 21.7 %collective-permute-start.62 = (bf16[176,1536]{1,0:T(8,128)(2,1)S(1)}, bf16[176,1536]{1,0:T(8,128)(2,1)S(1)}, u32[]{:S(2)}, u32[]{:S(2)}) collective-permute-start(bf16[176,1536]{1,0:T(8,128)(2,1)S(1)} %collective-permute-done.44.refs_1_), channel_id=1, source_target_pairs={{0,1},{1,0},{2,3},{3,2},{4,5},{5,4},{6,7},{7,6}} | collective-permute-start | bytes 1622024 | tf_op jit(solution)/shard_map/ppermute | solution.py:791
  677.1 22.5 %collective-permute-start.57 = (bf16[176,1536]{1,0:T(8,128)(2,1)S(1)}, bf16[176,1536]{1,0:T(8,128)(2,1)S(1)}, u32[]{:S(2)}, u32[]{:S(2)}) collective-permute-start(bf16[176,1536]{1,0:T(8,128)(2,1)S(1)} %collective-permute-done.47.refs_0_), channel_id=1, source_target_pairs={{0,1},{1,0},{2,3},{3,2},{4,5},{5,4},{6,7},{7,6}} | collective-permute-start | bytes 1622024 | tf_op jit(solution)/shard_map/ppermute | solution.py:791
  699.7 26.1 %collective-permute-start.24 = (bf16[192,1408]{1,0:T(8,128)(2,1)S(1)}, bf16[192,1408]{1,0:T(8,128)(2,1)S(1)}, u32[]{:S(2)}, u32[]{:S(2)}) collective-permute-start(bf16[192,1408]{1,0:T(8,128)(2,1)S(1)} %collective-permute-done.22.refs_1_), channel_id=1, source_target_pairs={{0,1},{1,0},{2,3},{3,2},{4,5},{5,4},{6,7},{7,6}} | collective-permute-start | bytes 1622024 | tf_op jit(solution)/shard_map/ppermute | solution.py:791
  709.4 26.3 %collective-permute-start.19 = (bf16[192,1408]{1,0:T(8,128)(2,1)}, bf16[192,1408]{1,0:T(8,128)(2,1)}, u32[]{:S(2)}, u32[]{:S(2)}) collective-permute-start(bf16[192,1408]{1,0:T(8,128)(2,1)} %collective-permute-done.18.refs_0_), channel_id=1, source_target_pairs={{0,1},{1,0},{2,3},{3,2},{4,5},{5,4},{6,7},{7,6}} | collective-permute-start | bytes 1622024 | tf_op jit(solution)/shard_map/ppermute | solution.py:791
  715.5 50.1 %collective-permute-start.13 = (bf16[192,2816]{1,0:T(8,128)(2,1)}, bf16[192,2816]{1,0:T(8,128)(2,1)}, u32[]{:S(2)}, u32[]{:S(2)}) collective-permute-start(bf16[192,2816]{1,0:T(8,128)(2,1)} %get-tuple-element.72.refs_0_), channel_id=1, source_target_pairs={{0,1},{1,0},{2,3},{3,2},{4,5},{5,4},{6,7},{7,6}} | collective-permute-start | bytes 3244040 | tf_op jit(solution)/shard_map/ppermute | solution.py:791
  716.4 19.6 %collective-permute-start.20 = (bf16[192,1408]{1,0:T(8,128)(2,1)}, bf16[192,1408]{1,0:T(8,128)(2,1)}, u32[]{:S(2)}, u32[]{:S(2)}) collective-permute-start(bf16[192,1408]{1,0:T(8,128)(2,1)} %collective-permute-done.3.refs_1_), channel_id=1, source_target_pairs={{0,1},{1,0},{2,3},{3,2},{4,5},{5,4},{6,7},{7,6}} | collective-permute-start | bytes 1622024 | tf_op jit(solution)/shard_map/ppermute | solution.py:791
  716.9 20.3 %collective-permute-start.15 = (bf16[192,1408]{1,0:T(8,128)(2,1)}, bf16[192,1408]{1,0:T(8,128)(2,1)}, u32[]{:S(2)}, u32[]{:S(2)}) collective-permute-start(bf16[192,1408]{1,0:T(8,128)(2,1)} %collective-permute-done.refs_0_), channel_id=1, source_target_pairs={{0,1},{1,0},{2,3},{3,2},{4,5},{5,4},{6,7},{7,6}} | collective-permute-start | bytes 1622024 | tf_op jit(solution)/shard_map/ppermute | solution.py:791
  726.6 37.8 %collective-permute-start.16 = (bf16[192,1408]{1,0:T(8,128)(2,1)}, bf16[192,1408]{1,0:T(8,128)(2,1)}, u32[]{:S(2)}, u32[]{:S(2)}) collective-permute-start(bf16[192,1408]{1,0:T(8,128)(2,1)} %collective-permute-done.14.refs_1_), channel_id=1, source_target_pairs={{0,1},{1,0},{2,3},{3,2},{4,5},{5,4},{6,7},{7,6}} | collective-permute-start | bytes 1622024 | tf_op jit(solution)/shard_map/ppermute | solution.py:791
  735.7 55.9 %collective-permute-start.43 = (bf16[192,4224]{1,0:T(8,128)(2,1)S(1)}, bf16[192,4224]{1,0:T(8,128)(2,1)}, u32[]{:S(2)}, u32[]{:S(2)}) collective-permute-start(bf16[192,4224]{1,0:T(8,128)(2,1)S(1)} %get-tuple-element.74.refs_0_), channel_id=1, source_target_pairs={{0,1},{1,0},{2,3},{3,2},{4,5},{5,4},{6,7},{7,6}} | collective-permute-start | bytes 4866056 | tf_op jit(solution)/shard_map/ppermute | solution.py:791
  736.0 57.2 %collective-permute-start.30 = (bf16[192,4224]{1,0:T(8,128)(2,1)S(1)}, bf16[192,4224]{1,0:T(8,128)(2,1)}, u32[]{:S(2)}, u32[]{:S(2)}) collective-permute-start(bf16[192,4224]{1,0:T(8,128)(2,1)S(1)} %get-tuple-element.74.refs_0_), channel_id=1, source_target_pairs={{0,2},{1,3},{2,0},{3,1},{4,6},{5,7},{6,4},{7,5}} | collective-permute-start | bytes 4866056 | tf_op jit(solution)/shard_map/ppermute | solution.py:791
  737.2 29.3 %collective-permute-start.10 = (bf16[192,1408]{1,0:T(8,128)(2,1)}, bf16[192,1408]{1,0:T(8,128)(2,1)}, u32[]{:S(2)}, u32[]{:S(2)}) collective-permute-start(bf16[192,1408]{1,0:T(8,128)(2,1)} %copy-done.60), channel_id=1, source_target_pairs={{0,4},{1,5},{2,6},{3,7},{4,0},{5,1},{6,2},{7,3}} | collective-permute-start | bytes 1622024 | tf_op jit(solution)/shard_map/ppermute | solution.py:791
  764.4 38.4 %collective-permute-start.40 = (bf16[192,4224]{1,0:T(8,128)(2,1)S(1)}, bf16[192,4224]{1,0:T(8,128)(2,1)}, u32[]{:S(2)}, u32[]{:S(2)}) collective-permute-start(bf16[192,4224]{1,0:T(8,128)(2,1)S(1)} %get-tuple-element.74.refs_0_), channel_id=1, source_target_pairs={{0,4},{1,5},{2,6},{3,7},{4,0},{5,1},{6,2},{7,3}} | collective-permute-start | bytes 4866056 | tf_op jit(solution)/shard_map/ppermute | solution.py:791
  765.7 19.5 %collective-permute-start.7 = (bf16[192,1408]{1,0:T(8,128)(2,1)}, bf16[192,1408]{1,0:T(8,128)(2,1)S(1)}, u32[]{:S(2)}, u32[]{:S(2)}) collective-permute-start(bf16[192,1408]{1,0:T(8,128)(2,1)} %collective-permute-done.6.refs_0_), channel_id=1, source_target_pairs={{0,2},{1,3},{2,0},{3,1},{4,6},{5,7},{6,4},{7,5}} | collective-permute-start | bytes 1622024 | tf_op jit(solution)/shard_map/ppermute | solution.py:791
  766.5 39.0 %collective-permute-start.39 = (bf16[192,4224]{1,0:T(8,128)(2,1)S(1)}, bf16[192,4224]{1,0:T(8,128)(2,1)S(1)}, u32[]{:S(2)}, u32[]{:S(2)}) collective-permute-start(bf16[192,4224]{1,0:T(8,128)(2,1)S(1)} %get-tuple-element.77.refs_0_), channel_id=1, source_target_pairs={{0,1},{1,0},{2,3},{3,2},{4,5},{5,4},{6,7},{7,6}} | collective-permute-start | bytes 4866056 | tf_op jit(solution)/shard_map/ppermute | solution.py:791
  785.2 51.1 %collective-permute-start.33 = (bf16[192,4224]{1,0:T(8,128)(2,1)S(1)}, bf16[192,4224]{1,0:T(8,128)(2,1)S(1)}, u32[]{:S(2)}, u32[]{:S(2)}) collective-permute-start(bf16[192,4224]{1,0:T(8,128)(2,1)S(1)} %get-tuple-element.77.refs_0_), channel_id=1, source_target_pairs={{0,4},{1,5},{2,6},{3,7},{4,0},{5,1},{6,2},{7,3}} | collective-permute-start | bytes 4866056 | tf_op jit(solution)/shard_map/ppermute | solution.py:791
  791.6 44.7 %collective-permute-start.70 = (bf16[352,1536]{1,0:T(8,128)(2,1)S(1)}, bf16[352,1536]{1,0:T(8,128)(2,1)S(1)}, u32[]{:S(2)}, u32[]{:S(2)}) collective-permute-start(bf16[352,1536]{1,0:T(8,128)(2,1)S(1)} %copy-done.14), channel_id=1, source_target_pairs={{0,1},{1,0},{2,3},{3,2},{4,5},{5,4},{6,7},{7,6}} | collective-permute-start | bytes 3244040 | tf_op jit(solution)/shard_map/ppermute | solution.py:791
  793.2 92.8 %collective-permute-start.12 = (bf16[3,192,2816]{2,1,0:T(8,128)(2,1)}, bf16[3,192,2816]{2,1,0:T(8,128)(2,1)}, u32[]{:S(2)}, u32[]{:S(2)}) collective-permute-start(bf16[3,192,2816]{2,1,0:T(8,128)(2,1)} %adamw_ahead.1.new_ref), channel_id=1, source_target_pairs={{0,1},{1,0},{2,3},{3,2},{4,5},{5,4},{6,7},{7,6}} | collective-permute-start | bytes 9732104 | tf_op jit(solution)/shard_map/ppermute | solution.py:791
  802.8 55.1 %collective-permute-start.36 = (bf16[192,4224]{1,0:T(8,128)(2,1)S(1)}, bf16[192,4224]{1,0:T(8,128)(2,1)S(1)}, u32[]{:S(2)}, u32[]{:S(2)}) collective-permute-start(bf16[192,4224]{1,0:T(8,128)(2,1)S(1)} %get-tuple-element.77.refs_0_), channel_id=1, source_target_pairs={{0,2},{1,3},{2,0},{3,1},{4,6},{5,7},{6,4},{7,5}} | collective-permute-start | bytes 4866056 | tf_op jit(solution)/shard_map/ppermute | solution.py:791
  805.5 44.8 %collective-permute-start.69 = (bf16[352,1536]{1,0:T(8,128)(2,1)}, bf16[352,1536]{1,0:T(8,128)(2,1)}, u32[]{:S(2)}, u32[]{:S(2)}) collective-permute-start(bf16[352,1536]{1,0:T(8,128)(2,1)} %collective-permute-done.68.refs_0_), channel_id=1, source_target_pairs={{0,1},{1,0},{2,3},{3,2},{4,5},{5,4},{6,7},{7,6}} | collective-permute-start | bytes 3244040 | tf_op jit(solution)/shard_map/ppermute | solution.py:791
  836.3 24.9 %collective-permute-start.65 = (bf16[352,1536]{1,0:T(8,128)(2,1)S(1)}, bf16[352,1536]{1,0:T(8,128)(2,1)}, u32[]{:S(2)}, u32[]{:S(2)}) collective-permute-start(bf16[352,1536]{1,0:T(8,128)(2,1)S(1)} %copy-done.16), channel_id=1, source_target_pairs={{0,1},{1,0},{2,3},{3,2},{4,5},{5,4},{6,7},{7,6}} | collective-permute-start | bytes 3244040 | tf_op jit(solution)/shard_map/ppermute | solution.py:791
  836.3 24.9 %collective-permute-start.66 = (bf16[352,1536]{1,0:T(8,128)(2,1)S(1)}, bf16[352,1536]{1,0:T(8,128)(2,1)}, u32[]{:S(2)}, u32[]{:S(2)}) collective-permute-start(bf16[352,1536]{1,0:T(8,128)(2,1)S(1)} %copy-done.18), channel_id=1, source_target_pairs={{0,1},{1,0},{2,3},{3,2},{4,5},{5,4},{6,7},{7,6}} | collective-permute-start | bytes 3244040 | tf_op jit(solution)/shard_map/ppermute | solution.py:791
  850.4 25.9 %collective-permute-start.54 = (bf16[352,1536]{1,0:T(8,128)(2,1)S(1)}, bf16[352,1536]{1,0:T(8,128)(2,1)}, u32[]{:S(2)}, u32[]{:S(2)}) collective-permute-start(bf16[352,1536]{1,0:T(8,128)(2,1)S(1)} %copy-done.16), channel_id=1, source_target_pairs={{0,2},{1,3},{2,0},{3,1},{4,6},{5,7},{6,4},{7,5}} | collective-permute-start | bytes 3244040 | tf_op jit(solution)/shard_map/ppermute | solution.py:791
  857.9 25.6 %collective-permute-start.51 = (bf16[352,1536]{1,0:T(8,128)(2,1)S(1)}, bf16[352,1536]{1,0:T(8,128)(2,1)}, u32[]{:S(2)}, u32[]{:S(2)}) collective-permute-start(bf16[352,1536]{1,0:T(8,128)(2,1)S(1)} %copy-done.14), channel_id=1, source_target_pairs={{0,4},{1,5},{2,6},{3,7},{4,0},{5,1},{6,2},{7,3}} | collective-permute-start | bytes 3244040 | tf_op jit(solution)/shard_map/ppermute | solution.py:791
  861.3 36.8 %collective-permute-start.42 = (bf16[192,4224]{1,0:T(8,128)(2,1)}, bf16[192,4224]{1,0:T(8,128)(2,1)}, u32[]{:S(2)}, u32[]{:S(2)}) collective-permute-start(bf16[192,4224]{1,0:T(8,128)(2,1)} %collective-permute-done.30.refs_1_), channel_id=1, source_target_pairs={{0,1},{1,0},{2,3},{3,2},{4,5},{5,4},{6,7},{7,6}} | collective-permute-start | bytes 4866056 | tf_op jit(solution)/shard_map/ppermute | solution.py:791
  873.0 29.8 %collective-permute-start.41 = (bf16[192,4224]{1,0:T(8,128)(2,1)}, bf16[192,4224]{1,0:T(8,128)(2,1)S(1)}, u32[]{:S(2)}, u32[]{:S(2)}) collective-permute-start(bf16[192,4224]{1,0:T(8,128)(2,1)} %collective-permute-done.40.refs_0_), channel_id=1, source_target_pairs={{0,1},{1,0},{2,3},{3,2},{4,5},{5,4},{6,7},{7,6}} | collective-permute-start | bytes 4866056 | tf_op jit(solution)/shard_map/ppermute | solution.py:791
  876.3 26.5 %collective-permute-start.37 = (bf16[192,4224]{1,0:T(8,128)(2,1)S(1)}, bf16[192,4224]{1,0:T(8,128)(2,1)S(1)}, u32[]{:S(2)}, u32[]{:S(2)}) collective-permute-start(bf16[192,4224]{1,0:T(8,128)(2,1)S(1)} %collective-permute-done.33.refs_0_), channel_id=1, source_target_pairs={{0,1},{1,0},{2,3},{3,2},{4,5},{5,4},{6,7},{7,6}} | collective-permute-start | bytes 4866056 | tf_op jit(solution)/shard_map/ppermute | solution.py:791
  886.0 30.0 %collective-permute-start.38 = (bf16[192,4224]{1,0:T(8,128)(2,1)S(1)}, bf16[192,4224]{1,0:T(8,128)(2,1)}, u32[]{:S(2)}, u32[]{:S(2)}) collective-permute-start(bf16[192,4224]{1,0:T(8,128)(2,1)S(1)} %collective-permute-done.36.refs_1_), channel_id=1, source_target_pairs={{0,1},{1,0},{2,3},{3,2},{4,5},{5,4},{6,7},{7,6}} | collective-permute-start | bytes 4866056 | tf_op jit(solution)/shard_map/ppermute | solution.py:791
  897.1 37.4 %collective-permute-start.34 = (bf16[192,4224]{1,0:T(8,128)(2,1)S(1)}, bf16[192,4224]{1,0:T(8,128)(2,1)S(1)}, u32[]{:S(2)}, u32[]{:S(2)}) collective-permute-start(bf16[192,4224]{1,0:T(8,128)(2,1)S(1)} %collective-permute-done.33.refs_0_), channel_id=1, source_target_pairs={{0,2},{1,3},{2,0},{3,1},{4,6},{5,7},{6,4},{7,5}} | collective-permute-start | bytes 4866056 | tf_op jit(solution)/shard_map/ppermute | solution.py:791
  898.0 38.5 %collective-permute-start.31 = (bf16[192,4224]{1,0:T(8,128)(2,1)}, bf16[192,4224]{1,0:T(8,128)(2,1)S(1)}, u32[]{:S(2)}, u32[]{:S(2)}) collective-permute-start(bf16[192,4224]{1,0:T(8,128)(2,1)} %collective-permute-done.30.refs_1_), channel_id=1, source_target_pairs={{0,4},{1,5},{2,6},{3,7},{4,0},{5,1},{6,2},{7,3}} | collective-permute-start | bytes 4866056 | tf_op jit(solution)/shard_map/ppermute | solution.py:791
  902.8 45.4 %collective-permute-start.55 = (bf16[352,1536]{1,0:T(8,128)(2,1)}, bf16[352,1536]{1,0:T(8,128)(2,1)}, u32[]{:S(2)}, u32[]{:S(2)}) collective-permute-start(bf16[352,1536]{1,0:T(8,128)(2,1)} %collective-permute-done.54.refs_1_), channel_id=1, source_target_pairs={{0,1},{1,0},{2,3},{3,2},{4,5},{5,4},{6,7},{7,6}} | collective-permute-start | bytes 3244040 | tf_op jit(solution)/shard_map/ppermute | solution.py:791
  902.8 45.9 %collective-permute-start.52 = (bf16[352,1536]{1,0:T(8,128)(2,1)}, bf16[352,1536]{1,0:T(8,128)(2,1)}, u32[]{:S(2)}, u32[]{:S(2)}) collective-permute-start(bf16[352,1536]{1,0:T(8,128)(2,1)} %collective-permute-done.51.refs_0_), channel_id=1, source_target_pairs={{0,1},{1,0},{2,3},{3,2},{4,5},{5,4},{6,7},{7,6}} | collective-permute-start | bytes 3244040 | tf_op jit(solution)/shard_map/ppermute | solution.py:791
  916.1 32.1 %collective-permute-start.4 = (bf16[192,1408]{1,0:T(8,128)(2,1)}, bf16[192,1408]{1,0:T(8,128)(2,1)S(1)}, u32[]{:S(2)}, u32[]{:S(2)}) collective-permute-start(bf16[192,1408]{1,0:T(8,128)(2,1)} %collective-permute-done.3.refs_1_), channel_id=1, source_target_pairs={{0,4},{1,5},{2,6},{3,7},{4,0},{5,1},{6,2},{7,3}} | collective-permute-start | bytes 1622024 | tf_op jit(solution)/shard_map/ppermute | solution.py:791
  934.5 24.1 %collective-permute-start.45 = (bf16[176,1536]{1,0:T(8,128)(2,1)S(1)}, bf16[176,1536]{1,0:T(8,128)(2,1)S(1)}, u32[]{:S(2)}, u32[]{:S(2)}) collective-permute-start(bf16[176,1536]{1,0:T(8,128)(2,1)S(1)} %copy-done.29), channel_id=1, source_target_pairs={{0,4},{1,5},{2,6},{3,7},{4,0},{5,1},{6,2},{7,3}} | collective-permute-start | bytes 1622024 | tf_op jit(solution)/shard_map/ppermute | solution.py:791
  936.6 22.0 %collective-permute-start.1 = (bf16[192,1408]{1,0:T(8,128)(2,1)}, bf16[192,1408]{1,0:T(8,128)(2,1)S(1)}, u32[]{:S(2)}, u32[]{:S(2)}) collective-permute-start(bf16[192,1408]{1,0:T(8,128)(2,1)} %collective-permute-done.refs_0_), channel_id=1, source_target_pairs={{0,2},{1,3},{2,0},{3,1},{4,6},{5,7},{6,4},{7,5}} | collective-permute-start | bytes 1622024 | tf_op jit(solution)/shard_map/ppermute | solution.py:791
  (108 other events, 1546.8 us)
